TPU v7x, 256 devices: a whole 4x4x8 slice. The times are simulated.
256 devices in a mesh: graph: 64 (over z, y, core), feat: 4 (over x).
Axes of the slice: x: 4, y: 4, z: 8, core: 2. Of those that a mesh axis runs over, the one named last changes fastest.
Arguments:
- node_feats: bfloat16 [20480, 512], P(('graph', 'feat')), may hold values from -6 to 6
- edge_feats: bfloat16 [131072, 512], P(('graph', 'feat')), may hold values from -6 to 6
- senders: int32 [131072], P(('graph', 'feat')), may hold values from 0 to 319
- receiver_ref: int32 [131072], P(('graph', 'feat')), may hold values from 0 to 6463, as said below
- send_list: int32 [64, 64, 96], P('graph'), may hold values from 0 to 319, as said below
- edge_count: int32 [64], P('graph'), may hold values from 1024 to 2048, as said below
- edge_w1: bfloat16 [1536, 512], replicated, may hold values from -0.15625 to 0.15625
- edge_w2: bfloat16 [512, 512], replicated, may hold values from -0.25 to 0.25
- edge_gain: bfloat16 [512], replicated, may hold values from 0.099609375 to 1.8984375
- edge_shift: bfloat16 [512], replicated, may hold values from -3 to 3
- node_w1: bfloat16 [1024, 512], replicated, may hold values from -0.1875 to 0.1875
- node_w2: bfloat16 [512, 512], replicated, may hold values from -0.25 to 0.25
- node_gain: bfloat16 [512], replicated, may hold values from 0.099609375 to 1.8984375
- node_shift: bfloat16 [512], replicated, may hold values from -3 to 3
Outputs:
- new_edges: bfloat16 [131072, 512], P(('graph', 'feat'))
- new_nodes: bfloat16 [20480, 512], P(('graph', 'feat'))
Inputs may be any that keep to these rules, and one draw needn't show every extreme that they name: `senders`: local node indices of the edge's own region. `receiver_ref`: A value below 320 is a node of the edge's own region. Otherwise q = value - 320 names slot q % 96 of the list that region s = q // 96 keeps for the edge's region; s is never the edge's own region, and when s is more than 2 steps away around the region order (either direction, wrapping) the slot is below 16. In every draw each region has an edge on slot 95 of the next region and an edge on slot 15 of the region 3 steps on. Each list send_list[s, g] holds 96 distinct local node indices of region s. Region g's live edges are its first edge_count[g] edge slots; some region has all 2048 live.
All inputs are finite; a program needn't handle non-finite values.
Results may differ from a plain program's by a relative error of at most 0.009.
Values may be sent and summed in bfloat16 or wider, within the bound.
No kernel may reach another device: no remote copies, remote signals or barrier semaphores. Data moves between devices by JAX's collectives and lax.ppermute only.
A program may use at most 128 MiB of HBM per device.

v0:
```python
import jax
import jax.numpy as jnp
from jax import lax
from jax.sharding import PartitionSpec as P

NODE_DEV = 320
SLOT = 96
FAR_SLOT = 16
REACH = 2


epsilon = 1e-05


def in_order(tiles, dim):
    dims = list(tiles.shape[1:])
    dims[dim] *= tiles.shape[0]
    return jnp.moveaxis(tiles, 0, dim).reshape(dims)


def copy_for_each(value, axis):
    devices = lax.axis_size(axis)
    return lax.all_to_all(
        jnp.broadcast_to(value[None], (devices, *value.shape)), axis, 0, 0, tiled=True
    )


def gathered_copies(value, axis, dim):
    return in_order(copy_for_each(value, axis), dim)


def passed_along(value, axis, by):
    devices = lax.axis_size(axis)
    return lax.ppermute(value, axis, [(i, (i + by) % devices) for i in range(devices)])


def cut_along(value, dim, devices):
    before, after = (value.shape[:dim], value.shape[dim + 1 :])
    return jnp.moveaxis(value.reshape(*before, devices, -1, *after), dim, 0)


def sum_at_owner(value, axis, dim):
    tiles = cut_along(value, dim, lax.axis_size(axis))
    arrived = lax.all_to_all(tiles, axis, split_axis=0, concat_axis=0, tiled=True)
    return arrived.astype(jnp.float32).sum(axis=0)


def layer_norm(outputs, norm_gain, norm_shift):
    average = jnp.mean(outputs, axis=-1, keepdims=True)
    centered = outputs - average
    variance = jnp.mean(centered * centered, axis=-1, keepdims=True)
    return centered * lax.rsqrt(variance + epsilon) * norm_gain + norm_shift


def perceptron(inputs, first_weight, second_weight, norm_gain, norm_shift):
    joined = jnp.concatenate(inputs, axis=1)
    activation = jnp.dot(joined, first_weight, preferred_element_type=jnp.float32)
    hidden = jax.nn.silu(activation).astype(jnp.bfloat16)
    outputs = jnp.dot(hidden, second_weight, preferred_element_type=jnp.float32)
    return layer_norm(outputs, norm_gain, norm_shift)


def one_hot_rows(indices, width):
    return (indices[:, None] == lax.iota(jnp.int32, width)[None, :]).astype(jnp.bfloat16)


def sum_into(selector, values):
    return lax.dot_general(
        selector, values, (((0,), (0,)), ((), ())), preferred_element_type=jnp.float32
    )


def per_device(
    node_feats,
    edge_feats,
    senders,
    receiver_ref,
    send_list,
    edge_count,
    edge_w1,
    edge_w2,
    edge_gain,
    edge_shift,
    node_w1,
    node_w2,
    node_gain,
    node_shift,
):
    feature_width = node_feats.shape[1]
    edge_local = edge_feats.shape[0]
    groups = lax.axis_size("graph")
    own_index = lax.axis_index("graph")
    share_index = lax.axis_index("feat")
    region_nodes = gathered_copies(node_feats, "feat", 0)
    send_rows = send_list[0]
    pieces = 1
    part_index = 0
    quarter = SLOT // pieces
    far_count = FAR_SLOT // pieces
    my_rows = lax.dynamic_index_in_dim(
        send_rows.reshape(groups, quarter, pieces), part_index, 2, keepdims=False
    ).reshape(-1)
    list_select = one_hot_rows(my_rows, NODE_DEV)
    outgoing = (
        jnp.dot(list_select, region_nodes, preferred_element_type=jnp.float32)
        .astype(jnp.bfloat16)
        .reshape(groups, quarter, feature_width)
    )
    offsets = [distance for distance in range(-REACH, REACH + 1) if distance != 0]
    far_part = lax.all_to_all(
        outgoing[:, :far_count], "graph", split_axis=0, concat_axis=0, tiled=True
    )
    received = jnp.pad(far_part, ((0, 0), (0, quarter - far_count), (0, 0)))
    for distance in offsets:
        near_block = lax.dynamic_index_in_dim(
            outgoing, (own_index - distance) % groups, 0, keepdims=False
        )
        arrived = passed_along(near_block, "graph", -distance)
        received = lax.dynamic_update_index_in_dim(
            received, arrived, (own_index + distance) % groups, 0
        )
    offset = jnp.maximum(receiver_ref - NODE_DEV, 0)
    source = offset // SLOT
    slot_index = offset % SLOT
    arranged = source * SLOT + slot_index % pieces * quarter + slot_index // pieces
    row_index = jnp.where(receiver_ref < NODE_DEV, receiver_ref, NODE_DEV + arranged)
    table_rows = NODE_DEV + groups * SLOT
    table = jnp.concatenate([region_nodes, received.reshape(groups * SLOT, feature_width)], axis=0)
    receiver_select = one_hot_rows(row_index, table_rows)
    sender_select = one_hot_rows(senders, NODE_DEV)
    sender_rows = jnp.dot(sender_select, region_nodes, preferred_element_type=jnp.float32).astype(
        jnp.bfloat16
    )
    receiver_rows = jnp.dot(receiver_select, table, preferred_element_type=jnp.float32).astype(
        jnp.bfloat16
    )
    update = edge_feats.astype(jnp.float32) + perceptron(
        (edge_feats, sender_rows, receiver_rows), edge_w1, edge_w2, edge_gain, edge_shift
    )
    live_mask = share_index * edge_local + lax.iota(jnp.int32, edge_local) < edge_count[0]
    new_edges = jnp.where(live_mask[:, None], update, edge_feats.astype(jnp.float32)).astype(
        jnp.bfloat16
    )
    messages = jnp.where(live_mask[:, None], new_edges, jnp.zeros_like(new_edges))
    segment_totals = sum_into(receiver_select, messages)
    own_sums = segment_totals[:NODE_DEV]
    partial_value = segment_totals[NODE_DEV:].reshape(groups, SLOT, feature_width)
    far_back = lax.all_to_all(
        partial_value[:, :far_count].astype(jnp.bfloat16),
        "graph",
        split_axis=0,
        concat_axis=0,
        tiled=True,
    ).astype(jnp.float32)
    returned = jnp.pad(far_back, ((0, 0), (0, quarter - far_count), (0, 0)))
    for distance in offsets:
        near_block = lax.dynamic_index_in_dim(
            partial_value, (own_index + distance) % groups, 0, keepdims=False
        )
        arrived = passed_along(near_block.astype(jnp.bfloat16), "graph", distance).astype(
            near_block.dtype
        )
        returned = lax.dynamic_update_index_in_dim(
            returned, arrived, (own_index - distance) % groups, 0
        )
    flat_returned = returned.reshape(groups * quarter, feature_width)
    upper_part = flat_returned.astype(jnp.bfloat16)
    lower_part = (flat_returned - upper_part.astype(jnp.float32)).astype(jnp.bfloat16)
    listed_sums = sum_into(list_select, upper_part) + sum_into(list_select, lower_part)
    node_sums = sum_at_owner((own_sums + listed_sums).astype(jnp.bfloat16), "feat", 0)
    aggregate = node_sums.astype(jnp.bfloat16)
    node_update = node_feats.astype(jnp.float32) + perceptron(
        (node_feats, aggregate), node_w1, node_w2, node_gain, node_shift
    )
    return (new_edges, node_update.astype(jnp.bfloat16))


def solution(mesh):
    return jax.shard_map(
        per_device,
        mesh=mesh,
        in_specs=(
            P(("graph", "feat"), None),
            P(("graph", "feat"), None),
            P(("graph", "feat")),
            P(("graph", "feat")),
            P("graph", None, None),
            P("graph"),
            P(),
            P(),
            P(),
            P(),
            P(),
            P(),
            P(),
            P(),
        ),
        out_specs=(P(("graph", "feat"), None), P(("graph", "feat"), None)),
        check_vma=False,
    )
```

profile of v0, /device:TPU:1, one launch (start us, length us, event | category | flops | bytes accessed | tf_op | source)
XLA Modules:
  0.0 173.4 jit_solution(17367850225809019450)
XLA Ops:
  0.6 0.0 copy-start
  0.6 1.8 %broadcast_in_dim.77 = bf16[4,80,512]{2,1,0:T(8,128)(2,1)} broadcast(bf16[80,512]{1,0:T(8,128)(2,1)} %param.14), dimensions={1,2} | broadcast | bytes 409600 | tf_op jit(solution)/shard_map/broadcast_in_dim | solution.py:24
  2.4 4.8 %all-to-all-start = ((bf16[4,80,512]{2,1,0:T(8,128)(2,1)}), bf16[4,80,512]{2,1,0:T(8,128)(2,1)S(1)}, u32[]{:S(2)}, u32[]{:S(2)}) async-start(bf16[4,80,512]{2,1,0:T(8,128)(2,1)} %broadcast_in_dim.77), calls=%async_computation | async-start | bytes 655360 | tf_op jit(solution)/shard_map/all_to_all | solution.py:23
  7.2 0.8 eq.67
  8.1 5.0 %all-to-all-done = bf16[4,80,512]{2,1,0:T(8,128)(2,1)S(1)} async-done(((bf16[4,80,512]{2,1,0:T(8,128)(2,1)}), bf16[4,80,512]{2,1,0:T(8,128)(2,1)S(1)}, u32[]{:S(2)}, u32[]{:S(2)}) %all-to-all-start) | async-done | bytes 327712 | tf_op jit(solution)/shard_map/all_to_all | solution.py:23
  13.1 3.7 %convolution_convert_fusion = bf16[6144,512]{1,0:T(8,128)(2,1)S(1)} fusion(bf16[320,512]{1,0:T(8,128)(2,1)S(1)} %bitcast.62, s32[6144]{0:T(1024)S(1)} %eq.67), kind=kOutput, calls=%fused_computation.6 | convolution fusion | flops 2018377728 | bytes 6643712 | tf_op jit(solution)/shard_map/dot_general | solution.py:105
  16.9 2.7 %copy-done.5 = bf16[6144,512]{1,0:T(8,128)(2,1)} copy-done((bf16[6144,512]{1,0:T(8,128)(2,1)}, bf16[6144,512]{1,0:T(8,128)(2,1)S(1)}, u32[]{:S(2)}) %copy-start.5) | copy-done | bytes 6291480
  19.5 1.1 slice.17
  20.6 14.1 %all-to-all-start.1 = ((bf16[64,16,512]{2,1,0:T(8,128)(2,1)}), bf16[64,16,512]{2,1,0:T(8,128)(2,1)S(1)}, u32[]{:S(2)}, u32[]{:S(2)}) async-start(bf16[64,16,512]{2,1,0:T(8,128)(2,1)} %slice.17), calls=%async_computation.1 | async-start | bytes 2097152 | tf_op jit(solution)/shard_map/all_to_all | solution.py:110
  35.4 1.3 copy.18
  36.8 1.8 %dynamic-slice_bitcast_fusion = (bf16[96,512]{1,0:T(8,128)(2,1)}, bf16[96,512]{1,0:T(8,128)(2,1)}, bf16[96,512]{1,0:T(8,128)(2,1)}, bf16[96,512]{1,0:T(8,128)(2,1)}) fusion(bf16[64,96,512]{2,1,0:T(8,128)(2,1)} %bitcast.61, s32[]{:T(128)S(6)} %select_n.104, s32[]{:T(128)S(6)} %select_n.108, s32[]{:T(128)S(6)} %select_n.106, s32[]{:T(128)S(6)} %select_n.102), kind=kLoop, calls=%fused_computation.67 | loop fusion | bytes 786448 | tf_op jit(solution)/shard_map/jit(dynamic_index_in_dim)/squeeze | solution.py:115
  38.6 1.4 collective-permute-start
  39.9 1.7 %collective-permute-start.1 = (bf16[96,512]{1,0:T(8,128)(2,1)}, bf16[96,512]{1,0:T(8,128)(2,1)}, u32[]{:S(2)}, u32[]{:S(2)}) collective-permute-start(bf16[96,512]{1,0:T(8,128)(2,1)} %get-tuple-element.14), channel_id=1, source_target_pairs={{0,4},{4,8},{8,12},{12,16},{16,20},{20,24},{24,28},{28,32},{32,36}... | collective-permute-start | bytes 294920 | tf_op jit(solution)/shard_map/ppermute | solution.py:34
  41.7 0.0 collective-permute-start.2
  41.7 3.6 %collective-permute-start.3 = (bf16[96,512]{1,0:T(8,128)(2,1)}, bf16[96,512]{1,0:T(8,128)(2,1)}, u32[]{:S(2)}, u32[]{:S(2)}) collective-permute-start(bf16[96,512]{1,0:T(8,128)(2,1)} %get-tuple-element.12), channel_id=1, source_target_pairs={{0,248},{4,252},{8,0},{12,4},{16,8},{20,12},{24,16},{28,20},{32,24... | collective-permute-start | bytes 294920 | tf_op jit(solution)/shard_map/ppermute | solution.py:34
  45.3 1.3 convolution_convert_fusion.1
  46.5 17.8 %all-to-all-done.1 = bf16[64,16,512]{2,1,0:T(8,128)(2,1)S(1)} async-done(((bf16[64,16,512]{2,1,0:T(8,128)(2,1)}), bf16[64,16,512]{2,1,0:T(8,128)(2,1)S(1)}, u32[]{:S(2)}, u32[]{:S(2)}) %all-to-all-start.1) | async-done | bytes 1048608 | tf_op jit(solution)/shard_map/all_to_all | solution.py:110
  64.3 0.8 pad.11
  65.1 0.0 collective-permute-done
  65.1 0.9 bitcast_dynamic-update-slice_fusion.3
  66.0 0.0 collective-permute-done.1
  66.0 0.9 bitcast_dynamic-update-slice_fusion.2
  67.0 0.0 collective-permute-done.2
  67.0 0.9 bitcast_dynamic-update-slice_fusion.1
  67.9 0.0 collective-permute-done.3
  67.9 0.9 bitcast_dynamic-update-slice_fusion
  68.8 4.5 %fusion.21 = bf16[512,512]{1,0:T(8,128)(2,1)} fusion(bf16[6144,512]{1,0:T(8,128)(2,1)S(1)} %bitcast.59, bf16[320,512]{1,0:T(8,128)(2,1)S(1)} %bitcast.64, s32[512]{0:T(512)S(1)} %compare_select_fusion), kind=kOutput, calls=%fused_computation.28 | convolution fusion | flops 3405807616 | bytes 7145472 | tf_op jit(solution)/shard_map/dot_general | solution.py:134
  73.3 3.1 %fusion.65 = (f32[512]{0:T(512)S(1)}, f32[512,512]{0,1:T(8,128)S(1)}) fusion(bf16[512,512]{1,0:T(8,128)(2,1)} %param.21, bf16[1536,512]{1,0:T(8,128)(2,1)S(1)} %copy-done, bf16[512,512]{1,0:T(8,128)(2,1)} %fusion.21, bf16[512,512]{1,0:T(8,128)(2,1)} %convolution_convert_fusion.1, bf16[512,512]{1,0:T(8,128)(2,1)} %param.15), kind=kOutput, calls=%fused_computation.93 | convolution fusion | flops 1080032768 | bytes 4720640 | tf_op jit(solution)/shard_map/dot_general | solution.py:59
  76.4 0.2 multiply_reduce_fusion
  76.5 0.3 fusion.27
  76.9 0.0 copy-start.3
  76.9 7.1 %fusion.5 = f32[6464,512]{1,0:T(8,128)} fusion(s32[512]{0:T(512)S(1)} %compare_select_fusion, bf16[512,512]{0,1:T(8,128)(2,1)S(1)} %fusion.27, pred[512]{0:T(512)(128)(4,1)S(1)} %add_compare_fusion), kind=kOutput, calls=%fused_computation.10 | convolution fusion | flops 3395878912 | bytes 13765120 | tf_op jit(solution)/shard_map/dot_general | solution.py:68
  84.0 8.0 %slice.19 = bf16[6144,512]{1,0:T(8,128)(2,1)} slice(f32[6464,512]{1,0:T(8,128)} %fusion.5), slice={[320:6464], [0:512]} | slice | bytes 12582912 | tf_op jit(solution)/shard_map/slice | solution.py:147
  92.0 2.3 %slice.23 = bf16[64,16,512]{2,1,0:T(8,128)(2,1)} slice(bf16[64,96,512]{2,1,0:T(8,128)(2,1)} %bitcast.57), slice={[0:64], [0:16], [0:512]} | slice | bytes 2097152 | tf_op jit(solution)/shard_map/slice | solution.py:149
  94.3 6.0 %all-to-all-start.2 = ((bf16[64,16,512]{2,1,0:T(8,128)(2,1)}), bf16[64,16,512]{2,1,0:T(8,128)(2,1)S(1)}, u32[]{:S(2)}, u32[]{:S(2)}) async-start(bf16[64,16,512]{2,1,0:T(8,128)(2,1)} %slice.23), calls=%async_computation.2 | async-start | bytes 2097152 | tf_op jit(solution)/shard_map/all_to_all | solution.py:148
  100.2 1.1 fusion.50
  101.3 5.1 %collective-permute-start.4 = (bf16[96,512]{1,0:T(8,128)(2,1)S(1)}, bf16[96,512]{1,0:T(8,128)(2,1)S(1)}, u32[]{:S(2)}, u32[]{:S(2)}) collective-permute-start(bf16[96,512]{1,0:T(8,128)(2,1)S(1)} %get-tuple-element.11), channel_id=1, source_target_pairs={{0,248},{4,252},{8,0},{12,4},{16,8},{20,12},{24,16},{28,20},{32,24... | collective-permute-start | bytes 294920 | tf_op jit(solution)/shard_map/ppermute | solution.py:34
  106.4 0.7 collective-permute-start.5
  107.0 1.1 collective-permute-start.6
  108.1 0.0 collective-permute-start.7
  108.1 21.8 %all-to-all-done.2 = bf16[64,16,512]{2,1,0:T(8,128)(2,1)S(1)} async-done(((bf16[64,16,512]{2,1,0:T(8,128)(2,1)}), bf16[64,16,512]{2,1,0:T(8,128)(2,1)S(1)}, u32[]{:S(2)}, u32[]{:S(2)}) %all-to-all-start.2) | async-done | bytes 1048608 | tf_op jit(solution)/shard_map/all_to_all | solution.py:148
  129.9 6.2 %pad_convert_fusion = f32[64,96,512]{2,1,0:T(8,128)} fusion(bf16[64,16,512]{2,1,0:T(8,128)(2,1)S(1)} %all-to-all-done.2), kind=kLoop, calls=%fused_computation.16 | loop fusion | flops 3145728 | bytes 13631488 | tf_op jit(solution)/shard_map/jit(_pad)/pad | solution.py:155
  136.1 0.0 collective-permute-done.4
  136.1 0.7 convert_dynamic-update-slice_fusion.3
  136.8 0.0 collective-permute-done.5
  136.8 0.7 convert_dynamic-update-slice_fusion.2
  137.5 0.0 collective-permute-done.6
  137.5 0.7 convert_dynamic-update-slice_fusion.1
  138.2 0.7 convert_dynamic-update-slice_fusion
  138.9 11.1 %fusion.2 = (bf16[6144,512]{1,0:T(8,128)(2,1)}, bf16[6144,512]{1,0:T(8,128)(2,1)}) fusion(f32[64,96,512]{2,1,0:T(8,128)} %convert_dynamic-update-slice_fusion), kind=kLoop, calls=%fused_computation.5 | loop fusion | flops 12582912 | bytes 25165824 | tf_op jit(solution)/shard_map/convert_element_type | solution.py:168
  149.9 5.1 %fusion.3 = f32[320,512]{1,0:T(8,128)S(1)} fusion(bf16[6144,512]{1,0:T(8,128)(2,1)} %get-tuple-element.6, s32[6144]{0:T(1024)S(1)} %eq.67), kind=kOutput, calls=%fused_computation.8 | convolution fusion | flops 2015232000 | bytes 6971392 | tf_op jit(solution)/shard_map/dot_general | solution.py:68
  155.1 0.0 copy-start.10
  155.1 0.0 copy-start.11
  155.1 0.0 copy-start.4
  155.1 0.0 copy-start.6
  155.1 0.0 copy-start.12
  155.1 0.0 copy-start.1
  155.2 4.2 %fusion.26 = bf16[320,512]{1,0:T(8,128)(2,1)} fusion(f32[320,512]{1,0:T(8,128)S(1)} %fusion.3, bf16[6144,512]{1,0:T(8,128)(2,1)S(1)} %copy-done.2, s32[6144]{0:T(1024)S(1)} %eq.67, f32[6464,512]{1,0:T(8,128)} %fusion.5), kind=kOutput, calls=%fused_computation.32 | convolution fusion | flops 2015723520 | bytes 7954432 | tf_op jit(solution)/shard_map/dot_general | solution.py:68
  159.3 3.5 %all-to-all-start.3 = ((bf16[4,80,512]{2,1,0:T(8,128)(2,1)}), bf16[4,80,512]{2,1,0:T(8,128)(2,1)S(1)}, u32[]{:S(2)}, u32[]{:S(2)}) async-start(bf16[4,80,512]{2,1,0:T(8,128)(2,1)} %bitcast.22), calls=%async_computation.3 | async-start | bytes 655360 | tf_op jit(solution)/shard_map/all_to_all | solution.py:44
  162.8 1.0 copy.19
  163.8 6.7 %all-to-all-done.3 = bf16[4,80,512]{2,1,0:T(8,128)(2,1)S(1)} async-done(((bf16[4,80,512]{2,1,0:T(8,128)(2,1)}), bf16[4,80,512]{2,1,0:T(8,128)(2,1)S(1)}, u32[]{:S(2)}, u32[]{:S(2)}) %all-to-all-start.3) | async-done | bytes 327712 | tf_op jit(solution)/shard_map/all_to_all | solution.py:44
  170.6 1.8 %fusion.68 = (f32[80]{0:T(128)S(1)}, f32[80,512]{1,0:T(8,128)S(1)}) fusion(bf16[512,512]{1,0:T(8,128)(2,1)S(1)} %copy-done.12, bf16[1024,512]{1,0:T(8,128)(2,1)} %param.24, bf16[80,512]{1,0:T(8,128)(2,1)S(1)} %reduce_sum.50, bf16[80,512]{1,0:T(8,128)(2,1)S(1)} %copy-done.6), kind=kOutput, calls=%fused_computation.94 | convolution fusion | flops 126402480 | bytes 1900864 | tf_op jit(solution)/shard_map/dot_general | solution.py:59
  172.4 0.2 multiply_reduce_fusion.1
  172.6 0.8 add_convert_fusion
  (31 shorter events, 0.2 us)
Async XLA Ops:
  0.6 72.7 %copy-start = (bf16[1536,512]{1,0:T(8,128)(2,1)S(1)}, bf16[1536,512]{1,0:T(8,128)(2,1)}, u32[]{:S(2)}) copy-start(bf16[1536,512]{1,0:T(8,128)(2,1)} %param.20) | copy-start | bytes 4718596
  2.4 10.7 %all-to-all-start = ((bf16[4,80,512]{2,1,0:T(8,128)(2,1)}), bf16[4,80,512]{2,1,0:T(8,128)(2,1)S(1)}, u32[]{:S(2)}, u32[]{:S(2)}) async-start(bf16[4,80,512]{2,1,0:T(8,128)(2,1)} %broadcast_in_dim.77), calls=%async_computation | async-start | bytes 655360 | tf_op jit(solution)/shard_map/all_to_all | solution.py:23
  13.1 23.6 %copy-start.8 = (bf16[512]{0:T(512)(128)(2,1)S(1)}, bf16[512]{0:T(512)(128)(2,1)}, u32[]{:S(2)}) copy-start(bf16[512]{0:T(512)(128)(2,1)} %param.22) | copy-start | bytes 3076
  13.1 23.6 %copy-start.9 = (bf16[512]{0:T(512)(128)(2,1)S(1)}, bf16[512]{0:T(512)(128)(2,1)}, u32[]{:S(2)}) copy-start(bf16[512]{0:T(512)(128)(2,1)} %param.23) | copy-start | bytes 3076
  13.1 23.6 %copy-start.7 = (s32[512]{0:T(512)S(1)}, s32[512]{0:T(512)}, u32[]{:S(2)}) copy-start(s32[512]{0:T(512)} %param.17) | copy-start | bytes 6148
  13.1 32.2 %copy-start.13 = (s32[512]{0:T(512)S(1)}, s32[512]{0:T(512)}, u32[]{:S(2)}) copy-start(s32[512]{0:T(512)} %param.16) | copy-start | bytes 6148
  16.9 2.7 %copy-start.5 = (bf16[6144,512]{1,0:T(8,128)(2,1)}, bf16[6144,512]{1,0:T(8,128)(2,1)S(1)}, u32[]{:S(2)}) copy-start(bf16[6144,512]{1,0:T(8,128)(2,1)S(1)} %convolution_convert_fusion) | copy-start | bytes 18874372
  20.6 43.7 %all-to-all-start.1 = ((bf16[64,16,512]{2,1,0:T(8,128)(2,1)}), bf16[64,16,512]{2,1,0:T(8,128)(2,1)S(1)}, u32[]{:S(2)}, u32[]{:S(2)}) async-start(bf16[64,16,512]{2,1,0:T(8,128)(2,1)} %slice.17), calls=%async_computation.1 | async-start | bytes 2097152 | tf_op jit(solution)/shard_map/all_to_all | solution.py:110
  38.6 26.6 %collective-permute-start = (bf16[96,512]{1,0:T(8,128)(2,1)}, bf16[96,512]{1,0:T(8,128)(2,1)}, u32[]{:S(2)}, u32[]{:S(2)}) collective-permute-start(bf16[96,512]{1,0:T(8,128)(2,1)} %get-tuple-element.15), channel_id=1, source_target_pairs={{0,8},{4,12},{8,16},{12,20},{16,24},{20,28},{24,32},{28,36},{32,40... | collective-permute-start | bytes 294920 | tf_op jit(solution)/shard_map/ppermute | solution.py:34
  39.9 26.1 %collective-permute-start.1 = (bf16[96,512]{1,0:T(8,128)(2,1)}, bf16[96,512]{1,0:T(8,128)(2,1)}, u32[]{:S(2)}, u32[]{:S(2)}) collective-permute-start(bf16[96,512]{1,0:T(8,128)(2,1)} %get-tuple-element.14), channel_id=1, source_target_pairs={{0,4},{4,8},{8,12},{12,16},{16,20},{20,24},{24,28},{28,32},{32,36}... | collective-permute-start | bytes 294920 | tf_op jit(solution)/shard_map/ppermute | solution.py:34
  41.7 25.3 %collective-permute-start.2 = (bf16[96,512]{1,0:T(8,128)(2,1)}, bf16[96,512]{1,0:T(8,128)(2,1)}, u32[]{:S(2)}, u32[]{:S(2)}) collective-permute-start(bf16[96,512]{1,0:T(8,128)(2,1)} %get-tuple-element.13), channel_id=1, source_target_pairs={{0,252},{4,0},{8,4},{12,8},{16,12},{20,16},{24,20},{28,24},{32,28}... | collective-permute-start | bytes 294920 | tf_op jit(solution)/shard_map/ppermute | solution.py:34
  41.7 26.2 %collective-permute-start.3 = (bf16[96,512]{1,0:T(8,128)(2,1)}, bf16[96,512]{1,0:T(8,128)(2,1)}, u32[]{:S(2)}, u32[]{:S(2)}) collective-permute-start(bf16[96,512]{1,0:T(8,128)(2,1)} %get-tuple-element.12), channel_id=1, source_target_pairs={{0,248},{4,252},{8,0},{12,4},{16,8},{20,12},{24,16},{28,20},{32,24... | collective-permute-start | bytes 294920 | tf_op jit(solution)/shard_map/ppermute | solution.py:34
  76.9 7.1 %copy-start.3 = (bf16[512,512]{0,1:T(8,128)(2,1)}, bf16[512,512]{0,1:T(8,128)(2,1)S(1)}, u32[]{:S(2)}) copy-start(bf16[512,512]{0,1:T(8,128)(2,1)S(1)} %fusion.27) | copy-start | bytes 1572868
  94.3 35.6 %all-to-all-start.2 = ((bf16[64,16,512]{2,1,0:T(8,128)(2,1)}), bf16[64,16,512]{2,1,0:T(8,128)(2,1)S(1)}, u32[]{:S(2)}, u32[]{:S(2)}) async-start(bf16[64,16,512]{2,1,0:T(8,128)(2,1)} %slice.23), calls=%async_computation.2 | async-start | bytes 2097152 | tf_op jit(solution)/shard_map/all_to_all | solution.py:148
  101.3 34.8 %collective-permute-start.4 = (bf16[96,512]{1,0:T(8,128)(2,1)S(1)}, bf16[96,512]{1,0:T(8,128)(2,1)S(1)}, u32[]{:S(2)}, u32[]{:S(2)}) collective-permute-start(bf16[96,512]{1,0:T(8,128)(2,1)S(1)} %get-tuple-element.11), channel_id=1, source_target_pairs={{0,248},{4,252},{8,0},{12,4},{16,8},{20,12},{24,16},{28,20},{32,24... | collective-permute-start | bytes 294920 | tf_op jit(solution)/shard_map/ppermute | solution.py:34
  106.4 30.4 %collective-permute-start.5 = (bf16[96,512]{1,0:T(8,128)(2,1)S(1)}, bf16[96,512]{1,0:T(8,128)(2,1)S(1)}, u32[]{:S(2)}, u32[]{:S(2)}) collective-permute-start(bf16[96,512]{1,0:T(8,128)(2,1)S(1)} %get-tuple-element.10), channel_id=1, source_target_pairs={{0,252},{4,0},{8,4},{12,8},{16,12},{20,16},{24,20},{28,24},{32,28}... | collective-permute-start | bytes 294920 | tf_op jit(solution)/shard_map/ppermute | solution.py:34
  107.0 30.4 %collective-permute-start.6 = (bf16[96,512]{1,0:T(8,128)(2,1)S(1)}, bf16[96,512]{1,0:T(8,128)(2,1)S(1)}, u32[]{:S(2)}, u32[]{:S(2)}) collective-permute-start(bf16[96,512]{1,0:T(8,128)(2,1)S(1)} %get-tuple-element.9), channel_id=1, source_target_pairs={{0,4},{4,8},{8,12},{12,16},{16,20},{20,24},{24,28},{28,32},{32,36}... | collective-permute-start | bytes 294920 | tf_op jit(solution)/shard_map/ppermute | solution.py:34
  108.1 30.0 %collective-permute-start.7 = (bf16[96,512]{1,0:T(8,128)(2,1)S(1)}, bf16[96,512]{1,0:T(8,128)(2,1)S(1)}, u32[]{:S(2)}, u32[]{:S(2)}) collective-permute-start(bf16[96,512]{1,0:T(8,128)(2,1)S(1)} %get-tuple-element.8), channel_id=1, source_target_pairs={{0,8},{4,12},{8,16},{12,20},{16,24},{20,28},{24,32},{28,36},{32,40... | collective-permute-start | bytes 294920 | tf_op jit(solution)/shard_map/ppermute | solution.py:34
  149.9 5.1 %copy-start.2 = (bf16[6144,512]{1,0:T(8,128)(2,1)S(1)}, bf16[6144,512]{1,0:T(8,128)(2,1)}, u32[]{:S(2)}) copy-start(bf16[6144,512]{1,0:T(8,128)(2,1)} %get-tuple-element.7) | copy-start | bytes 18874372
  155.1 7.7 %copy-start.10 = (bf16[512]{0:T(512)(128)(2,1)S(1)}, bf16[512]{0:T(512)(128)(2,1)}, u32[]{:S(2)}) copy-start(bf16[512]{0:T(512)(128)(2,1)} %param.26) | copy-start | bytes 3076
  155.1 7.7 %copy-start.11 = (bf16[512]{0:T(512)(128)(2,1)S(1)}, bf16[512]{0:T(512)(128)(2,1)}, u32[]{:S(2)}) copy-start(bf16[512]{0:T(512)(128)(2,1)} %param.27) | copy-start | bytes 3076
  155.1 7.7 %copy-start.4 = (bf16[512,512]{0,1:T(8,128)(2,1)S(1)}, bf16[512,512]{0,1:T(8,128)(2,1)}, u32[]{:S(2)}) copy-start(bf16[512,512]{0,1:T(8,128)(2,1)} %copy-done.3) | copy-start | bytes 1572868
  155.1 15.5 %copy-start.6 = (bf16[80,512]{1,0:T(8,128)(2,1)S(1)}, bf16[80,512]{1,0:T(8,128)(2,1)}, u32[]{:S(2)}) copy-start(bf16[80,512]{1,0:T(8,128)(2,1)} %param.14) | copy-start | bytes 245764
  155.1 15.5 %copy-start.12 = (bf16[512,512]{1,0:T(8,128)(2,1)S(1)}, bf16[512,512]{1,0:T(8,128)(2,1)}, u32[]{:S(2)}) copy-start(bf16[512,512]{1,0:T(8,128)(2,1)} %param.25) | copy-start | bytes 1572868
  155.1 18.3 %copy-start.1 = (bf16[1536,512]{1,0:T(8,128)(2,1)S(1)}, bf16[1536,512]{1,0:T(8,128)(2,1)}, u32[]{:S(2)}) copy-start(bf16[1536,512]{1,0:T(8,128)(2,1)} %param.20) | copy-start | bytes 4718596
  159.3 11.2 %all-to-all-start.3 = ((bf16[4,80,512]{2,1,0:T(8,128)(2,1)}), bf16[4,80,512]{2,1,0:T(8,128)(2,1)S(1)}, u32[]{:S(2)}, u32[]{:S(2)}) async-start(bf16[4,80,512]{2,1,0:T(8,128)(2,1)} %bitcast.22), calls=%async_computation.3 | async-start | bytes 655360 | tf_op jit(solution)/shard_map/all_to_all | solution.py:44
where the time goes:
time: 174 us; the launch traced here: 173 us
  waiting for transfers between devices  51.3 us (29%)
  starting transfers between devices  41.8 us (24%)
  matrix products  30.8 us (18%)
  local copies, waits for them, and re-layouts  26.2 us (15%)
  other arithmetic  21.6 us (12%)
    all_to_all x1, waiting for transfers between devices, per_device(): lax.all_to_all(partial_value[:, :far_count].astype(jnp.bfloat16), 'graph'...  21.8 us
    all_to_all x1, waiting for transfers between devices, per_device(): lax.all_to_all(outgoing[:, :far_count], 'graph', split_axis=0, concat_axi...  17.8 us
    dot_general x3, matrix products, sum_into(): lax.dot_general(selector, values, (((0,), (0,)), ((), ())), preferred_ele...  16.4 us
    all_to_all x1, starting transfers between devices, per_device(): lax.all_to_all(outgoing[:, :far_count], 'graph', split_axis=0, concat_axi...  14.1 us
    ppermute x8, starting transfers between devices, passed_along(): lax.ppermute(value, axis, [(i, (i + by) % devices) for i in range(devices)])  13.5 us
    convert_element_type x1, other arithmetic, per_device(): (flat_returned - upper_part.astype(jnp.float32)).astype(jnp.bfloat16)  11.1 us
    slice x1, local copies, waits for them, and re-layouts, per_device(): segment_totals[NODE_DEV:].reshape(groups, SLOT, feature_width)  7.98 us
    all_to_all x1, waiting for transfers between devices, sum_at_owner(): lax.all_to_all(tiles, axis, split_axis=0, concat_axis=0, tiled=True)  6.71 us
  transfers between devices with their start and end apart: 12, of which 4 were waited for; matrix products, arithmetic and copies ran while one was open for 11% of the time, Pallas kernels for 0%

commit v1 on v0

v1 whole, which is shorter than its diff:
```python
import functools

import jax
import jax.numpy as jnp
from jax import lax
from jax.experimental import pallas as pl
from jax.experimental.pallas import tpu as pltpu
from jax.sharding import PartitionSpec as P

D = 512
Q = 128
FEAT = 4
GROUPS = 64
NODES = 320
OWN = 80
SLOT = 96
FAR = 16
NEAR = SLOT - FAR
EDGES = 512
REGION_EDGES = FEAT * EDGES
OFFSETS = (-2, -1, 1, 2)
FAR_ROWS = GROUPS * FAR
NEAR_ROWS = len(OFFSETS) * NEAR
LIST_ROWS = FAR_ROWS + NEAR_ROWS
EPSILON = 1e-05
F32 = jnp.float32
BF16 = jnp.bfloat16
I32 = jnp.int32


def dot(a, b):
    return jnp.dot(a, b, preferred_element_type=F32)


def iota(shape, dim):
    return lax.broadcasted_iota(I32, shape, dim)


def column(row):
    return jnp.transpose(jnp.broadcast_to(row, (Q, Q)))


def widened(tile, width):
    full, rest = divmod(width, Q)
    parts = [tile] * full + ([tile[:, :rest]] if rest else [])
    return jnp.concatenate(parts, axis=1)


def hot(mask):
    return jnp.where(mask, 1.0, 0.0).astype(BF16)


def call(body, outs, scratch=(), flops=10**8):
    return pl.pallas_call(
        body,
        out_shape=outs,
        scratch_shapes=list(scratch),
        cost_estimate=pl.CostEstimate(flops=flops, bytes_accessed=10**6, transcendentals=0),
    )


def shape(dims, kind):
    return jax.ShapeDtypeStruct(dims, kind)


def project_body(nodes, w1, senders, refs, out, scratch):
    rows = nodes[...]
    sent = dot(rows, w1[D : 2 * D, :]).astype(BF16)
    taken = dot(rows, w1[2 * D : 3 * D, :]).astype(BF16)
    scratch[0:4, :] = senders[...]
    scratch[4:8, :] = refs[...]
    both = scratch[...]
    planes = jnp.concatenate(
        [lax.shift_right_logical(both, 7).astype(F32), (both & 127).astype(F32)], axis=0
    ).astype(BF16)
    for q in range(FEAT):
        cols = slice(q * Q, (q + 1) * Q)
        out[q, 0:OWN, 0:Q] = taken[:, cols]
        out[q, 0:OWN, Q : 2 * Q] = sent[:, cols]
        out[q, OWN : OWN + 16, 0:Q] = planes
        out[q, OWN : OWN + 16, Q : 2 * Q] = jnp.zeros((16, Q), BF16)


def lists_body(lists, select, spread):
    for b in range(8):
        col = column(lists[b : b + 1, :])
        select[b * Q : (b + 1) * Q, :] = hot(widened(col, NODES) == iota((Q, NODES), 1))
    for j in range(4):
        col = column(lists[8 + j : 9 + j, :])[:NEAR]
        at = FAR_ROWS + j * NEAR
        select[at : at + NEAR, :] = hot(widened(col, NODES) == iota((NEAR, NODES), 1))
    for b in range(12):
        spread[:, b * Q : (b + 1) * Q] = hot(
            jnp.broadcast_to(lists[b : b + 1, :], (NODES, Q)) == iota((NODES, Q), 0)
        )


def select_body(table, select, far, near0, near1, near2, near3):
    rows = jnp.concatenate([table[q, 0:OWN, 0:Q] for q in range(FEAT)], axis=0)
    for b in range(4):
        picked = dot(select[b * 256 : (b + 1) * 256, :], rows).astype(BF16)
        far[b * 16 : (b + 1) * 16] = picked.reshape(16, FAR, Q)
    for j, out in enumerate((near0, near1, near2, near3)):
        at = FAR_ROWS + j * NEAR
        out[...] = dot(select[at : at + NEAR, :], rows).astype(BF16)


def local_body(table, rowid, cols, acc):
    region = lax.axis_index("graph")
    both = jnp.concatenate(
        [table[q, 0:OWN, 0:Q] for q in range(FEAT)]
        + [table[q, 0:OWN, Q : 2 * Q] for q in range(FEAT)],
        axis=0,
    )
    for q in range(FEAT):
        planes = table[q, OWN : OWN + 16, 0:Q].astype(F32)
        ids = (planes[0:8] * 128.0 + planes[8:16]).astype(I32)
        ref = ids
        offset = jnp.maximum(ref - NODES, 0)
        source = lax.shift_right_logical(lax.shift_right_logical(offset, 5) * 171, 9)
        slot = offset - source * SLOT
        apart = (source - region) & (GROUPS - 1)
        which = jnp.where(apart >= GROUPS - 2, apart - (GROUPS - 2), apart + 1)
        listed = jnp.where(
            slot < FAR,
            NODES + source * FAR + slot,
            NODES + FAR_ROWS + which * NEAR + slot - FAR,
        )
        ref = jnp.where(ref < NODES, ref, listed)
        rowid[q * 4 : (q + 1) * 4, :] = ref[4:8]
        for r in range(4):
            e = (q * 4 + r) * Q
            taken = column(ref[4 + r : 5 + r, :])
            sent = column(ids[r : r + 1, :])
            cols[e : e + Q, :] = taken
            picks = jnp.concatenate(
                [
                    hot(widened(taken, NODES) == iota((Q, NODES), 1)),
                    hot(widened(sent, NODES) == iota((Q, NODES), 1)),
                ],
                axis=1,
            )
            acc[e : e + Q, :] = dot(picks, both)


def gather_body(acc, cols, far, near0, near1, near2, near3, out):
    table = [far[b * 16 : (b + 1) * 16].reshape(256, Q) for b in range(4)]
    table.append(jnp.concatenate([near0[...], near1[...], near2[...], near3[...]], axis=0))
    for m in range(8):
        col = cols[m * 256 : (m + 1) * 256, :]
        total = acc[m * 256 : (m + 1) * 256, :]
        for b in range(5):
            width = table[b].shape[0]
            picks = hot(widened(col, width) == iota((256, width), 1) + (NODES + b * 256))
            total += dot(picks, table[b])
        at = (m % 2) * 256
        out[m // 2, at : at + 256, :] = total.astype(BF16)


def normed(outputs, gain, shift):
    average = jnp.mean(outputs, axis=-1, keepdims=True)
    centered = outputs - average
    variance = jnp.mean(centered * centered, axis=-1, keepdims=True)
    return centered * lax.rsqrt(variance + EPSILON) * gain + shift


def silu(v):
    return v / (1.0 + jnp.exp(-v))


def edge_body(count, edges, picked, w1, w2, gain, shift, new_edges, messages):
    scale = gain[...].astype(F32)
    move = shift[...].astype(F32)
    first = lax.axis_index("feat") * EDGES
    for m in range(2):
        rows = slice(m * 256, (m + 1) * 256)
        feats = edges[rows, :]
        pre = dot(feats, w1[0:D, :])
        pre += jnp.concatenate([picked[q, rows, :] for q in range(FEAT)], axis=1).astype(F32)
        hidden = silu(pre).astype(BF16)
        update = normed(dot(hidden, w2[...]), scale, move)
        live = first + m * 256 + iota((256, D), 0) < count[0]
        result = feats.astype(F32) + jnp.where(live, update, 0.0)
        new_edges[rows, :] = result.astype(BF16)
        kept = jnp.where(live, result, 0.0).astype(BF16)
        for q in range(FEAT):
            messages[q, rows, :] = kept[:, q * Q : (q + 1) * Q]


def sums_body(messages, rowid, own, far, near0, near1, near2, near3):
    blocks = [(0, 320), (320, 256), (576, 256), (832, 256), (1088, 256), (1344, 320)]
    for base, size in blocks:
        total = jnp.zeros((size, Q), F32)
        for c in range(8):
            q, half = divmod(c, 2)
            ids = jnp.concatenate([rowid[2 * c : 2 * c + 1, :], rowid[2 * c + 1 : 2 * c + 2, :]], axis=1)
            picks = hot(jnp.broadcast_to(ids, (size, 256)) == iota((size, 256), 0) + base)
            total += dot(picks, messages[q, half * 256 : (half + 1) * 256, :])
        if base == 0:
            own[...] = total
        elif base < NODES + FAR_ROWS:
            at = (base - NODES) // FAR
            far[at : at + 16] = total.astype(BF16).reshape(16, FAR, Q)
        else:
            for j, out in enumerate((near0, near1, near2, near3)):
                out[...] = total[j * NEAR : (j + 1) * NEAR].astype(BF16)


def spread_body(spread, own, far, near0, near1, near2, near3, out):
    total = own[...]
    for b in range(4):
        total += dot(
            spread[:, b * 256 : (b + 1) * 256], far[b * 16 : (b + 1) * 16].reshape(256, Q)
        )
    for j, near in enumerate((near0, near1, near2, near3)):
        at = FAR_ROWS + j * Q
        total += dot(spread[:, at : at + NEAR], near[...])
    total = total.astype(BF16)
    for q in range(FEAT):
        out[q] = total[q * OWN : (q + 1) * OWN]


def node_body(nodes, sums, w1, w2, gain, shift, out):
    feats = nodes[...]
    pre = dot(feats, w1[0:D, :])
    pre += dot(jnp.concatenate([sums[q] for q in range(FEAT)], axis=1), w1[D : 2 * D, :])
    hidden = silu(pre).astype(BF16)
    update = normed(dot(hidden, w2[...]), gain[...].astype(F32), shift[...].astype(F32))
    out[...] = (feats.astype(F32) + update).astype(BF16)


def swapped(value, axis):
    return lax.all_to_all(value, axis, split_axis=0, concat_axis=0, tiled=True)


def moved(value, by):
    return lax.ppermute(value, "graph", [(i, (i + by) % GROUPS) for i in range(GROUPS)])


def per_device(
    node_feats,
    edge_feats,
    senders,
    receiver_ref,
    send_list,
    edge_count,
    edge_w1,
    edge_w2,
    edge_gain,
    edge_shift,
    node_w1,
    node_w2,
    node_gain,
    node_shift,
):
    region = lax.axis_index("graph")
    projected = call(
        project_body, shape((FEAT, 96, 256), BF16), [pltpu.VMEM((8, Q), I32)]
    )(node_feats, edge_w1, senders.reshape(4, Q), receiver_ref.reshape(4, Q))
    table = swapped(projected, "feat")

    rows = send_list[0]
    near_lists = [
        jnp.pad(
            lax.dynamic_slice(rows, ((region - d) % GROUPS, FAR), (1, NEAR)),
            ((0, 0), (0, Q - NEAR)),
            constant_values=-1,
        )
        for d in OFFSETS
    ]
    lists = jnp.concatenate([rows[:, :FAR].reshape(8, Q)] + near_lists, axis=0)
    select, spread = call(
        lists_body, (shape((LIST_ROWS, NODES), BF16), shape((NODES, 12 * Q), BF16))
    )(lists)

    near_shape = [shape((NEAR, Q), BF16)] * 4
    far_shape = shape((GROUPS, FAR, Q), BF16)
    far, *near = call(select_body, (far_shape, *near_shape))(table, select)
    far = swapped(far, "graph")
    near = [moved(value, -d) for value, d in zip(near, OFFSETS)]

    rowid, cols, acc = call(
        local_body,
        (
            shape((16, Q), I32),
            shape((REGION_EDGES, Q), I32),
            shape((REGION_EDGES, Q), F32),
        ),
        flops=10**9,
    )(table)
    picked = call(gather_body, shape((FEAT, EDGES, Q), BF16), flops=10**9)(
        acc, cols, far, *near
    )
    picked = swapped(picked, "feat")

    new_edges, messages = pl.pallas_call(
        edge_body,
        out_shape=(shape((EDGES, D), BF16), shape((FEAT, EDGES, Q), BF16)),
        in_specs=[pl.BlockSpec(memory_space=pltpu.SMEM)]
        + [pl.BlockSpec(memory_space=pltpu.VMEM)] * 6,
        cost_estimate=pl.CostEstimate(flops=10**9, bytes_accessed=10**6, transcendentals=0),
    )(
        edge_count,
        edge_feats,
        picked,
        edge_w1,
        edge_w2,
        edge_gain.reshape(1, D),
        edge_shift.reshape(1, D),
    )
    messages = swapped(messages, "feat")

    own, far, *near = call(
        sums_body, (shape((NODES, Q), F32), far_shape, *near_shape), flops=10**9
    )(messages, rowid)
    far = swapped(far, "graph")
    near = [moved(value, d) for value, d in zip(near, OFFSETS)]
    sums = call(spread_body, shape((FEAT, OWN, Q), BF16))(spread, own, far, *near)
    sums = swapped(sums, "feat")
    new_nodes = call(node_body, shape((OWN, D), BF16))(
        node_feats, sums, node_w1, node_w2, node_gain.reshape(1, D), node_shift.reshape(1, D)
    )
    return (new_edges, new_nodes)


def solution(mesh):
    split = P(("graph", "feat"))
    return jax.shard_map(
        per_device,
        mesh=mesh,
        in_specs=(split, split, split, split, P("graph"), P("graph")) + (P(),) * 8,
        out_specs=(split, split),
        check_vma=False,
    )
```

time: 174 us -> 117 us (0.67)
  matrix products: 30.8 us -> 0 us
  waiting for transfers between devices: 51.3 us -> 21.4 us
  Pallas kernels: 0 us -> 27.9 us
  other arithmetic: 21.6 us -> 0 us
  local copies, waits for them, and re-layouts: 26.2 us -> 7.2 us
  blocking collectives: 0 us -> 12.6 us
  starting transfers between devices: 41.8 us -> 45.2 us
    all_to_all x4 -> x5, waiting for transfers between devices: 51.3 us -> 14.9 us  [swapped(): return lax.all_to_all(value, axis, split_axis=0, concat_axis=0, tiled=True)]
    dot_general x8 -> x0, matrix products: 30.8 us -> none  [the longest x3 16.4 us: sum_into(): lax.dot_general(selector, values, (((0,), (0,)), ((), ())), preferred_ele...]
    pallas_call x0 -> x9, Pallas kernels: none -> 27.9 us  [the longest x1 4.31 us: per_device(): pl.pallas_call(edge_body, out_shape=(shape((EDGES, D), BF16), shape((FEAT...]
    all_to_all x0 -> x1, blocking collectives: none -> 12.6 us  [swapped(): return lax.all_to_all(value, axis, split_axis=0, concat_axis=0, tiled=True)]
    convert_element_type x7 -> x0, other arithmetic: 12.2 us -> none  [the longest x1 11.1 us: per_device(): (flat_returned - upper_part.astype(jnp.float32)).astype(jnp.bfloat16)]
    slice x3 -> x0, local copies, waits for them, and re-layouts: 11.3 us -> none  [the longest x1 7.98 us: per_device(): segment_totals[NODE_DEV:].reshape(groups, SLOT, feature_width)]
    ppermute x8, waiting for transfers between devices: 0.02 us -> 6.51 us  [moved(): lax.ppermute(value, 'graph', [(i, (i + by) % GROUPS) for i in range(GROUP...]
    pad x1 -> x0, other arithmetic: 6.2 us -> none  [per_device(): returned = jnp.pad(far_back, ((0, 0), (0, quarter - far_count), (0, 0)))]
  transfers between devices with their start and end apart: 12 -> 13, of which waited for: 4 -> 6; matrix products, arithmetic and copies ran while one was open for 11% -> 3% of each run, Pallas kernels for 0% -> 5%
where the time goes in v1:
time: 117 us; the launch traced here: 116 us
  starting transfers between devices  45.2 us (39%)
  Pallas kernels  27.9 us (24%)
  waiting for transfers between devices  21.4 us (18%)
  blocking collectives  12.6 us (11%)
  local copies, waits for them, and re-layouts  7.2 us (6%)
  between operations  1.46 us (1%)
    all_to_all x5, starting transfers between devices, swapped(): return lax.all_to_all(value, axis, split_axis=0, concat_axis=0, tiled=True)  31.6 us
    all_to_all x5, waiting for transfers between devices, swapped(): return lax.all_to_all(value, axis, split_axis=0, concat_axis=0, tiled=True)  14.9 us
    ppermute x8, starting transfers between devices, moved(): lax.ppermute(value, 'graph', [(i, (i + by) % GROUPS) for i in range(GROUP...  13.6 us
    all_to_all x1, blocking collectives, swapped(): return lax.all_to_all(value, axis, split_axis=0, concat_axis=0, tiled=True)  12.6 us
    ppermute x8, waiting for transfers between devices, moved(): lax.ppermute(value, 'graph', [(i, (i + by) % GROUPS) for i in range(GROUP...  6.51 us
    pallas_call x1, Pallas kernels, per_device(): pl.pallas_call(edge_body, out_shape=(shape((EDGES, D), BF16), shape((FEAT...  4.31 us
    pallas_call x1, Pallas kernels, per_device(): call(gather_body, shape((FEAT, EDGES, Q), BF16), flops=10 ** 9)  4.09 us
    pallas_call x1, Pallas kernels, per_device(): call(local_body, (shape((16, Q), I32), shape((REGION_EDGES, Q), I32), sha...  3.6 us
  transfers between devices with their start and end apart: 13, of which 6 were waited for; matrix products, arithmetic and copies ran while one was open for 3% of the time, Pallas kernels for 5%

profile of v1, /device:TPU:1, one launch (start us, length us, event | category | flops | bytes accessed | tf_op | source)
XLA Modules:
  0.0 115.8 jit_solution(4897395051520282838)
XLA Ops:
  0.6 0.0 copy-start.5
  0.6 2.4 %shard_map.149 = bf16[4,96,256]{2,1,0:T(8,128)(2,1)} custom-call(bf16[80,512]{1,0:T(8,128)(2,1)} %nodes.3, bf16[1536,512]{1,0:T(8,128)(2,1)} %w1.4, s32[4,128]{1,0:T(4,128)} %bitcast.13, s32[4,128]{1,0:T(4,128)} %bitcast.14), custom_call_target="tpu_custom_call" | custom-call | flops 100000000 | bytes 1000000 | tf_op jit(solution)/shard_map/pallas_call | solution.py:257
  3.0 4.8 %all-to-all-start = ((bf16[4,96,256]{2,1,0:T(8,128)(2,1)}), bf16[4,96,256]{2,1,0:T(8,128)(2,1)S(1)}, u32[]{:S(2)}, u32[]{:S(2)}) async-start(bf16[4,96,256]{2,1,0:T(8,128)(2,1)} %shard_map.149), calls=%async_computation | async-start | bytes 393216 | tf_op jit(solution)/shard_map/all_to_all | solution.py:233
  7.9 0.0 copy-done.5
  7.9 0.1 fusion.3
  8.0 0.1 reshape.31
  8.1 1.2 %concatenate.3.lists = s32[12,128]{1,0:T(8,128)} concatenate(s32[8,128]{1,0:T(8,128)S(1)} %reshape.31, s32[1,128]{1,0:T(1,128)S(1)} %pad.13, s32[1,128]{1,0:T(1,128)S(1)} %pad.14, s32[1,128]{1,0:T(1,128)S(1)} %pad.15, s32[1,128]{1,0:T(1,128)S(1)} %pad.16), dimensions={0} | concatenate | bytes 12288 | tf_op jit(solution)/shard_map/concatenate | solution.py:271
  9.3 2.3 %shard_map.151 = (bf16[1344,320]{1,0:T(8,128)(2,1)}, bf16[320,1536]{1,0:T(8,128)(2,1)}) custom-call(s32[12,128]{1,0:T(8,128)} %concatenate.3.lists), custom_call_target="tpu_custom_call" | custom-call | flops 100000000 | bytes 1000000 | tf_op jit(solution)/shard_map/pallas_call | solution.py:272
  11.6 1.5 %all-to-all-done.table = bf16[4,96,256]{2,1,0:T(8,128)(2,1)S(1)} async-done(((bf16[4,96,256]{2,1,0:T(8,128)(2,1)}), bf16[4,96,256]{2,1,0:T(8,128)(2,1)S(1)}, u32[]{:S(2)}, u32[]{:S(2)}) %all-to-all-start) | async-done | bytes 196640 | tf_op jit(solution)/shard_map/all_to_all | solution.py:233
  13.0 0.7 copy-done.1
  13.7 2.4 %shard_map.152 = (bf16[64,16,128]{2,1,0:T(8,128)(2,1)}, bf16[80,128]{1,0:T(8,128)(2,1)}, bf16[80,128]{1,0:T(8,128)(2,1)}, bf16[80,128]{1,0:T(8,128)(2,1)}, bf16[80,128]{1,0:T(8,128)(2,1)}) custom-call(bf16[4,96,256]{2,1,0:T(8,128)(2,1)} %copy-done.1, bf16[1344,320]{1,0:T(8,128)(2,1)} %get-tuple-element.22.select), custom_call_target="tpu_custom_call" | custom-call | flops 100000000 | bytes 1000000 | tf_op jit(solution)/shard_map/pallas_call | solution.py:278
  16.1 13.8 %all-to-all-start.1 = ((bf16[64,16,128]{2,1,0:T(8,128)(2,1)}), bf16[64,16,128]{2,1,0:T(8,128)(2,1)S(1)}, u32[]{:S(2)}, u32[]{:S(2)}) async-start(bf16[64,16,128]{2,1,0:T(8,128)(2,1)} %get-tuple-element.23), calls=%async_computation.1 | async-start | bytes 524288 | tf_op jit(solution)/shard_map/all_to_all | solution.py:233
  29.9 1.4 %collective-permute-start = (bf16[80,128]{1,0:T(8,128)(2,1)}, bf16[80,128]{1,0:T(8,128)(2,1)S(1)}, u32[]{:S(2)}, u32[]{:S(2)}) collective-permute-start(bf16[80,128]{1,0:T(8,128)(2,1)} %get-tuple-element.24), channel_id=1, source_target_pairs={{0,8},{4,12},{8,16},{12,20},{16,24},{20,28},{24,32},{28,36},{32,40... | collective-permute-start | bytes 61448 | tf_op jit(solution)/shard_map/ppermute | solution.py:237
  31.3 1.7 %collective-permute-start.1 = (bf16[80,128]{1,0:T(8,128)(2,1)}, bf16[80,128]{1,0:T(8,128)(2,1)S(1)}, u32[]{:S(2)}, u32[]{:S(2)}) collective-permute-start(bf16[80,128]{1,0:T(8,128)(2,1)} %get-tuple-element.25), channel_id=1, source_target_pairs={{0,4},{4,8},{8,12},{12,16},{16,20},{20,24},{24,28},{28,32},{32,36}... | collective-permute-start | bytes 61448 | tf_op jit(solution)/shard_map/ppermute | solution.py:237
  33.1 0.0 collective-permute-start.2
  33.1 3.6 %collective-permute-start.3 = (bf16[80,128]{1,0:T(8,128)(2,1)}, bf16[80,128]{1,0:T(8,128)(2,1)S(1)}, u32[]{:S(2)}, u32[]{:S(2)}) collective-permute-start(bf16[80,128]{1,0:T(8,128)(2,1)} %get-tuple-element.27), channel_id=1, source_target_pairs={{0,248},{4,252},{8,0},{12,4},{16,8},{20,12},{24,16},{28,20},{32,24... | collective-permute-start | bytes 61448 | tf_op jit(solution)/shard_map/ppermute | solution.py:237
  36.7 3.6 %shard_map.150 = (s32[16,128]{1,0:T(8,128)}, s32[2048,128]{1,0:T(8,128)}, f32[2048,128]{1,0:T(8,128)}) custom-call(bf16[4,96,256]{2,1,0:T(8,128)(2,1)} %copy-done.1), custom_call_target="tpu_custom_call" | custom-call | flops 1000000000 | bytes 1000000 | tf_op jit(solution)/shard_map/pallas_call | solution.py:282
  40.3 0.0 collective-permute-done.near0
  40.3 0.0 collective-permute-done.1.near1
  40.3 0.0 copy-start.15
  40.3 0.0 collective-permute-done.2.near2
  40.3 0.0 copy-start.16
  40.3 0.0 collective-permute-done.3.near3
  40.3 0.0 copy-start.17
  40.3 2.6 %all-to-all-done.1.far = bf16[64,16,128]{2,1,0:T(8,128)(2,1)S(1)} async-done(((bf16[64,16,128]{2,1,0:T(8,128)(2,1)}), bf16[64,16,128]{2,1,0:T(8,128)(2,1)S(1)}, u32[]{:S(2)}, u32[]{:S(2)}) %all-to-all-start.1) | async-done | bytes 262176 | tf_op jit(solution)/shard_map/all_to_all | solution.py:233
  43.0 0.0 copy-done.14
  43.0 0.0 copy-done.15
  43.0 0.0 copy-done.16
  43.0 0.0 copy-done.17
  43.0 0.7 copy-done.4
  43.6 4.1 %shard_map.153 = bf16[4,512,128]{2,1,0:T(8,128)(2,1)} custom-call(f32[2048,128]{1,0:T(8,128)} %get-tuple-element.20.acc, s32[2048,128]{1,0:T(8,128)} %get-tuple-element.21.cols, bf16[64,16,128]{2,1,0:T(8,128)(2,1)} %copy-done.4, bf16[80,128]{1,0:T(8,128)(2,1)} %copy-done.14, bf16[80,128]{1,0:T(8,128)(2,1)} %copy-done.15, bf16[80,128]{1,0:T(8,128)(2,1)} %copy-done.16, ...), custom_call_target="tpu_custom_call" | custom-call | flops 1000000000 | bytes 1000000 | tf_op jit(solution)/shard_map/pallas_call | solution.py:291
  47.7 3.5 %all-to-all-start.2 = ((bf16[4,512,128]{2,1,0:T(8,128)(2,1)}), bf16[4,512,128]{2,1,0:T(8,128)(2,1)S(1)}, u32[]{:S(2)}, u32[]{:S(2)}) async-start(bf16[4,512,128]{2,1,0:T(8,128)(2,1)} %shard_map.153), calls=%async_computation.2 | async-start | bytes 1048576 | tf_op jit(solution)/shard_map/all_to_all | solution.py:233
  51.2 0.0 copy-done.10
  51.2 0.6 reshape.32.gain
  51.8 0.0 copy-done.11
  51.8 0.6 reshape.33.shift
  53.0 7.4 %all-to-all-done.2.picked = bf16[4,512,128]{2,1,0:T(8,128)(2,1)S(1)} async-done(((bf16[4,512,128]{2,1,0:T(8,128)(2,1)}), bf16[4,512,128]{2,1,0:T(8,128)(2,1)S(1)}, u32[]{:S(2)}, u32[]{:S(2)}) %all-to-all-start.2) | async-done | bytes 524320 | tf_op jit(solution)/shard_map/all_to_all | solution.py:233
  60.5 0.8 copy-done.2
  61.3 4.3 %shard_map.154 = (bf16[512,512]{1,0:T(8,128)(2,1)}, bf16[4,512,128]{2,1,0:T(8,128)(2,1)}) custom-call(s32[1]{0:T(128)S(6)} %copy.16.count, bf16[512,512]{1,0:T(8,128)(2,1)} %edges.1, bf16[4,512,128]{2,1,0:T(8,128)(2,1)} %copy-done.2, bf16[1536,512]{1,0:T(8,128)(2,1)} %w1.4, bf16[512,512]{1,0:T(8,128)(2,1)} %w2.2, bf16[1,512]{1,0:T(2,128)(2,1)} %reshape.32.gain, ...), custom_call_target="tpu_custom_call" | custom-call | flops 1000000000 | bytes 1000000 | tf_op jit(solution)/shard_map/pallas_call | solution.py:296
  65.6 12.6 %all_to_all.30.messages = bf16[4,512,128]{2,1,0:T(8,128)(2,1)} all-to-all(bf16[4,512,128]{2,1,0:T(8,128)(2,1)} %get-tuple-element.30), channel_id=1, replica_groups=mesh['graph'=64,'feat'=4] {'feat'}, dimensions={0} | all-to-all | bytes 1048576 | tf_op jit(solution)/shard_map/all_to_all | solution.py:233
  78.2 3.6 %shard_map.155 = (f32[320,128]{1,0:T(8,128)}, bf16[64,16,128]{2,1,0:T(8,128)(2,1)}, bf16[80,128]{1,0:T(8,128)(2,1)}, bf16[80,128]{1,0:T(8,128)(2,1)}, bf16[80,128]{1,0:T(8,128)(2,1)}, /*index=5*/bf16[80,128]{1,0:T(8,128)(2,1)}) custom-call(bf16[4,512,128]{2,1,0:T(8,128)(2,1)} %all_to_all.30.messages, s32[16,128]{1,0:T(8,128)} %get-tuple-element.31.rowid), custom_call_target="tpu_custom_call" | custom-call | flops 1000000000 | bytes 1000000 | tf_op jit(solution)/shard_map/pallas_call | solution.py:313
  81.8 6.3 %all-to-all-start.4 = ((bf16[64,16,128]{2,1,0:T(8,128)(2,1)}), bf16[64,16,128]{2,1,0:T(8,128)(2,1)S(1)}, u32[]{:S(2)}, u32[]{:S(2)}) async-start(bf16[64,16,128]{2,1,0:T(8,128)(2,1)} %get-tuple-element.33), calls=%async_computation.4 | async-start | bytes 524288 | tf_op jit(solution)/shard_map/all_to_all | solution.py:233
  88.1 5.1 %collective-permute-start.4 = (bf16[80,128]{1,0:T(8,128)(2,1)}, bf16[80,128]{1,0:T(8,128)(2,1)S(1)}, u32[]{:S(2)}, u32[]{:S(2)}) collective-permute-start(bf16[80,128]{1,0:T(8,128)(2,1)} %get-tuple-element.34), channel_id=1, source_target_pairs={{0,248},{4,252},{8,0},{12,4},{16,8},{20,12},{24,16},{28,20},{32,24... | collective-permute-start | bytes 61448 | tf_op jit(solution)/shard_map/ppermute | solution.py:237
  93.2 0.7 collective-permute-start.5
  93.8 1.1 collective-permute-start.6
  94.9 0.0 collective-permute-start.7
  94.9 0.0 collective-permute-done.4.near0
  94.9 2.0 %collective-permute-done.5.near1 = bf16[80,128]{1,0:T(8,128)(2,1)S(1)} collective-permute-done((bf16[80,128]{1,0:T(8,128)(2,1)}, bf16[80,128]{1,0:T(8,128)(2,1)S(1)}, u32[]{:S(2)}, u32[]{:S(2)}) %collective-permute-start.5) | collective-permute-done | bytes 20512 | tf_op jit(solution)/shard_map/ppermute | solution.py:237
  96.9 0.0 collective-permute-done.6.near2
  96.9 4.5 %collective-permute-done.7.near3 = bf16[80,128]{1,0:T(8,128)(2,1)S(1)} collective-permute-done((bf16[80,128]{1,0:T(8,128)(2,1)}, bf16[80,128]{1,0:T(8,128)(2,1)S(1)}, u32[]{:S(2)}, u32[]{:S(2)}) %collective-permute-start.7) | collective-permute-done | bytes 20512 | tf_op jit(solution)/shard_map/ppermute | solution.py:237
  101.4 0.0 all-to-all-done.4.far
  101.4 0.0 copy-done.6
  101.4 0.0 copy-done.7
  101.4 0.0 copy-done.8
  101.4 0.6 copy-done.9
  102.0 0.1 copy-done
  102.1 2.4 %shard_map.156 = bf16[4,80,128]{2,1,0:T(8,128)(2,1)} custom-call(bf16[320,1536]{1,0:T(8,128)(2,1)} %get-tuple-element.29.spread, f32[320,128]{1,0:T(8,128)} %get-tuple-element.32.own, bf16[64,16,128]{2,1,0:T(8,128)(2,1)} %copy-done, bf16[80,128]{1,0:T(8,128)(2,1)} %copy-done.6, bf16[80,128]{1,0:T(8,128)(2,1)} %copy-done.7, bf16[80,128]{1,0:T(8,128)(2,1)} %copy-done.8, ...), custom_call_target="tpu_custom_call" | custom-call | flops 100000000 | bytes 1000000 | tf_op jit(solution)/shard_map/pallas_call | solution.py:318
  104.6 3.3 %all-to-all-start.5 = ((bf16[4,80,128]{2,1,0:T(8,128)(2,1)}), bf16[4,80,128]{2,1,0:T(8,128)(2,1)S(1)}, u32[]{:S(2)}, u32[]{:S(2)}) async-start(bf16[4,80,128]{2,1,0:T(8,128)(2,1)} %shard_map.156), calls=%async_computation.5 | async-start | bytes 163840 | tf_op jit(solution)/shard_map/all_to_all | solution.py:233
  107.9 0.6 reshape.34.gain
  108.5 0.0 copy-done.13
  108.5 0.6 reshape.35.shift
  109.1 3.3 %all-to-all-done.5.sums = bf16[4,80,128]{2,1,0:T(8,128)(2,1)S(1)} async-done(((bf16[4,80,128]{2,1,0:T(8,128)(2,1)}), bf16[4,80,128]{2,1,0:T(8,128)(2,1)S(1)}, u32[]{:S(2)}, u32[]{:S(2)}) %all-to-all-start.5) | async-done | bytes 81952 | tf_op jit(solution)/shard_map/all_to_all | solution.py:233
  112.4 0.6 copy-done.3
  113.0 2.8 %shard_map.157 = bf16[80,512]{1,0:T(8,128)(2,1)} custom-call(bf16[80,512]{1,0:T(8,128)(2,1)} %nodes.3, bf16[4,80,128]{2,1,0:T(8,128)(2,1)} %copy-done.3, bf16[1024,512]{1,0:T(8,128)(2,1)} %w1.5, bf16[512,512]{1,0:T(8,128)(2,1)} %w2.3, bf16[1,512]{1,0:T(2,128)(2,1)} %reshape.34.gain, bf16[1,512]{1,0:T(2,128)(2,1)} %reshape.35.shift), custom_call_target="tpu_custom_call" | custom-call | flops 100000000 | bytes 1000000 | tf_op jit(solution)/shard_map/pallas_call | solution.py:320
  (19 shorter events, 0.0 us)
Async XLA Ops:
  0.6 7.2 %copy-start.5 = (s32[1,64,96]{2,1,0:T(8,128)S(1)}, s32[1,64,96]{2,1,0:T(8,128)}, u32[]{:S(2)}) copy-start(s32[1,64,96]{2,1,0:T(8,128)} %param.18) | copy-start | bytes 73732
  3.0 10.0 %all-to-all-start = ((bf16[4,96,256]{2,1,0:T(8,128)(2,1)}), bf16[4,96,256]{2,1,0:T(8,128)(2,1)S(1)}, u32[]{:S(2)}, u32[]{:S(2)}) async-start(bf16[4,96,256]{2,1,0:T(8,128)(2,1)} %shard_map.149), calls=%async_computation | async-start | bytes 393216 | tf_op jit(solution)/shard_map/all_to_all | solution.py:233
  13.0 0.7 copy-start.1
  16.1 26.8 %all-to-all-start.1 = ((bf16[64,16,128]{2,1,0:T(8,128)(2,1)}), bf16[64,16,128]{2,1,0:T(8,128)(2,1)S(1)}, u32[]{:S(2)}, u32[]{:S(2)}) async-start(bf16[64,16,128]{2,1,0:T(8,128)(2,1)} %get-tuple-element.23), calls=%async_computation.1 | async-start | bytes 524288 | tf_op jit(solution)/shard_map/all_to_all | solution.py:233
  29.9 10.4 %collective-permute-start = (bf16[80,128]{1,0:T(8,128)(2,1)}, bf16[80,128]{1,0:T(8,128)(2,1)S(1)}, u32[]{:S(2)}, u32[]{:S(2)}) collective-permute-start(bf16[80,128]{1,0:T(8,128)(2,1)} %get-tuple-element.24), channel_id=1, source_target_pairs={{0,8},{4,12},{8,16},{12,20},{16,24},{20,28},{24,32},{28,36},{32,40... | collective-permute-start | bytes 61448 | tf_op jit(solution)/shard_map/ppermute | solution.py:237
  31.3 9.0 %collective-permute-start.1 = (bf16[80,128]{1,0:T(8,128)(2,1)}, bf16[80,128]{1,0:T(8,128)(2,1)S(1)}, u32[]{:S(2)}, u32[]{:S(2)}) collective-permute-start(bf16[80,128]{1,0:T(8,128)(2,1)} %get-tuple-element.25), channel_id=1, source_target_pairs={{0,4},{4,8},{8,12},{12,16},{16,20},{20,24},{24,28},{28,32},{32,36}... | collective-permute-start | bytes 61448 | tf_op jit(solution)/shard_map/ppermute | solution.py:237
  33.1 7.2 %collective-permute-start.2 = (bf16[80,128]{1,0:T(8,128)(2,1)}, bf16[80,128]{1,0:T(8,128)(2,1)S(1)}, u32[]{:S(2)}, u32[]{:S(2)}) collective-permute-start(bf16[80,128]{1,0:T(8,128)(2,1)} %get-tuple-element.26), channel_id=1, source_target_pairs={{0,252},{4,0},{8,4},{12,8},{16,12},{20,16},{24,20},{28,24},{32,28}... | collective-permute-start | bytes 61448 | tf_op jit(solution)/shard_map/ppermute | solution.py:237
  33.1 7.3 %collective-permute-start.3 = (bf16[80,128]{1,0:T(8,128)(2,1)}, bf16[80,128]{1,0:T(8,128)(2,1)S(1)}, u32[]{:S(2)}, u32[]{:S(2)}) collective-permute-start(bf16[80,128]{1,0:T(8,128)(2,1)} %get-tuple-element.27), channel_id=1, source_target_pairs={{0,248},{4,252},{8,0},{12,4},{16,8},{20,12},{24,16},{28,20},{32,24... | collective-permute-start | bytes 61448 | tf_op jit(solution)/shard_map/ppermute | solution.py:237
  40.3 2.7 %copy-start.14 = (bf16[80,128]{1,0:T(8,128)(2,1)}, bf16[80,128]{1,0:T(8,128)(2,1)S(1)}, u32[]{:S(2)}) copy-start(bf16[80,128]{1,0:T(8,128)(2,1)S(1)} %collective-permute-done.near0) | copy-start | bytes 61444
  40.3 2.7 %copy-start.15 = (bf16[80,128]{1,0:T(8,128)(2,1)}, bf16[80,128]{1,0:T(8,128)(2,1)S(1)}, u32[]{:S(2)}) copy-start(bf16[80,128]{1,0:T(8,128)(2,1)S(1)} %collective-permute-done.1.near1) | copy-start | bytes 61444
  40.3 2.7 %copy-start.16 = (bf16[80,128]{1,0:T(8,128)(2,1)}, bf16[80,128]{1,0:T(8,128)(2,1)S(1)}, u32[]{:S(2)}) copy-start(bf16[80,128]{1,0:T(8,128)(2,1)S(1)} %collective-permute-done.2.near2) | copy-start | bytes 61444
  40.3 2.7 %copy-start.17 = (bf16[80,128]{1,0:T(8,128)(2,1)}, bf16[80,128]{1,0:T(8,128)(2,1)S(1)}, u32[]{:S(2)}) copy-start(bf16[80,128]{1,0:T(8,128)(2,1)S(1)} %collective-permute-done.3.near3) | copy-start | bytes 61444
  43.0 0.7 copy-start.4
  43.6 7.6 %copy-start.10 = (bf16[512]{0:T(512)(128)(2,1)S(1)}, bf16[512]{0:T(512)(128)(2,1)}, u32[]{:S(2)}) copy-start(bf16[512]{0:T(512)(128)(2,1)} %param.22) | copy-start | bytes 3076
  43.6 8.2 %copy-start.11 = (bf16[512]{0:T(512)(128)(2,1)S(1)}, bf16[512]{0:T(512)(128)(2,1)}, u32[]{:S(2)}) copy-start(bf16[512]{0:T(512)(128)(2,1)} %param.23) | copy-start | bytes 3076
  47.7 12.8 %all-to-all-start.2 = ((bf16[4,512,128]{2,1,0:T(8,128)(2,1)}), bf16[4,512,128]{2,1,0:T(8,128)(2,1)S(1)}, u32[]{:S(2)}, u32[]{:S(2)}) async-start(bf16[4,512,128]{2,1,0:T(8,128)(2,1)} %shard_map.153), calls=%async_computation.2 | async-start | bytes 1048576 | tf_op jit(solution)/shard_map/all_to_all | solution.py:233
  60.5 0.8 copy-start.2
  81.8 26.1 %copy-start.12 = (bf16[512]{0:T(512)(128)(2,1)S(1)}, bf16[512]{0:T(512)(128)(2,1)}, u32[]{:S(2)}) copy-start(bf16[512]{0:T(512)(128)(2,1)} %param.26) | copy-start | bytes 3076
  81.8 26.7 %copy-start.13 = (bf16[512]{0:T(512)(128)(2,1)S(1)}, bf16[512]{0:T(512)(128)(2,1)}, u32[]{:S(2)}) copy-start(bf16[512]{0:T(512)(128)(2,1)} %param.27) | copy-start | bytes 3076
  81.8 19.6 %all-to-all-start.4 = ((bf16[64,16,128]{2,1,0:T(8,128)(2,1)}), bf16[64,16,128]{2,1,0:T(8,128)(2,1)S(1)}, u32[]{:S(2)}, u32[]{:S(2)}) async-start(bf16[64,16,128]{2,1,0:T(8,128)(2,1)} %get-tuple-element.33), calls=%async_computation.4 | async-start | bytes 524288 | tf_op jit(solution)/shard_map/all_to_all | solution.py:233
  88.1 6.8 %collective-permute-start.4 = (bf16[80,128]{1,0:T(8,128)(2,1)}, bf16[80,128]{1,0:T(8,128)(2,1)S(1)}, u32[]{:S(2)}, u32[]{:S(2)}) collective-permute-start(bf16[80,128]{1,0:T(8,128)(2,1)} %get-tuple-element.34), channel_id=1, source_target_pairs={{0,248},{4,252},{8,0},{12,4},{16,8},{20,12},{24,16},{28,20},{32,24... | collective-permute-start | bytes 61448 | tf_op jit(solution)/shard_map/ppermute | solution.py:237
  93.2 3.7 %collective-permute-start.5 = (bf16[80,128]{1,0:T(8,128)(2,1)}, bf16[80,128]{1,0:T(8,128)(2,1)S(1)}, u32[]{:S(2)}, u32[]{:S(2)}) collective-permute-start(bf16[80,128]{1,0:T(8,128)(2,1)} %get-tuple-element.35), channel_id=1, source_target_pairs={{0,252},{4,0},{8,4},{12,8},{16,12},{20,16},{24,20},{28,24},{32,28}... | collective-permute-start | bytes 61448 | tf_op jit(solution)/shard_map/ppermute | solution.py:237
  93.8 3.0 %collective-permute-start.6 = (bf16[80,128]{1,0:T(8,128)(2,1)}, bf16[80,128]{1,0:T(8,128)(2,1)S(1)}, u32[]{:S(2)}, u32[]{:S(2)}) collective-permute-start(bf16[80,128]{1,0:T(8,128)(2,1)} %get-tuple-element.36), channel_id=1, source_target_pairs={{0,4},{4,8},{8,12},{12,16},{16,20},{20,24},{24,28},{28,32},{32,36}... | collective-permute-start | bytes 61448 | tf_op jit(solution)/shard_map/ppermute | solution.py:237
  94.9 6.5 %collective-permute-start.7 = (bf16[80,128]{1,0:T(8,128)(2,1)}, bf16[80,128]{1,0:T(8,128)(2,1)S(1)}, u32[]{:S(2)}, u32[]{:S(2)}) collective-permute-start(bf16[80,128]{1,0:T(8,128)(2,1)} %get-tuple-element.37), channel_id=1, source_target_pairs={{0,8},{4,12},{8,16},{12,20},{16,24},{20,28},{24,32},{28,36},{32,40... | collective-permute-start | bytes 61448 | tf_op jit(solution)/shard_map/ppermute | solution.py:237
  94.9 6.5 %copy-start.6 = (bf16[80,128]{1,0:T(8,128)(2,1)}, bf16[80,128]{1,0:T(8,128)(2,1)S(1)}, u32[]{:S(2)}) copy-start(bf16[80,128]{1,0:T(8,128)(2,1)S(1)} %collective-permute-done.4.near0) | copy-start | bytes 61444
  96.9 4.6 %copy-start.7 = (bf16[80,128]{1,0:T(8,128)(2,1)}, bf16[80,128]{1,0:T(8,128)(2,1)S(1)}, u32[]{:S(2)}) copy-start(bf16[80,128]{1,0:T(8,128)(2,1)S(1)} %collective-permute-done.5.near1) | copy-start | bytes 61444
  96.9 4.6 %copy-start.8 = (bf16[80,128]{1,0:T(8,128)(2,1)}, bf16[80,128]{1,0:T(8,128)(2,1)S(1)}, u32[]{:S(2)}) copy-start(bf16[80,128]{1,0:T(8,128)(2,1)S(1)} %collective-permute-done.6.near2) | copy-start | bytes 61444
  101.4 0.6 copy-start.9
  101.4 0.7 copy-start
  104.6 7.8 %all-to-all-start.5 = ((bf16[4,80,128]{2,1,0:T(8,128)(2,1)}), bf16[4,80,128]{2,1,0:T(8,128)(2,1)S(1)}, u32[]{:S(2)}, u32[]{:S(2)}) async-start(bf16[4,80,128]{2,1,0:T(8,128)(2,1)} %shard_map.156), calls=%async_computation.5 | async-start | bytes 163840 | tf_op jit(solution)/shard_map/all_to_all | solution.py:233
  112.4 0.6 copy-start.3

commit v2 on v1

v2 whole, which is shorter than its diff:
```python
import jax
import jax.numpy as jnp
from jax import lax
from jax.experimental import pallas as pl
from jax.experimental.pallas import tpu as pltpu
from jax.sharding import PartitionSpec as P

D = 512
Q = 128
FEAT = 4
GROUPS = 64
NODES = 320
OWN = 80
SLOT = 96
FAR = 16
NEAR = SLOT - FAR
EDGES = 512
REGION_EDGES = FEAT * EDGES
OFFSETS = (-2, -1, 1, 2)
FAR_ROWS = GROUPS * FAR
NEAR_ROWS = len(OFFSETS) * NEAR
LIST_ROWS = FAR_ROWS + NEAR_ROWS
TABLE_ROWS = NODES + LIST_ROWS
EPSILON = 1e-05
F32 = jnp.float32
BF16 = jnp.bfloat16
I32 = jnp.int32
VMEM = pl.BlockSpec(memory_space=pltpu.VMEM)
SMEM = pl.BlockSpec(memory_space=pltpu.SMEM)
HBM = pl.BlockSpec(memory_space=pltpu.HBM)


def dot(a, b):
    return jnp.dot(a, b, preferred_element_type=F32)


def iota(shape, dim):
    return lax.broadcasted_iota(I32, shape, dim)


def column(row):
    return jnp.transpose(jnp.broadcast_to(row, (Q, Q)))


def widened(tile, width):
    full, rest = divmod(width, Q)
    parts = [tile] * full + ([tile[:, :rest]] if rest else [])
    return jnp.concatenate(parts, axis=1)


def hot(mask):
    return jnp.where(mask, 1.0, 0.0).astype(BF16)


def call(body, outs, specs, scratch=(), flops=10**8, room=8):
    return pl.pallas_call(
        body,
        out_shape=outs,
        in_specs=specs,
        scratch_shapes=list(scratch),
        compiler_params=pltpu.CompilerParams(vmem_limit_bytes=room * 2**20),
        cost_estimate=pl.CostEstimate(flops=flops, bytes_accessed=10**6, transcendentals=0),
    )


def shape(dims, kind):
    return jax.ShapeDtypeStruct(dims, kind)


def peer(p):
    return (lax.axis_index("feat") + p) & (FEAT - 1)


def relative(node):
    owner = lax.shift_right_logical(node * 205, 14)
    return ((owner - lax.axis_index("feat")) & (FEAT - 1)) * OWN + node - owner * OWN


def project_body(nodes, w1, senders, refs, *rest):
    outs, (weights, ids, quarters, sems) = rest[:FEAT], rest[FEAT:]
    loads = [
        pltpu.make_async_copy(
            w1.at[pl.ds(D + k * D, D), :], weights.at[pl.ds(k * D, D), :], sems.at[k]
        )
        for k in range(2)
    ]
    for load in loads:
        load.start()
    rows = nodes[...]
    ids[0:4, :] = senders[...]
    ids[4:8, :] = refs[...]
    both = ids[...]
    planes = jnp.concatenate(
        [lax.shift_right_logical(both, 7).astype(F32), (both & 127).astype(F32)], axis=0
    ).astype(BF16)
    for k in range(2):
        loads[k].wait()
        product = dot(rows, weights[k * D : (k + 1) * D, :]).astype(BF16)
        for q in range(FEAT):
            quarters[q, :, (1 - k) * Q : (2 - k) * Q] = product[:, q * Q : (q + 1) * Q]
    for p, out in enumerate(outs):
        out[0:OWN, :] = quarters[peer(p)]
        out[OWN : OWN + 16, 0:Q] = planes
        out[OWN : OWN + 16, Q : 2 * Q] = jnp.zeros((16, Q), BF16)


def list_rows(lists, select):
    region = lax.axis_index("graph")
    across = iota((FAR, NODES), 1)
    flipped = jnp.transpose(
        jnp.concatenate([relative(lists[...]), jnp.zeros((GROUPS, Q - SLOT), I32)], axis=1)
    )
    for s in range(GROUPS):
        col = jnp.broadcast_to(flipped[0:FAR, s : s + 1], (FAR, NODES))
        select[s * FAR : (s + 1) * FAR, :] = hot(col == across)
    for j, d in enumerate(OFFSETS):
        row = relative(lists[pl.ds((region - d) & (GROUPS - 1), 1), :])
        row = jnp.concatenate([row, jnp.zeros((1, Q - SLOT), I32)], axis=1)
        col = column(row)[FAR:SLOT]
        at = FAR_ROWS + j * NEAR
        select[at : at + NEAR, :] = hot(widened(col, NODES) == iota((NEAR, NODES), 1))


def lists_body(lists, select):
    list_rows(lists, select)


def select_body(tile0, tile1, tile2, tile3, select, far, near0, near1, near2, near3):
    rows = jnp.concatenate(
        [tile[0:OWN, 0:Q] for tile in (tile0, tile1, tile2, tile3)], axis=0
    )
    for b in range(4):
        picked = dot(select[b * 256 : (b + 1) * 256, :], rows).astype(BF16)
        far[b * 16 : (b + 1) * 16] = picked.reshape(16, FAR, Q)
    for j, out in enumerate((near0, near1, near2, near3)):
        at = FAR_ROWS + j * NEAR
        out[...] = dot(select[at : at + NEAR, :], rows).astype(BF16)


def local_body(tile0, tile1, tile2, tile3, rowid, acc):
    region = lax.axis_index("graph")
    tiles = (tile0, tile1, tile2, tile3)
    both = jnp.concatenate(
        [tile[0:OWN, 0:Q] for tile in tiles] + [tile[0:OWN, Q : 2 * Q] for tile in tiles], axis=0
    )
    for p, tile in enumerate(tiles):
        planes = tile[OWN : OWN + 16, 0:Q].astype(F32)
        ids = (planes[0:8] * 128.0 + planes[8:16]).astype(I32)
        near = relative(ids)
        offset = jnp.maximum(ids - NODES, 0)
        source = lax.shift_right_logical(lax.shift_right_logical(offset, 5) * 171, 9)
        slot = offset - source * SLOT
        apart = (source - region) & (GROUPS - 1)
        which = jnp.where(apart >= GROUPS - 2, apart - (GROUPS - 2), apart + 1)
        listed = jnp.where(
            slot < FAR,
            NODES + source * FAR + slot,
            NODES + FAR_ROWS + which * NEAR + slot - FAR,
        )
        ref = jnp.where(ids < NODES, near, listed)
        rowid[p * 4 : (p + 1) * 4, :] = ref[4:8]
        for r in range(4):
            e = (p * 4 + r) * Q
            taken = column(ref[4 + r : 5 + r, :])
            sent = column(near[r : r + 1, :])
            picks = jnp.concatenate(
                [
                    hot(widened(taken, NODES) == iota((Q, NODES), 1)),
                    hot(widened(sent, NODES) == iota((Q, NODES), 1)),
                ],
                axis=1,
            )
            acc[e : e + Q, :] = dot(picks, both)


def gather_body(acc, rowid, far, near0, near1, near2, near3, *outs):
    table = [far[b * 16 : (b + 1) * 16].reshape(256, Q) for b in range(4)]
    table.append(jnp.concatenate([near0[...], near1[...], near2[...], near3[...]], axis=0))
    for p, out in enumerate(outs):
        for half in range(2):
            m = p * 2 + half
            col = jnp.concatenate(
                [column(rowid[2 * m + k : 2 * m + k + 1, :]) for k in range(2)], axis=0
            )
            total = acc[m * 256 : (m + 1) * 256, :]
            for b in range(5):
                width = table[b].shape[0]
                picks = hot(widened(col, width) == iota((256, width), 1) + (NODES + b * 256))
                total += dot(picks, table[b])
            out[half * 256 : (half + 1) * 256, :] = total.astype(BF16)


def wide(quarters):
    return jnp.concatenate([quarters[q : q + 1, :] for q in range(FEAT)], axis=1).astype(F32)


def normed(outputs, gain, shift):
    average = jnp.mean(outputs, axis=-1, keepdims=True)
    centered = outputs - average
    variance = jnp.mean(centered * centered, axis=-1, keepdims=True)
    return centered * lax.rsqrt(variance + EPSILON) * gain + shift


def silu(v):
    half = 0.5 * v
    return half + half * jnp.tanh(half)


def edge_body(count, edges, tile0, tile1, tile2, tile3, w1, w2, gain, shift, *rest):
    outs, (quarters, kept) = rest[:FEAT], rest[FEAT:]
    scale = wide(gain)
    move = wide(shift)
    first = lax.axis_index("feat") * EDGES
    for p, tile in enumerate((tile0, tile1, tile2, tile3)):
        quarters[peer(p)] = tile[...]
    for m in range(2):
        rows = slice(m * 256, (m + 1) * 256)
        feats = edges[rows, :]
        pre = dot(feats, w1[...])
        pre += jnp.concatenate([quarters[q, rows, :] for q in range(FEAT)], axis=1).astype(F32)
        hidden = silu(pre).astype(BF16)
        update = normed(dot(hidden, w2[...]), scale, move)
        live = first + m * 256 + iota((256, D), 0) < count[0]
        result = jnp.where(live, feats.astype(F32) + update, 0.0).astype(BF16)
        for q in range(FEAT):
            kept[q, rows, :] = result[:, q * Q : (q + 1) * Q]
    for p, out in enumerate(outs):
        out[...] = kept[peer(p)]


def finish_body(count, edges, tile0, tile1, tile2, tile3, out, done, kept):
    done[...] = jnp.zeros((8, Q), F32)
    first = lax.axis_index("feat") * EDGES
    for p, tile in enumerate((tile0, tile1, tile2, tile3)):
        kept[peer(p)] = tile[...]
    live = first + iota((EDGES, Q), 0) < count[0]
    for q in range(FEAT):
        cols = slice(q * Q, (q + 1) * Q)
        out[:, cols] = jnp.where(
            live, kept[q].astype(F32), edges[:, cols].astype(F32)
        ).astype(BF16)


BLOCKS = ((0, 320), (320, 256), (576, 256), (832, 256), (1088, 256), (1344, 320))


def block_sum(base, size, rowid, tile, p):
    total = jnp.zeros((size, Q), F32)
    for half in range(2):
        c = p * 4 + half * 2
        ids = jnp.concatenate([rowid[c : c + 1, :], rowid[c + 1 : c + 2, :]], axis=1)
        picks = hot(jnp.broadcast_to(ids, (size, 256)) == iota((size, 256), 0) + base)
        total += dot(picks, tile[half * 256 : (half + 1) * 256, :])
    return total


def first_sums_body(tile0, rowid, acc):
    for base, size in BLOCKS:
        acc[base : base + size, :] = block_sum(base, size, rowid, tile0, 0)


def sums_body(acc, tile1, tile2, tile3, rowid, own, far, near0, near1, near2, near3):
    for base, size in BLOCKS:
        total = acc[base : base + size, :]
        for p, tile in enumerate((tile1, tile2, tile3)):
            total += block_sum(base, size, rowid, tile, p + 1)
        if base == 0:
            own[...] = total
        elif base < NODES + FAR_ROWS:
            at = (base - NODES) // FAR
            far[at : at + 16] = total.astype(BF16).reshape(16, FAR, Q)
        else:
            for j, out in enumerate((near0, near1, near2, near3)):
                out[...] = total[j * NEAR : (j + 1) * NEAR].astype(BF16)


def flip_body(lists, spread, select):
    list_rows(lists, select)
    for at in range(0, LIST_ROWS, Q):
        size = min(Q, LIST_ROWS - at)
        spread[:, at : at + size] = jnp.transpose(select[at : at + size, :].astype(F32)).astype(
            BF16
        )


def spread_body(spread, own, far, near0, near1, near2, near3, after, *outs):
    total = own[...]
    for b in range(4):
        total += dot(
            spread[:, b * 256 : (b + 1) * 256], far[b * 16 : (b + 1) * 16].reshape(256, Q)
        )
    near = jnp.concatenate([near0[...], near1[...], near2[...], near3[...]], axis=0)
    total += dot(spread[:, FAR_ROWS:LIST_ROWS], near)
    total = total.astype(BF16)
    for p, out in enumerate(outs):
        out[...] = total[p * OWN : (p + 1) * OWN]


def node_body(nodes, tile0, tile1, tile2, tile3, w1, w2, gain, shift, out, quarters):
    feats = nodes[...]
    for p, tile in enumerate((tile0, tile1, tile2, tile3)):
        quarters[peer(p)] = tile[...]
    pre = dot(feats, w1[0:D, :])
    pre += dot(jnp.concatenate([quarters[q] for q in range(FEAT)], axis=1), w1[D : 2 * D, :])
    hidden = silu(pre).astype(BF16)
    update = normed(dot(hidden, w2[...]), wide(gain), wide(shift))
    out[...] = (feats.astype(F32) + update).astype(BF16)


def exchanged(tiles):
    arrived = [
        lax.ppermute(tiles[j], "feat", [(i, (i + j) % FEAT) for i in range(FEAT)])
        for j in (2, 1, 3)
    ]
    return tiles[0], arrived[2], arrived[0], arrived[1]


def swapped(value):
    return lax.all_to_all(value, "graph", split_axis=0, concat_axis=0, tiled=True)


def moved(value, by):
    return lax.ppermute(value, "graph", [(i, (i + by) % GROUPS) for i in range(GROUPS)])


def per_device(
    node_feats,
    edge_feats,
    senders,
    receiver_ref,
    send_list,
    edge_count,
    edge_w1,
    edge_w2,
    edge_gain,
    edge_shift,
    node_w1,
    node_w2,
    node_gain,
    node_shift,
):
    tiles = call(
        project_body,
        [shape((96, 256), BF16)] * FEAT,
        [VMEM, HBM, VMEM, VMEM],
        [
            pltpu.VMEM((2 * D, D), BF16),
            pltpu.VMEM((8, Q), I32),
            pltpu.VMEM((FEAT, OWN, 2 * Q), BF16),
            pltpu.SemaphoreType.DMA((2,)),
        ],
    )(node_feats, pltpu.with_memory_space_constraint(edge_w1, pltpu.HBM), senders.reshape(4, Q), receiver_ref.reshape(4, Q))
    tiles = exchanged(tiles)
    select = call(lists_body, shape((LIST_ROWS, NODES), BF16), [VMEM])(send_list[0])

    near_shape = [shape((NEAR, Q), BF16)] * 4
    far_shape = shape((GROUPS, FAR, Q), BF16)
    far, *near = call(select_body, (far_shape, *near_shape), [VMEM] * 5)(*tiles, select)
    far = swapped(far)
    near = [moved(value, -d) for value, d in zip(near, OFFSETS)]

    rowid, acc = call(
        local_body,
        (
            shape((16, Q), I32),
            shape((REGION_EDGES, Q), F32),
        ),
        [VMEM] * 4,
        flops=10**9,
    )(*tiles)
    quarter = [shape((EDGES, Q), BF16)] * FEAT
    picked = call(gather_body, quarter, [VMEM] * 7, flops=10**9)(acc, rowid, far, *near)
    picked = exchanged(picked)

    messages = call(
        edge_body,
        quarter,
        [SMEM] + [VMEM] * 9,
        [pltpu.VMEM((FEAT, EDGES, Q), BF16)] * 2,
        flops=10**9,
    )(
        edge_count,
        edge_feats,
        *picked,
        edge_w1[0:D],
        edge_w2,
        edge_gain.reshape(4, Q),
        edge_shift.reshape(4, Q),
    )
    arrived = exchanged(messages)
    partial = call(first_sums_body, shape((TABLE_ROWS, Q), F32), [VMEM] * 2, flops=10**8)(
        messages[0], rowid
    )
    own, far, *near = call(
        sums_body,
        (shape((NODES, Q), F32), far_shape, *near_shape),
        [VMEM] * 5,
        flops=10**9,
    )(partial, *arrived[1:], rowid)
    far = swapped(far)
    near = [moved(value, d) for value, d in zip(near, OFFSETS)]
    new_edges, done = call(
        finish_body,
        (shape((EDGES, D), BF16), shape((8, Q), F32)),
        [SMEM] + [VMEM] * 5,
        [pltpu.VMEM((FEAT, EDGES, Q), BF16)],
    )(edge_count, edge_feats, *messages)
    spread = call(
        flip_body,
        shape((NODES, LIST_ROWS), BF16),
        [VMEM],
        [pltpu.VMEM((LIST_ROWS, NODES), BF16)],
    )(send_list[0])
    sums = call(spread_body, [shape((OWN, Q), BF16)] * FEAT, [VMEM] * 8)(
        spread, own, far, *near, done
    )
    sums = exchanged(sums)
    new_nodes = call(
        node_body,
        shape((OWN, D), BF16),
        [VMEM] * 9,
        [pltpu.VMEM((FEAT, OWN, Q), BF16)],
    )(
        node_feats,
        *sums,
        node_w1,
        node_w2,
        node_gain.reshape(4, Q),
        node_shift.reshape(4, Q),
    )
    return (new_edges, new_nodes)


def solution(mesh):
    split = P(("graph", "feat"))
    return jax.shard_map(
        per_device,
        mesh=mesh,
        in_specs=(split, split, split, split, P("graph"), P("graph")) + (P(),) * 8,
        out_specs=(split, split),
        check_vma=False,
    )
```

time: 117 us -> 95.7 us (0.82)
  Pallas kernels: 27.9 us -> 14.1 us
  blocking collectives: 12.6 us -> 0 us
  waiting for transfers between devices: 21.4 us -> 25.8 us
  local copies, waits for them, and re-layouts: 7.2 us -> 10.3 us
  starting transfers between devices: 45.2 us -> 43.4 us
    ppermute x0 -> x12, waiting for transfers between devices: none -> 19.7 us  [exchanged(): lax.ppermute(tiles[j], 'feat', [(i, (i + j) % FEAT) for i in range(FEAT)])]
    pallas_call x9 -> x12, Pallas kernels: 27.9 us -> 14.1 us  [the longest x1 2.22 us: per_device(): call(sums_body, (shape((NODES, Q), F32), far_shape, *near_shape), [VMEM]...]
    all_to_all x1 -> x0, blocking collectives: 12.6 us -> none  [swapped(): return lax.all_to_all(value, axis, split_axis=0, concat_axis=0, tiled=True)]
    all_to_all x5 -> x2, starting transfers between devices: 31.6 us -> 19.2 us  [swapped(): lax.all_to_all(value, 'graph', split_axis=0, concat_axis=0, tiled=True)]
    all_to_all x5 -> x2, waiting for transfers between devices: 14.9 us -> 3.18 us  [swapped(): lax.all_to_all(value, 'graph', split_axis=0, concat_axis=0, tiled=True)]
    ppermute x0 -> x12, starting transfers between devices: none -> 10.5 us  [exchanged(): lax.ppermute(tiles[j], 'feat', [(i, (i + j) % FEAT) for i in range(FEAT)])]
    unnamed x36 -> x50, local copies, waits for them, and re-layouts: 3.47 us -> 9.23 us
    ppermute x8, waiting for transfers between devices: 6.51 us -> 2.95 us  [moved(): lax.ppermute(value, 'graph', [(i, (i + by) % GROUPS) for i in range(GROUP...]
  transfers between devices with their start and end apart: 13 -> 22, of which waited for: 6 -> 14; matrix products, arithmetic and copies ran while one was open for 3% -> 1% of each run, Pallas kernels for 5% -> 5%
where the time goes in v2:
time: 95.7 us; the launch traced here: 95.2 us
  starting transfers between devices  43.4 us (45%)
  waiting for transfers between devices  25.8 us (27%)
  Pallas kernels  14.1 us (15%)
  local copies, waits for them, and re-layouts  10.3 us (11%)
  between operations  1.52 us (2%)
    ppermute x12, waiting for transfers between devices, exchanged(): lax.ppermute(tiles[j], 'feat', [(i, (i + j) % FEAT) for i in range(FEAT)])  19.7 us
    all_to_all x2, starting transfers between devices, swapped(): lax.all_to_all(value, 'graph', split_axis=0, concat_axis=0, tiled=True)  19.2 us
    ppermute x8, starting transfers between devices, moved(): lax.ppermute(value, 'graph', [(i, (i + by) % GROUPS) for i in range(GROUP...  13.7 us
    ppermute x12, starting transfers between devices, exchanged(): lax.ppermute(tiles[j], 'feat', [(i, (i + j) % FEAT) for i in range(FEAT)])  10.5 us
    unnamed x50, local copies, waits for them, and re-layouts  9.23 us
    all_to_all x2, waiting for transfers between devices, swapped(): lax.all_to_all(value, 'graph', split_axis=0, concat_axis=0, tiled=True)  3.18 us
    ppermute x8, waiting for transfers between devices, moved(): lax.ppermute(value, 'graph', [(i, (i + by) % GROUPS) for i in range(GROUP...  2.95 us
    pallas_call x1, Pallas kernels, per_device(): call(sums_body, (shape((NODES, Q), F32), far_shape, *near_shape), [VMEM]...  2.22 us
  transfers between devices with their start and end apart: 22, of which 14 were waited for; matrix products, arithmetic and copies ran while one was open for 1% of the time, Pallas kernels for 5%

profile of v2, /device:TPU:1, one launch (start us, length us, event | category | flops | bytes accessed | tf_op | source)
XLA Modules:
  0.0 95.2 jit_solution(520319557916130422)
XLA Ops:
  0.6 0.0 copy-start.3
  0.6 0.9 copy-done.3
  1.5 0.7 copy-done.18
  2.2 0.7 copy-done.19
  2.9 1.5 %shard_map.149 = (bf16[96,256]{1,0:T(8,128)(2,1)S(1)}, bf16[96,256]{1,0:T(8,128)(2,1)S(1)}, bf16[96,256]{1,0:T(8,128)(2,1)S(1)}, bf16[96,256]{1,0:T(8,128)(2,1)S(1)}) custom-call(bf16[80,512]{1,0:T(8,128)(2,1)S(1)} %copy-done.3, bf16[1536,512]{1,0:T(8,128)(2,1)} %w1.2, s32[4,128]{1,0:T(4,128)S(1)} %bitcast.9, s32[4,128]{1,0:T(4,128)S(1)} %bitcast.10), custom_call_target="tpu_custom_call" | custom-call | flops 100000000 | bytes 1000000 | tf_op jit(solution)/shard_map/pallas_call | solution.py:342
  4.4 3.4 %collective-permute-start = (bf16[96,256]{1,0:T(8,128)(2,1)S(1)}, bf16[96,256]{1,0:T(8,128)(2,1)S(1)}, u32[]{:S(2)}, u32[]{:S(2)}) collective-permute-start(bf16[96,256]{1,0:T(8,128)(2,1)S(1)} %get-tuple-element.34), channel_id=1, source_target_pairs={{0,3},{1,0},{2,1},{3,2},{4,7},{5,4},{6,5},{7,6},{8,11},{9,8},{10,9... | collective-permute-start | bytes 147464 | tf_op jit(solution)/shard_map/ppermute | solution.py:312
  7.8 0.5 collective-permute-start.1
  8.3 0.6 collective-permute-start.2
  8.9 0.5 shard_map.151.select
  9.4 2.9 %collective-permute-done.1.tile2 = bf16[96,256]{1,0:T(8,128)(2,1)S(1)} collective-permute-done((bf16[96,256]{1,0:T(8,128)(2,1)S(1)}, bf16[96,256]{1,0:T(8,128)(2,1)S(1)}, u32[]{:S(2)}, u32[]{:S(2)}) %collective-permute-start.1) | collective-permute-done | bytes 49184 | tf_op jit(solution)/shard_map/ppermute | solution.py:312
  12.3 0.5 collective-permute-done.2.tile3
  12.8 1.1 %shard_map.152 = (bf16[64,16,128]{2,1,0:T(8,128)(2,1)}, bf16[80,128]{1,0:T(8,128)(2,1)S(1)}, bf16[80,128]{1,0:T(8,128)(2,1)S(1)}, bf16[80,128]{1,0:T(8,128)(2,1)S(1)}, bf16[80,128]{1,0:T(8,128)(2,1)S(1)}) custom-call(bf16[96,256]{1,0:T(8,128)(2,1)S(1)} %get-tuple-element.33.tile0, bf16[96,256]{1,0:T(8,128)(2,1)S(1)} %collective-permute-done.tile1, ...), custom_call_target="tpu_custom_call" | custom-call | flops 100000000 | bytes 1000000 | tf_op jit(solution)/shard_map/pallas_call | solution.py:358
  13.8 13.8 %all-to-all-start = ((bf16[64,16,128]{2,1,0:T(8,128)(2,1)}), bf16[64,16,128]{2,1,0:T(8,128)(2,1)S(1)}, u32[]{:S(2)}, u32[]{:S(2)}) async-start(bf16[64,16,128]{2,1,0:T(8,128)(2,1)} %get-tuple-element.39), calls=%async_computation | async-start | bytes 524288 | tf_op jit(solution)/shard_map/all_to_all | solution.py:319
  27.6 1.4 %collective-permute-start.3 = (bf16[80,128]{1,0:T(8,128)(2,1)S(1)}, bf16[80,128]{1,0:T(8,128)(2,1)S(1)}, u32[]{:S(2)}, u32[]{:S(2)}) collective-permute-start(bf16[80,128]{1,0:T(8,128)(2,1)S(1)} %get-tuple-element.40), channel_id=1, source_target_pairs={{0,8},{4,12},{8,16},{12,20},{16,24},{20,28},{24,32},{28,36},{32,40... | collective-permute-start | bytes 61448 | tf_op jit(solution)/shard_map/ppermute | solution.py:323
  29.0 1.7 %collective-permute-start.4 = (bf16[80,128]{1,0:T(8,128)(2,1)S(1)}, bf16[80,128]{1,0:T(8,128)(2,1)S(1)}, u32[]{:S(2)}, u32[]{:S(2)}) collective-permute-start(bf16[80,128]{1,0:T(8,128)(2,1)S(1)} %get-tuple-element.41), channel_id=1, source_target_pairs={{0,4},{4,8},{8,12},{12,16},{16,20},{20,24},{24,28},{28,32},{32,36}... | collective-permute-start | bytes 61448 | tf_op jit(solution)/shard_map/ppermute | solution.py:323
  30.8 3.6 %collective-permute-start.6 = (bf16[80,128]{1,0:T(8,128)(2,1)S(1)}, bf16[80,128]{1,0:T(8,128)(2,1)S(1)}, u32[]{:S(2)}, u32[]{:S(2)}) collective-permute-start(bf16[80,128]{1,0:T(8,128)(2,1)S(1)} %get-tuple-element.43), channel_id=1, source_target_pairs={{0,248},{4,252},{8,0},{12,4},{16,8},{20,12},{24,16},{28,20},{32,24... | collective-permute-start | bytes 61448 | tf_op jit(solution)/shard_map/ppermute | solution.py:323
  34.4 1.5 %shard_map.150 = (s32[16,128]{1,0:T(8,128)S(1)}, f32[2048,128]{1,0:T(8,128)S(1)}) custom-call(bf16[96,256]{1,0:T(8,128)(2,1)S(1)} %get-tuple-element.33.tile0, bf16[96,256]{1,0:T(8,128)(2,1)S(1)} %collective-permute-done.tile1, bf16[96,256]{1,0:T(8,128)(2,1)S(1)} %collective-permute-done.1.tile2, bf16[96,256]{1,0:T(8,128)(2,1)S(1)} %collective-permute-done.2.tile3), custom_call_target="tpu_custom_call" | custom-call | flops 1000000000 | bytes 1000000 | tf_op jit(solution)/shard_map/pallas_call | solution.py:362
  35.9 1.6 %collective-permute-done.3.near0 = bf16[80,128]{1,0:T(8,128)(2,1)S(1)} collective-permute-done((bf16[80,128]{1,0:T(8,128)(2,1)S(1)}, bf16[80,128]{1,0:T(8,128)(2,1)S(1)}, u32[]{:S(2)}, u32[]{:S(2)}) %collective-permute-start.3) | collective-permute-done | bytes 20512 | tf_op jit(solution)/shard_map/ppermute | solution.py:323
  37.5 3.2 %all-to-all-done.far = bf16[64,16,128]{2,1,0:T(8,128)(2,1)S(1)} async-done(((bf16[64,16,128]{2,1,0:T(8,128)(2,1)}), bf16[64,16,128]{2,1,0:T(8,128)(2,1)S(1)}, u32[]{:S(2)}, u32[]{:S(2)}) %all-to-all-start) | async-done | bytes 262176 | tf_op jit(solution)/shard_map/all_to_all | solution.py:319
  40.7 1.7 %shard_map.153 = (bf16[512,128]{1,0:T(8,128)(2,1)S(1)}, bf16[512,128]{1,0:T(8,128)(2,1)S(1)}, bf16[512,128]{1,0:T(8,128)(2,1)S(1)}, bf16[512,128]{1,0:T(8,128)(2,1)S(1)}) custom-call(f32[2048,128]{1,0:T(8,128)S(1)} %get-tuple-element.37.acc, s32[16,128]{1,0:T(8,128)S(1)} %get-tuple-element.38.rowid, bf16[64,16,128]{2,1,0:T(8,128)(2,1)S(1)} %all-to-all-done.far, ...), custom_call_target="tpu_custom_call" | custom-call | flops 1000000000 | bytes 1000000 | tf_op jit(solution)/shard_map/pallas_call | solution.py:372
  42.4 0.4 collective-permute-start.7
  42.8 1.0 %collective-permute-start.8 = (bf16[512,128]{1,0:T(8,128)(2,1)S(1)}, bf16[512,128]{1,0:T(8,128)(2,1)S(1)}, u32[]{:S(2)}, u32[]{:S(2)}) collective-permute-start(bf16[512,128]{1,0:T(8,128)(2,1)S(1)} %get-tuple-element.46), channel_id=1, source_target_pairs={{0,2},{1,3},{2,0},{3,1},{4,6},{5,7},{6,4},{7,5},{8,10},{9,11},{10,... | collective-permute-start | bytes 393224 | tf_op jit(solution)/shard_map/ppermute | solution.py:312
  43.8 0.8 collective-permute-start.9
  44.6 1.1 %slice.3.w1 = bf16[512,512]{1,0:T(8,128)(2,1)S(1)} slice(bf16[1536,512]{1,0:T(8,128)(2,1)} %w1.2), slice={[0:512], [0:512]} | slice | bytes 1048576 | tf_op jit(solution)/shard_map/slice | solution.py:385
  46.3 1.0 %collective-permute-done.7.tile1 = bf16[512,128]{1,0:T(8,128)(2,1)S(1)} collective-permute-done((bf16[512,128]{1,0:T(8,128)(2,1)S(1)}, bf16[512,128]{1,0:T(8,128)(2,1)S(1)}, u32[]{:S(2)}, u32[]{:S(2)}) %collective-permute-start.7) | collective-permute-done | bytes 131104 | tf_op jit(solution)/shard_map/ppermute | solution.py:312
  47.3 1.5 %collective-permute-done.8.tile2 = bf16[512,128]{1,0:T(8,128)(2,1)S(1)} collective-permute-done((bf16[512,128]{1,0:T(8,128)(2,1)S(1)}, bf16[512,128]{1,0:T(8,128)(2,1)S(1)}, u32[]{:S(2)}, u32[]{:S(2)}) %collective-permute-start.8) | collective-permute-done | bytes 131104 | tf_op jit(solution)/shard_map/ppermute | solution.py:312
  48.8 3.7 %collective-permute-done.9.tile3 = bf16[512,128]{1,0:T(8,128)(2,1)S(1)} collective-permute-done((bf16[512,128]{1,0:T(8,128)(2,1)S(1)}, bf16[512,128]{1,0:T(8,128)(2,1)S(1)}, u32[]{:S(2)}, u32[]{:S(2)}) %collective-permute-start.9) | collective-permute-done | bytes 131104 | tf_op jit(solution)/shard_map/ppermute | solution.py:312
  52.5 1.4 %shard_map.154 = (bf16[512,128]{1,0:T(8,128)(2,1)S(1)}, bf16[512,128]{1,0:T(8,128)(2,1)S(1)}, bf16[512,128]{1,0:T(8,128)(2,1)S(1)}, bf16[512,128]{1,0:T(8,128)(2,1)S(1)}) custom-call(s32[1]{0:T(128)S(6)} %copy.16.count, bf16[512,512]{1,0:T(8,128)(2,1)S(1)} %copy-done.1, bf16[512,128]{1,0:T(8,128)(2,1)S(1)} %get-tuple-element.44.tile0, ...), custom_call_target="tpu_custom_call" | custom-call | flops 1000000000 | bytes 1000000 | tf_op jit(solution)/shard_map/pallas_call | solution.py:375
  54.0 0.0 copy-start.8
  54.0 0.1 collective-permute-start.10
  54.1 1.1 %collective-permute-start.11 = (bf16[512,128]{1,0:T(8,128)(2,1)S(1)}, bf16[512,128]{1,0:T(8,128)(2,1)S(1)}, u32[]{:S(2)}, u32[]{:S(2)}) collective-permute-start(bf16[512,128]{1,0:T(8,128)(2,1)S(1)} %get-tuple-element.50.tile2), channel_id=1, source_target_pairs={{0,2},{1,3},{2,0},{3,1},{4,6},{5,7},{6,4},{7,5},{8,10},{9,11},{10,... | collective-permute-start | bytes 393224 | tf_op jit(solution)/shard_map/ppermute | solution.py:312
  55.2 0.8 collective-permute-start.12
  56.0 0.6 shard_map.157.acc
  56.6 2.1 %collective-permute-done.10.tile1 = bf16[512,128]{1,0:T(8,128)(2,1)S(1)} collective-permute-done((bf16[512,128]{1,0:T(8,128)(2,1)S(1)}, bf16[512,128]{1,0:T(8,128)(2,1)S(1)}, u32[]{:S(2)}, u32[]{:S(2)}) %collective-permute-start.10) | collective-permute-done | bytes 131104 | tf_op jit(solution)/shard_map/ppermute | solution.py:312
  58.6 0.9 collective-permute-done.11.tile2
  59.6 3.9 %collective-permute-done.12.tile3 = bf16[512,128]{1,0:T(8,128)(2,1)S(1)} collective-permute-done((bf16[512,128]{1,0:T(8,128)(2,1)S(1)}, bf16[512,128]{1,0:T(8,128)(2,1)S(1)}, u32[]{:S(2)}, u32[]{:S(2)}) %collective-permute-start.12) | collective-permute-done | bytes 131104 | tf_op jit(solution)/shard_map/ppermute | solution.py:312
  63.4 2.2 %shard_map.158 = (f32[320,128]{1,0:T(8,128)S(1)}, bf16[64,16,128]{2,1,0:T(8,128)(2,1)}, bf16[80,128]{1,0:T(8,128)(2,1)}, bf16[80,128]{1,0:T(8,128)(2,1)}, bf16[8...) custom-call(f32[1664,128]{1,0:T(8,128)S(1)} %shard_map.157.acc, bf16[512,128]{1,0:T(8,128)(2,1)S(1)} %collective-permute-done.10.tile1, ...), custom_call_target="tpu_custom_call" | custom-call | flops 1000000000 | bytes 1000000 | tf_op jit(solution)/shard_map/pallas_call | solution.py:394
  65.7 0.7 copy-done.5
  66.3 5.5 %all-to-all-start.1 = ((bf16[64,16,128]{2,1,0:T(8,128)(2,1)}), bf16[64,16,128]{2,1,0:T(8,128)(2,1)S(1)}, u32[]{:S(2)}, u32[]{:S(2)}) async-start(bf16[64,16,128]{2,1,0:T(8,128)(2,1)} %get-tuple-element.54), calls=%async_computation.1 | async-start | bytes 524288 | tf_op jit(solution)/shard_map/all_to_all | solution.py:319
  71.8 5.1 %collective-permute-start.13 = (bf16[80,128]{1,0:T(8,128)(2,1)}, bf16[80,128]{1,0:T(8,128)(2,1)S(1)}, u32[]{:S(2)}, u32[]{:S(2)}) collective-permute-start(bf16[80,128]{1,0:T(8,128)(2,1)} %get-tuple-element.55), channel_id=1, source_target_pairs={{0,248},{4,252},{8,0},{12,4},{16,8},{20,12},{24,16},{28,20},{32,24... | collective-permute-start | bytes 61448 | tf_op jit(solution)/shard_map/ppermute | solution.py:323
  76.9 0.7 collective-permute-start.14
  77.5 1.1 %collective-permute-start.15 = (bf16[80,128]{1,0:T(8,128)(2,1)}, bf16[80,128]{1,0:T(8,128)(2,1)S(1)}, u32[]{:S(2)}, u32[]{:S(2)}) collective-permute-start(bf16[80,128]{1,0:T(8,128)(2,1)} %get-tuple-element.57), channel_id=1, source_target_pairs={{0,4},{4,8},{8,12},{12,16},{16,20},{20,24},{24,28},{28,32},{32,36}... | collective-permute-start | bytes 61448 | tf_op jit(solution)/shard_map/ppermute | solution.py:323
  78.6 0.1 collective-permute-start.16
  78.7 0.7 shard_map.156.spread
  79.5 0.0 copy-start.9
  79.5 0.9 copy-done.9
  80.4 0.9 copy-done.11
  81.3 0.9 copy-done.13
  82.2 1.1 %shard_map.155 = (bf16[512,512]{1,0:T(8,128)(2,1)}, f32[8,128]{1,0:T(8,128)S(1)}) custom-call(s32[1]{0:T(128)S(6)} %copy.16.count, bf16[512,512]{1,0:T(8,128)(2,1)S(1)} %copy-done.1, bf16[512,128]{1,0:T(8,128)(2,1)S(1)} %get-tuple-element.48.tile0, bf16[512,128]{1,0:T(8,128)(2,1)S(1)} %copy-done.9, bf16[512,128]{1,0:T(8,128)(2,1)S(1)} %copy-done.11, ...), custom_call_target="tpu_custom_call" | custom-call | flops 100000000 | bytes 1000000 | tf_op jit(solution)/shard_map/pallas_call | solution.py:402
  83.3 0.0 copy-start.14
  83.3 0.6 copy-done.14
  83.9 1.3 %collective-permute-done.16.near3 = bf16[80,128]{1,0:T(8,128)(2,1)S(1)} collective-permute-done((bf16[80,128]{1,0:T(8,128)(2,1)}, bf16[80,128]{1,0:T(8,128)(2,1)S(1)}, u32[]{:S(2)}, u32[]{:S(2)}) %collective-permute-start.16) | collective-permute-done | bytes 20512 | tf_op jit(solution)/shard_map/ppermute | solution.py:323
  85.2 0.6 copy-done.16
  85.8 0.9 copy-done.6
  86.8 0.7 copy-done.15
  87.5 0.7 copy-done.17
  88.2 0.4 shard_map.159
  88.6 0.7 collective-permute-start.17
  89.4 0.6 collective-permute-start.18
  90.0 0.6 collective-permute-start.19
  90.6 0.8 collective-permute-done.17.tile1
  91.3 2.2 %collective-permute-done.18.tile2 = bf16[80,128]{1,0:T(8,128)(2,1)S(1)} collective-permute-done((bf16[80,128]{1,0:T(8,128)(2,1)S(1)}, bf16[80,128]{1,0:T(8,128)(2,1)S(1)}, u32[]{:S(2)}, u32[]{:S(2)}) %collective-permute-start.18) | collective-permute-done | bytes 20512 | tf_op jit(solution)/shard_map/ppermute | solution.py:312
  93.5 0.3 collective-permute-done.19.tile3
  93.9 1.3 %shard_map.160 = bf16[80,512]{1,0:T(8,128)(2,1)} custom-call(bf16[80,512]{1,0:T(8,128)(2,1)S(1)} %copy-done.4, bf16[80,128]{1,0:T(8,128)(2,1)S(1)} %get-tuple-element.60.tile0, bf16[80,128]{1,0:T(8,128)(2,1)S(1)} %collective-permute-done.17.tile1, bf16[80,128]{1,0:T(8,128)(2,1)S(1)} %collective-permute-done.18.tile2, ...), custom_call_target="tpu_custom_call" | custom-call | flops 100000000 | bytes 1000000 | tf_op jit(solution)/shard_map/pallas_call | solution.py:418
  (43 shorter events, 0.1 us)
Async XLA Ops:
  0.6 0.9 copy-start.3
  1.5 0.7 copy-start.18
  2.2 0.7 copy-start.19
  2.9 6.0 %copy-start.7 = (s32[1,64,96]{2,1,0:T(8,128)S(1)}, s32[1,64,96]{2,1,0:T(8,128)}, u32[]{:S(2)}) copy-start(s32[1,64,96]{2,1,0:T(8,128)} %param.18) | copy-start | bytes 73732
  4.4 5.0 %collective-permute-start = (bf16[96,256]{1,0:T(8,128)(2,1)S(1)}, bf16[96,256]{1,0:T(8,128)(2,1)S(1)}, u32[]{:S(2)}, u32[]{:S(2)}) collective-permute-start(bf16[96,256]{1,0:T(8,128)(2,1)S(1)} %get-tuple-element.34), channel_id=1, source_target_pairs={{0,3},{1,0},{2,1},{3,2},{4,7},{5,4},{6,5},{7,6},{8,11},{9,8},{10,9... | collective-permute-start | bytes 147464 | tf_op jit(solution)/shard_map/ppermute | solution.py:312
  7.8 4.5 %collective-permute-start.1 = (bf16[96,256]{1,0:T(8,128)(2,1)S(1)}, bf16[96,256]{1,0:T(8,128)(2,1)S(1)}, u32[]{:S(2)}, u32[]{:S(2)}) collective-permute-start(bf16[96,256]{1,0:T(8,128)(2,1)S(1)} %get-tuple-element.35), channel_id=1, source_target_pairs={{0,2},{1,3},{2,0},{3,1},{4,6},{5,7},{6,4},{7,5},{8,10},{9,11},{10,... | collective-permute-start | bytes 147464 | tf_op jit(solution)/shard_map/ppermute | solution.py:312
  8.3 4.5 %collective-permute-start.2 = (bf16[96,256]{1,0:T(8,128)(2,1)S(1)}, bf16[96,256]{1,0:T(8,128)(2,1)S(1)}, u32[]{:S(2)}, u32[]{:S(2)}) collective-permute-start(bf16[96,256]{1,0:T(8,128)(2,1)S(1)} %get-tuple-element.36), channel_id=1, source_target_pairs={{0,1},{1,2},{2,3},{3,0},{4,5},{5,6},{6,7},{7,4},{8,9},{9,10},{10,1... | collective-permute-start | bytes 147464 | tf_op jit(solution)/shard_map/ppermute | solution.py:312
  13.8 26.8 %all-to-all-start = ((bf16[64,16,128]{2,1,0:T(8,128)(2,1)}), bf16[64,16,128]{2,1,0:T(8,128)(2,1)S(1)}, u32[]{:S(2)}, u32[]{:S(2)}) async-start(bf16[64,16,128]{2,1,0:T(8,128)(2,1)} %get-tuple-element.39), calls=%async_computation | async-start | bytes 524288 | tf_op jit(solution)/shard_map/all_to_all | solution.py:319
  27.6 9.9 %collective-permute-start.3 = (bf16[80,128]{1,0:T(8,128)(2,1)S(1)}, bf16[80,128]{1,0:T(8,128)(2,1)S(1)}, u32[]{:S(2)}, u32[]{:S(2)}) collective-permute-start(bf16[80,128]{1,0:T(8,128)(2,1)S(1)} %get-tuple-element.40), channel_id=1, source_target_pairs={{0,8},{4,12},{8,16},{12,20},{16,24},{20,28},{24,32},{28,36},{32,40... | collective-permute-start | bytes 61448 | tf_op jit(solution)/shard_map/ppermute | solution.py:323
  29.0 8.5 %collective-permute-start.4 = (bf16[80,128]{1,0:T(8,128)(2,1)S(1)}, bf16[80,128]{1,0:T(8,128)(2,1)S(1)}, u32[]{:S(2)}, u32[]{:S(2)}) collective-permute-start(bf16[80,128]{1,0:T(8,128)(2,1)S(1)} %get-tuple-element.41), channel_id=1, source_target_pairs={{0,4},{4,8},{8,12},{12,16},{16,20},{20,24},{24,28},{28,32},{32,36}... | collective-permute-start | bytes 61448 | tf_op jit(solution)/shard_map/ppermute | solution.py:323
  30.8 6.7 %collective-permute-start.5 = (bf16[80,128]{1,0:T(8,128)(2,1)S(1)}, bf16[80,128]{1,0:T(8,128)(2,1)S(1)}, u32[]{:S(2)}, u32[]{:S(2)}) collective-permute-start(bf16[80,128]{1,0:T(8,128)(2,1)S(1)} %get-tuple-element.42), channel_id=1, source_target_pairs={{0,252},{4,0},{8,4},{12,8},{16,12},{20,16},{24,20},{28,24},{32,28}... | collective-permute-start | bytes 61448 | tf_op jit(solution)/shard_map/ppermute | solution.py:323
  30.8 6.7 %collective-permute-start.6 = (bf16[80,128]{1,0:T(8,128)(2,1)S(1)}, bf16[80,128]{1,0:T(8,128)(2,1)S(1)}, u32[]{:S(2)}, u32[]{:S(2)}) collective-permute-start(bf16[80,128]{1,0:T(8,128)(2,1)S(1)} %get-tuple-element.43), channel_id=1, source_target_pairs={{0,248},{4,252},{8,0},{12,4},{16,8},{20,12},{24,16},{28,20},{32,24... | collective-permute-start | bytes 61448 | tf_op jit(solution)/shard_map/ppermute | solution.py:323
  40.7 11.8 %copy-start.1 = (bf16[512,512]{1,0:T(8,128)(2,1)S(1)}, bf16[512,512]{1,0:T(8,128)(2,1)}, u32[]{:S(2)}) copy-start(bf16[512,512]{1,0:T(8,128)(2,1)} %edges.3) | copy-start | bytes 1572868
  40.7 11.8 %copy-start.22 = (bf16[512,512]{1,0:T(8,128)(2,1)S(1)}, bf16[512,512]{1,0:T(8,128)(2,1)}, u32[]{:S(2)}) copy-start(bf16[512,512]{1,0:T(8,128)(2,1)} %w2.2) | copy-start | bytes 1572868
  40.7 11.8 %copy-start.23 = (bf16[512]{0:T(512)(128)(2,1)S(1)}, bf16[512]{0:T(512)(128)(2,1)}, u32[]{:S(2)}) copy-start(bf16[512]{0:T(512)(128)(2,1)} %param.22) | copy-start | bytes 3076
  40.7 11.8 %copy-start.24 = (bf16[512]{0:T(512)(128)(2,1)S(1)}, bf16[512]{0:T(512)(128)(2,1)}, u32[]{:S(2)}) copy-start(bf16[512]{0:T(512)(128)(2,1)} %param.23) | copy-start | bytes 3076
  42.4 4.9 %collective-permute-start.7 = (bf16[512,128]{1,0:T(8,128)(2,1)S(1)}, bf16[512,128]{1,0:T(8,128)(2,1)S(1)}, u32[]{:S(2)}, u32[]{:S(2)}) collective-permute-start(bf16[512,128]{1,0:T(8,128)(2,1)S(1)} %get-tuple-element.45), channel_id=1, source_target_pairs={{0,3},{1,0},{2,1},{3,2},{4,7},{5,4},{6,5},{7,6},{8,11},{9,8},{10,9... | collective-permute-start | bytes 393224 | tf_op jit(solution)/shard_map/ppermute | solution.py:312
  42.8 6.0 %collective-permute-start.8 = (bf16[512,128]{1,0:T(8,128)(2,1)S(1)}, bf16[512,128]{1,0:T(8,128)(2,1)S(1)}, u32[]{:S(2)}, u32[]{:S(2)}) collective-permute-start(bf16[512,128]{1,0:T(8,128)(2,1)S(1)} %get-tuple-element.46), channel_id=1, source_target_pairs={{0,2},{1,3},{2,0},{3,1},{4,6},{5,7},{6,4},{7,5},{8,10},{9,11},{10,... | collective-permute-start | bytes 393224 | tf_op jit(solution)/shard_map/ppermute | solution.py:312
  43.8 8.7 %collective-permute-start.9 = (bf16[512,128]{1,0:T(8,128)(2,1)S(1)}, bf16[512,128]{1,0:T(8,128)(2,1)S(1)}, u32[]{:S(2)}, u32[]{:S(2)}) collective-permute-start(bf16[512,128]{1,0:T(8,128)(2,1)S(1)} %get-tuple-element.47), channel_id=1, source_target_pairs={{0,1},{1,2},{2,3},{3,0},{4,5},{5,6},{6,7},{7,4},{8,9},{9,10},{10,1... | collective-permute-start | bytes 393224 | tf_op jit(solution)/shard_map/ppermute | solution.py:312
  54.0 11.7 %copy-start.8 = (bf16[512,128]{1,0:T(8,128)(2,1)}, bf16[512,128]{1,0:T(8,128)(2,1)S(1)}, u32[]{:S(2)}) copy-start(bf16[512,128]{1,0:T(8,128)(2,1)S(1)} %get-tuple-element.49.tile1) | copy-start | bytes 393220
  54.0 11.7 %copy-start.10 = (bf16[512,128]{1,0:T(8,128)(2,1)}, bf16[512,128]{1,0:T(8,128)(2,1)S(1)}, u32[]{:S(2)}) copy-start(bf16[512,128]{1,0:T(8,128)(2,1)S(1)} %get-tuple-element.50.tile2) | copy-start | bytes 393220
  54.0 11.7 %copy-start.12 = (bf16[512,128]{1,0:T(8,128)(2,1)}, bf16[512,128]{1,0:T(8,128)(2,1)S(1)}, u32[]{:S(2)}) copy-start(bf16[512,128]{1,0:T(8,128)(2,1)S(1)} %get-tuple-element.51.tile3) | copy-start | bytes 393220
  54.0 4.6 %collective-permute-start.10 = (bf16[512,128]{1,0:T(8,128)(2,1)S(1)}, bf16[512,128]{1,0:T(8,128)(2,1)S(1)}, u32[]{:S(2)}, u32[]{:S(2)}) collective-permute-start(bf16[512,128]{1,0:T(8,128)(2,1)S(1)} %get-tuple-element.51.tile3), channel_id=1, source_target_pairs={{0,3},{1,0},{2,1},{3,2},{4,7},{5,4},{6,5},{7,6},{8,11},{9,8},{10,9... | collective-permute-start | bytes 393224 | tf_op jit(solution)/shard_map/ppermute | solution.py:312
  54.1 5.5 %collective-permute-start.11 = (bf16[512,128]{1,0:T(8,128)(2,1)S(1)}, bf16[512,128]{1,0:T(8,128)(2,1)S(1)}, u32[]{:S(2)}, u32[]{:S(2)}) collective-permute-start(bf16[512,128]{1,0:T(8,128)(2,1)S(1)} %get-tuple-element.50.tile2), channel_id=1, source_target_pairs={{0,2},{1,3},{2,0},{3,1},{4,6},{5,7},{6,4},{7,5},{8,10},{9,11},{10,... | collective-permute-start | bytes 393224 | tf_op jit(solution)/shard_map/ppermute | solution.py:312
  55.2 8.2 %collective-permute-start.12 = (bf16[512,128]{1,0:T(8,128)(2,1)S(1)}, bf16[512,128]{1,0:T(8,128)(2,1)S(1)}, u32[]{:S(2)}, u32[]{:S(2)}) collective-permute-start(bf16[512,128]{1,0:T(8,128)(2,1)S(1)} %get-tuple-element.49.tile1), channel_id=1, source_target_pairs={{0,1},{1,2},{2,3},{3,0},{4,5},{5,6},{6,7},{7,4},{8,9},{9,10},{10,1... | collective-permute-start | bytes 393224 | tf_op jit(solution)/shard_map/ppermute | solution.py:312
  65.7 0.7 copy-start.5
  66.3 19.5 %all-to-all-start.1 = ((bf16[64,16,128]{2,1,0:T(8,128)(2,1)}), bf16[64,16,128]{2,1,0:T(8,128)(2,1)S(1)}, u32[]{:S(2)}, u32[]{:S(2)}) async-start(bf16[64,16,128]{2,1,0:T(8,128)(2,1)} %get-tuple-element.54), calls=%async_computation.1 | async-start | bytes 524288 | tf_op jit(solution)/shard_map/all_to_all | solution.py:319
  71.8 11.5 %collective-permute-start.13 = (bf16[80,128]{1,0:T(8,128)(2,1)}, bf16[80,128]{1,0:T(8,128)(2,1)S(1)}, u32[]{:S(2)}, u32[]{:S(2)}) collective-permute-start(bf16[80,128]{1,0:T(8,128)(2,1)} %get-tuple-element.55), channel_id=1, source_target_pairs={{0,248},{4,252},{8,0},{12,4},{16,8},{20,12},{24,16},{28,20},{32,24... | collective-permute-start | bytes 61448 | tf_op jit(solution)/shard_map/ppermute | solution.py:323
  76.9 6.4 %collective-permute-start.14 = (bf16[80,128]{1,0:T(8,128)(2,1)}, bf16[80,128]{1,0:T(8,128)(2,1)S(1)}, u32[]{:S(2)}, u32[]{:S(2)}) collective-permute-start(bf16[80,128]{1,0:T(8,128)(2,1)} %get-tuple-element.56), channel_id=1, source_target_pairs={{0,252},{4,0},{8,4},{12,8},{16,12},{20,16},{24,20},{28,24},{32,28}... | collective-permute-start | bytes 61448 | tf_op jit(solution)/shard_map/ppermute | solution.py:323
  77.5 5.8 %collective-permute-start.15 = (bf16[80,128]{1,0:T(8,128)(2,1)}, bf16[80,128]{1,0:T(8,128)(2,1)S(1)}, u32[]{:S(2)}, u32[]{:S(2)}) collective-permute-start(bf16[80,128]{1,0:T(8,128)(2,1)} %get-tuple-element.57), channel_id=1, source_target_pairs={{0,4},{4,8},{8,12},{12,16},{16,20},{20,24},{24,28},{28,32},{32,36}... | collective-permute-start | bytes 61448 | tf_op jit(solution)/shard_map/ppermute | solution.py:323
  78.6 15.2 %copy-start.20 = (bf16[512]{0:T(512)(128)(2,1)S(1)}, bf16[512]{0:T(512)(128)(2,1)}, u32[]{:S(2)}) copy-start(bf16[512]{0:T(512)(128)(2,1)} %param.26) | copy-start | bytes 3076
  78.6 15.2 %copy-start = (bf16[1024,512]{1,0:T(8,128)(2,1)S(1)}, bf16[1024,512]{1,0:T(8,128)(2,1)}, u32[]{:S(2)}) copy-start(bf16[1024,512]{1,0:T(8,128)(2,1)} %w1.3) | copy-start | bytes 3145732
  78.6 15.2 %copy-start.2 = (bf16[512,512]{1,0:T(8,128)(2,1)S(1)}, bf16[512,512]{1,0:T(8,128)(2,1)}, u32[]{:S(2)}) copy-start(bf16[512,512]{1,0:T(8,128)(2,1)} %w2.3) | copy-start | bytes 1572868
  78.6 15.2 %copy-start.4 = (bf16[80,512]{1,0:T(8,128)(2,1)S(1)}, bf16[80,512]{1,0:T(8,128)(2,1)}, u32[]{:S(2)}) copy-start(bf16[80,512]{1,0:T(8,128)(2,1)} %nodes.3) | copy-start | bytes 245764
  78.6 6.6 %collective-permute-start.16 = (bf16[80,128]{1,0:T(8,128)(2,1)}, bf16[80,128]{1,0:T(8,128)(2,1)S(1)}, u32[]{:S(2)}, u32[]{:S(2)}) collective-permute-start(bf16[80,128]{1,0:T(8,128)(2,1)} %get-tuple-element.58), channel_id=1, source_target_pairs={{0,8},{4,12},{8,16},{12,20},{16,24},{20,28},{24,32},{28,36},{32,40... | collective-permute-start | bytes 61448 | tf_op jit(solution)/shard_map/ppermute | solution.py:323
  79.5 0.9 copy-start.9
  80.4 0.9 copy-start.11
  81.3 0.9 copy-start.13
  82.2 11.7 %copy-start.21 = (bf16[512]{0:T(512)(128)(2,1)S(1)}, bf16[512]{0:T(512)(128)(2,1)}, u32[]{:S(2)}) copy-start(bf16[512]{0:T(512)(128)(2,1)} %param.27) | copy-start | bytes 3076
  83.3 0.6 copy-start.14
  85.2 0.6 copy-start.16
  85.8 0.9 copy-start.6
  86.8 0.7 copy-start.15
  87.5 0.7 copy-start.17
  88.6 2.7 %collective-permute-start.17 = (bf16[80,128]{1,0:T(8,128)(2,1)S(1)}, bf16[80,128]{1,0:T(8,128)(2,1)S(1)}, u32[]{:S(2)}, u32[]{:S(2)}) collective-permute-start(bf16[80,128]{1,0:T(8,128)(2,1)S(1)} %get-tuple-element.61), channel_id=1, source_target_pairs={{0,3},{1,0},{2,1},{3,2},{4,7},{5,4},{6,5},{7,6},{8,11},{9,8},{10,9... | collective-permute-start | bytes 61448 | tf_op jit(solution)/shard_map/ppermute | solution.py:312
  89.4 4.1 %collective-permute-start.18 = (bf16[80,128]{1,0:T(8,128)(2,1)S(1)}, bf16[80,128]{1,0:T(8,128)(2,1)S(1)}, u32[]{:S(2)}, u32[]{:S(2)}) collective-permute-start(bf16[80,128]{1,0:T(8,128)(2,1)S(1)} %get-tuple-element.62), channel_id=1, source_target_pairs={{0,2},{1,3},{2,0},{3,1},{4,6},{5,7},{6,4},{7,5},{8,10},{9,11},{10,... | collective-permute-start | bytes 61448 | tf_op jit(solution)/shard_map/ppermute | solution.py:312
  90.0 3.8 %collective-permute-start.19 = (bf16[80,128]{1,0:T(8,128)(2,1)S(1)}, bf16[80,128]{1,0:T(8,128)(2,1)S(1)}, u32[]{:S(2)}, u32[]{:S(2)}) collective-permute-start(bf16[80,128]{1,0:T(8,128)(2,1)S(1)} %get-tuple-element.63), channel_id=1, source_target_pairs={{0,1},{1,2},{2,3},{3,0},{4,5},{5,6},{6,7},{7,4},{8,9},{9,10},{10,1... | collective-permute-start | bytes 61448 | tf_op jit(solution)/shard_map/ppermute | solution.py:312

commit v3 on v2

--- a/solution.py
+++ b/solution.py
@@ -1,3 +1,5 @@
+import functools
+
 import jax
 import jax.numpy as jnp
 from jax import lax
@@ -52,12 +54,13 @@
     return jnp.where(mask, 1.0, 0.0).astype(BF16)
 
 
-def call(body, outs, specs, scratch=(), flops=10**8, room=8):
+def call(body, outs, specs, scratch=(), flops=10**8, room=8, alias=None):
     return pl.pallas_call(
         body,
         out_shape=outs,
         in_specs=specs,
         scratch_shapes=list(scratch),
+        input_output_aliases=alias or {},
         compiler_params=pltpu.CompilerParams(vmem_limit_bytes=room * 2**20),
         cost_estimate=pl.CostEstimate(flops=flops, bytes_accessed=10**6, transcendentals=0),
     )
@@ -76,32 +79,35 @@
     return ((owner - lax.axis_index("feat")) & (FEAT - 1)) * OWN + node - owner * OWN
 
 
-def project_body(nodes, w1, senders, refs, *rest):
-    outs, (weights, ids, quarters, sems) = rest[:FEAT], rest[FEAT:]
+def project_body(nodes_hbm, w1, senders, refs, *rest):
+    outs, (nodes, weights, ids, quarters, sems) = rest[:FEAT], rest[FEAT:]
     loads = [
-        pltpu.make_async_copy(
-            w1.at[pl.ds(D + k * D, D), :], weights.at[pl.ds(k * D, D), :], sems.at[k]
-        )
-        for k in range(2)
+        pltpu.make_async_copy(nodes_hbm, nodes, sems.at[2]),
+        pltpu.make_async_copy(w1.at[pl.ds(D, D), :], weights.at[pl.ds(0, D), :], sems.at[0]),
+        pltpu.make_async_copy(w1.at[pl.ds(2 * D, D), :], weights.at[pl.ds(D, D), :], sems.at[1]),
+        pltpu.make_async_copy(senders, ids.at[0], sems.at[3]),
+        pltpu.make_async_copy(refs, ids.at[1], sems.at[4]),
     ]
     for load in loads:
         load.start()
-    rows = nodes[...]
-    ids[0:4, :] = senders[...]
-    ids[4:8, :] = refs[...]
-    both = ids[...]
+    loads[3].wait()
+    loads[4].wait()
+    both = jnp.concatenate([ids[0], ids[1]], axis=0)
     planes = jnp.concatenate(
         [lax.shift_right_logical(both, 7).astype(F32), (both & 127).astype(F32)], axis=0
     ).astype(BF16)
+    for out in outs:
+        out[OWN : OWN + 16, 0:Q] = planes
+        out[OWN : OWN + 16, Q : 2 * Q] = jnp.zeros((16, Q), BF16)
+    loads[0].wait()
+    rows = nodes[...]
     for k in range(2):
-        loads[k].wait()
+        loads[1 + k].wait()
         product = dot(rows, weights[k * D : (k + 1) * D, :]).astype(BF16)
         for q in range(FEAT):
             quarters[q, :, (1 - k) * Q : (2 - k) * Q] = product[:, q * Q : (q + 1) * Q]
     for p, out in enumerate(outs):
         out[0:OWN, :] = quarters[peer(p)]
-        out[OWN : OWN + 16, 0:Q] = planes
-        out[OWN : OWN + 16, Q : 2 * Q] = jnp.zeros((16, Q), BF16)
 
 
 def list_rows(lists, select):
@@ -173,21 +179,20 @@
             acc[e : e + Q, :] = dot(picks, both)
 
 
-def gather_body(acc, rowid, far, near0, near1, near2, near3, *outs):
+def gather_body(p, acc, rowid, far, near0, near1, near2, near3, out):
     table = [far[b * 16 : (b + 1) * 16].reshape(256, Q) for b in range(4)]
     table.append(jnp.concatenate([near0[...], near1[...], near2[...], near3[...]], axis=0))
-    for p, out in enumerate(outs):
-        for half in range(2):
-            m = p * 2 + half
-            col = jnp.concatenate(
-                [column(rowid[2 * m + k : 2 * m + k + 1, :]) for k in range(2)], axis=0
-            )
-            total = acc[m * 256 : (m + 1) * 256, :]
-            for b in range(5):
-                width = table[b].shape[0]
-                picks = hot(widened(col, width) == iota((256, width), 1) + (NODES + b * 256))
-                total += dot(picks, table[b])
-            out[half * 256 : (half + 1) * 256, :] = total.astype(BF16)
+    for half in range(2):
+        m = p * 2 + half
+        col = jnp.concatenate(
+            [column(rowid[2 * m + k : 2 * m + k + 1, :]) for k in range(2)], axis=0
+        )
+        total = acc[m * 256 : (m + 1) * 256, :]
+        for b in range(5):
+            width = table[b].shape[0]
+            picks = hot(widened(col, width) == iota((256, width), 1) + (NODES + b * 256))
+            total += dot(picks, table[b])
+        out[half * 256 : (half + 1) * 256, :] = total.astype(BF16)
 
 
 def wide(quarters):
@@ -254,24 +259,30 @@
     return total
 
 
-def first_sums_body(tile0, rowid, acc):
+def first_sums_body(tile, rowid, acc):
     for base, size in BLOCKS:
-        acc[base : base + size, :] = block_sum(base, size, rowid, tile0, 0)
-
-
-def sums_body(acc, tile1, tile2, tile3, rowid, own, far, near0, near1, near2, near3):
+        acc[base : base + size, :] = block_sum(base, size, rowid, tile, 0)
+
+
+def more_sums_body(p, acc, tile, rowid, out):
     for base, size in BLOCKS:
-        total = acc[base : base + size, :]
-        for p, tile in enumerate((tile1, tile2, tile3)):
-            total += block_sum(base, size, rowid, tile, p + 1)
-        if base == 0:
-            own[...] = total
-        elif base < NODES + FAR_ROWS:
-            at = (base - NODES) // FAR
-            far[at : at + 16] = total.astype(BF16).reshape(16, FAR, Q)
-        else:
-            for j, out in enumerate((near0, near1, near2, near3)):
-                out[...] = total[j * NEAR : (j + 1) * NEAR].astype(BF16)
+        rows = slice(base, base + size)
+        out[rows, :] = acc[rows, :] + block_sum(base, size, rowid, tile, p)
+
+
+def far_sums_body(acc, tile, rowid, done, far):
+    for base, size in BLOCKS[1:5]:
+        total = acc[base : base + size, :] + block_sum(base, size, rowid, tile, 2)
+        at = (base - NODES) // FAR
+        far[at : at + 16] = total.astype(BF16).reshape(16, FAR, Q)
+
+
+def rest_sums_body(acc, tile, rowid, far, own, near0, near1, near2, near3):
+    own[...] = acc[0:NODES, :] + block_sum(0, NODES, rowid, tile, 2)
+    base = NODES + FAR_ROWS
+    total = acc[base:TABLE_ROWS, :] + block_sum(base, NEAR_ROWS, rowid, tile, 2)
+    for j, out in enumerate((near0, near1, near2, near3)):
+        out[...] = total[j * NEAR : (j + 1) * NEAR].astype(BF16)
 
 
 def flip_body(lists, spread, select):
@@ -283,7 +294,7 @@
         )
 
 
-def spread_body(spread, own, far, near0, near1, near2, near3, after, *outs):
+def spread_body(spread, own, far, near0, near1, near2, near3, *outs):
     total = own[...]
     for b in range(4):
         total += dot(
@@ -305,6 +316,10 @@
     hidden = silu(pre).astype(BF16)
     update = normed(dot(hidden, w2[...]), wide(gain), wide(shift))
     out[...] = (feats.astype(F32) + update).astype(BF16)
+
+
+def in_hbm(value):
+    return pltpu.with_memory_space_constraint(value, pltpu.HBM)
 
 
 def exchanged(tiles):
@@ -342,14 +357,15 @@
     tiles = call(
         project_body,
         [shape((96, 256), BF16)] * FEAT,
-        [VMEM, HBM, VMEM, VMEM],
+        [HBM] * 4,
         [
+            pltpu.VMEM((OWN, D), BF16),
             pltpu.VMEM((2 * D, D), BF16),
-            pltpu.VMEM((8, Q), I32),
+            pltpu.VMEM((2, 4, Q), I32),
             pltpu.VMEM((FEAT, OWN, 2 * Q), BF16),
-            pltpu.SemaphoreType.DMA((2,)),
+            pltpu.SemaphoreType.DMA((5,)),
         ],
-    )(node_feats, pltpu.with_memory_space_constraint(edge_w1, pltpu.HBM), senders.reshape(4, Q), receiver_ref.reshape(4, Q))
+    )(*(in_hbm(x) for x in (node_feats, edge_w1, senders.reshape(4, Q), receiver_ref.reshape(4, Q))))
     tiles = exchanged(tiles)
     select = call(lists_body, shape((LIST_ROWS, NODES), BF16), [VMEM])(send_list[0])
 
@@ -369,7 +385,10 @@
         flops=10**9,
     )(*tiles)
     quarter = [shape((EDGES, Q), BF16)] * FEAT
-    picked = call(gather_body, quarter, [VMEM] * 7, flops=10**9)(acc, rowid, far, *near)
+    picked = [
+        call(functools.partial(gather_body, p), quarter[0], [VMEM] * 7)(acc, rowid, far, *near)
+        for p in range(FEAT)
+    ]
     picked = exchanged(picked)
 
     messages = call(
@@ -387,32 +406,33 @@
         edge_gain.reshape(4, Q),
         edge_shift.reshape(4, Q),
     )
-    arrived = exchanged(messages)
-    partial = call(first_sums_body, shape((TABLE_ROWS, Q), F32), [VMEM] * 2, flops=10**8)(
-        messages[0], rowid
-    )
-    own, far, *near = call(
-        sums_body,
-        (shape((NODES, Q), F32), far_shape, *near_shape),
-        [VMEM] * 5,
-        flops=10**9,
-    )(partial, *arrived[1:], rowid)
-    far = swapped(far)
-    near = [moved(value, d) for value, d in zip(near, OFFSETS)]
     new_edges, done = call(
         finish_body,
         (shape((EDGES, D), BF16), shape((8, Q), F32)),
         [SMEM] + [VMEM] * 5,
         [pltpu.VMEM((FEAT, EDGES, Q), BF16)],
     )(edge_count, edge_feats, *messages)
+    arrived = exchanged(messages)
+    acc_shape = shape((TABLE_ROWS, Q), F32)
+    acc = call(first_sums_body, acc_shape, [VMEM] * 2)(messages[0], rowid)
+    for p in (3, 1):
+        acc = call(functools.partial(more_sums_body, p), acc_shape, [VMEM] * 3, alias={0: 0})(
+            acc, arrived[p], rowid
+        )
+    sent = call(far_sums_body, far_shape, [VMEM] * 4)(acc, arrived[2], rowid, done)
+    far = swapped(sent)
+    own, *near = call(
+        rest_sums_body, (shape((NODES, Q), F32), *near_shape), [VMEM] * 3 + [HBM]
+    )(acc, arrived[2], rowid, sent)
+    near = [moved(value, d) for value, d in zip(near, OFFSETS)]
     spread = call(
         flip_body,
         shape((NODES, LIST_ROWS), BF16),
         [VMEM],
         [pltpu.VMEM((LIST_ROWS, NODES), BF16)],
     )(send_list[0])
-    sums = call(spread_body, [shape((OWN, Q), BF16)] * FEAT, [VMEM] * 8)(
-        spread, own, far, *near, done
+    sums = call(spread_body, [shape((OWN, Q), BF16)] * FEAT, [VMEM] * 7)(
+        spread, own, far, *near
     )
     sums = exchanged(sums)
     new_nodes = call(

time: 95.7 us -> 90 us (0.940)
  local copies, waits for them, and re-layouts: 10.3 us -> 1.14 us
  starting transfers between devices: 43.4 us -> 49 us
  waiting for transfers between devices: 25.8 us -> 22.6 us
  Pallas kernels: 14.1 us -> 15.4 us
    unnamed x50 -> x20, local copies, waits for them, and re-layouts: 9.23 us -> 0.06 us
    ppermute x12, waiting for transfers between devices: 19.7 us -> 12.2 us  [exchanged(): lax.ppermute(tiles[j], 'feat', [(i, (i + j) % FEAT) for i in range(FEAT)])]
    ppermute x12, starting transfers between devices: 10.5 us -> 15.5 us  [exchanged(): lax.ppermute(tiles[j], 'feat', [(i, (i + j) % FEAT) for i in range(FEAT)])]
    ppermute x8, waiting for transfers between devices: 2.95 us -> 7.21 us  [moved(): lax.ppermute(value, 'graph', [(i, (i + by) % GROUPS) for i in range(GROUP...]
    pallas_call x5 -> x11, Pallas kernels: 6.47 us -> 7.77 us  [the longest x4 2.35 us: per_device(): call(functools.partial(gather_body, p), quarter[0], [VMEM] * 7)]
  transfers between devices with their start and end apart: 22 -> 22, of which waited for: 14 -> 11; matrix products, arithmetic and copies ran while one was open for 1% -> 1% of each run, Pallas kernels for 5% -> 9%
where the time goes in v3:
time: 90 us; the launch traced here: 89.7 us
  starting transfers between devices  49 us (54%)
  waiting for transfers between devices  22.6 us (25%)
  Pallas kernels  15.4 us (17%)
  between operations  1.57 us (2%)
  local copies, waits for them, and re-layouts  1.14 us (1%)
    all_to_all x2, starting transfers between devices, swapped(): lax.all_to_all(value, 'graph', split_axis=0, concat_axis=0, tiled=True)  20 us
    ppermute x12, starting transfers between devices, exchanged(): lax.ppermute(tiles[j], 'feat', [(i, (i + j) % FEAT) for i in range(FEAT)])  15.5 us
    ppermute x8, starting transfers between devices, moved(): lax.ppermute(value, 'graph', [(i, (i + by) % GROUPS) for i in range(GROUP...  13.6 us
    ppermute x12, waiting for transfers between devices, exchanged(): lax.ppermute(tiles[j], 'feat', [(i, (i + j) % FEAT) for i in range(FEAT)])  12.2 us
    ppermute x8, waiting for transfers between devices, moved(): lax.ppermute(value, 'graph', [(i, (i + by) % GROUPS) for i in range(GROUP...  7.21 us
    all_to_all x2, waiting for transfers between devices, swapped(): lax.all_to_all(value, 'graph', split_axis=0, concat_axis=0, tiled=True)  3.18 us
    pallas_call x4, Pallas kernels, per_device(): call(functools.partial(gather_body, p), quarter[0], [VMEM] * 7)  2.35 us
  transfers between devices with their start and end apart: 22, of which 11 were waited for; matrix products, arithmetic and copies ran while one was open for 1% of the time, Pallas kernels for 9%

profile of v3, /device:TPU:1, one launch (start us, length us, event | category | flops | bytes accessed | tf_op | source)
XLA Modules:
  0.0 89.7 jit_solution(16429087251288754926)
XLA Ops:
  0.6 1.6 %shard_map.149 = (bf16[96,256]{1,0:T(8,128)(2,1)S(1)}, bf16[96,256]{1,0:T(8,128)(2,1)S(1)}, bf16[96,256]{1,0:T(8,128)(2,1)S(1)}, bf16[96,256]{1,0:T(8,128)(2,1)S(1)}) custom-call(bf16[80,512]{1,0:T(8,128)(2,1)} %nodes.1, bf16[1536,512]{1,0:T(8,128)(2,1)} %w1.2, s32[4,128]{1,0:T(4,128)} %bitcast.13, s32[4,128]{1,0:T(4,128)} %bitcast.14), custom_call_target="tpu_custom_call" | custom-call | flops 100000000 | bytes 1000000 | tf_op jit(solution)/shard_map/pallas_call | solution.py:357
  2.2 3.4 %collective-permute-start = (bf16[96,256]{1,0:T(8,128)(2,1)S(1)}, bf16[96,256]{1,0:T(8,128)(2,1)S(1)}, u32[]{:S(2)}, u32[]{:S(2)}) collective-permute-start(bf16[96,256]{1,0:T(8,128)(2,1)S(1)} %get-tuple-element.29), channel_id=1, source_target_pairs={{0,3},{1,0},{2,1},{3,2},{4,7},{5,4},{6,5},{7,6},{8,11},{9,8},{10,9... | collective-permute-start | bytes 147464 | tf_op jit(solution)/shard_map/ppermute | solution.py:327
  5.6 0.5 collective-permute-start.1
  6.1 0.6 collective-permute-start.2
  6.7 0.5 shard_map.151.select
  7.2 2.9 %collective-permute-done.1.tile2 = bf16[96,256]{1,0:T(8,128)(2,1)S(1)} collective-permute-done((bf16[96,256]{1,0:T(8,128)(2,1)S(1)}, bf16[96,256]{1,0:T(8,128)(2,1)S(1)}, u32[]{:S(2)}, u32[]{:S(2)}) %collective-permute-start.1) | collective-permute-done | bytes 49184 | tf_op jit(solution)/shard_map/ppermute | solution.py:327
  10.1 0.5 collective-permute-done.2.tile3
  10.6 1.1 %shard_map.152 = (bf16[64,16,128]{2,1,0:T(8,128)(2,1)}, bf16[80,128]{1,0:T(8,128)(2,1)S(1)}, bf16[80,128]{1,0:T(8,128)(2,1)S(1)}, bf16[80,128]{1,0:T(8,128)(2,1)S(1)}, bf16[80,128]{1,0:T(8,128)(2,1)S(1)}) custom-call(bf16[96,256]{1,0:T(8,128)(2,1)S(1)} %get-tuple-element.28.tile0, bf16[96,256]{1,0:T(8,128)(2,1)S(1)} %collective-permute-done.tile1, ...), custom_call_target="tpu_custom_call" | custom-call | flops 100000000 | bytes 1000000 | tf_op jit(solution)/shard_map/pallas_call | solution.py:374
  11.7 13.8 %all-to-all-start = ((bf16[64,16,128]{2,1,0:T(8,128)(2,1)}), bf16[64,16,128]{2,1,0:T(8,128)(2,1)S(1)}, u32[]{:S(2)}, u32[]{:S(2)}) async-start(bf16[64,16,128]{2,1,0:T(8,128)(2,1)} %get-tuple-element.34), calls=%async_computation | async-start | bytes 524288 | tf_op jit(solution)/shard_map/all_to_all | solution.py:334
  25.4 1.4 %collective-permute-start.3 = (bf16[80,128]{1,0:T(8,128)(2,1)S(1)}, bf16[80,128]{1,0:T(8,128)(2,1)S(1)}, u32[]{:S(2)}, u32[]{:S(2)}) collective-permute-start(bf16[80,128]{1,0:T(8,128)(2,1)S(1)} %get-tuple-element.35), channel_id=1, source_target_pairs={{0,8},{4,12},{8,16},{12,20},{16,24},{20,28},{24,32},{28,36},{32,40... | collective-permute-start | bytes 61448 | tf_op jit(solution)/shard_map/ppermute | solution.py:338
  26.8 1.7 %collective-permute-start.4 = (bf16[80,128]{1,0:T(8,128)(2,1)S(1)}, bf16[80,128]{1,0:T(8,128)(2,1)S(1)}, u32[]{:S(2)}, u32[]{:S(2)}) collective-permute-start(bf16[80,128]{1,0:T(8,128)(2,1)S(1)} %get-tuple-element.36), channel_id=1, source_target_pairs={{0,4},{4,8},{8,12},{12,16},{16,20},{20,24},{24,28},{28,32},{32,36}... | collective-permute-start | bytes 61448 | tf_op jit(solution)/shard_map/ppermute | solution.py:338
  28.6 3.6 %collective-permute-start.6 = (bf16[80,128]{1,0:T(8,128)(2,1)S(1)}, bf16[80,128]{1,0:T(8,128)(2,1)S(1)}, u32[]{:S(2)}, u32[]{:S(2)}) collective-permute-start(bf16[80,128]{1,0:T(8,128)(2,1)S(1)} %get-tuple-element.38), channel_id=1, source_target_pairs={{0,248},{4,252},{8,0},{12,4},{16,8},{20,12},{24,16},{28,20},{32,24... | collective-permute-start | bytes 61448 | tf_op jit(solution)/shard_map/ppermute | solution.py:338
  32.2 1.5 %shard_map.150 = (s32[16,128]{1,0:T(8,128)S(1)}, f32[2048,128]{1,0:T(8,128)S(1)}) custom-call(bf16[96,256]{1,0:T(8,128)(2,1)S(1)} %get-tuple-element.28.tile0, bf16[96,256]{1,0:T(8,128)(2,1)S(1)} %collective-permute-done.tile1, bf16[96,256]{1,0:T(8,128)(2,1)S(1)} %collective-permute-done.1.tile2, bf16[96,256]{1,0:T(8,128)(2,1)S(1)} %collective-permute-done.2.tile3), custom_call_target="tpu_custom_call" | custom-call | flops 1000000000 | bytes 1000000 | tf_op jit(solution)/shard_map/pallas_call | solution.py:378
  33.7 1.6 %collective-permute-done.3.near0 = bf16[80,128]{1,0:T(8,128)(2,1)S(1)} collective-permute-done((bf16[80,128]{1,0:T(8,128)(2,1)S(1)}, bf16[80,128]{1,0:T(8,128)(2,1)S(1)}, u32[]{:S(2)}, u32[]{:S(2)}) %collective-permute-start.3) | collective-permute-done | bytes 20512 | tf_op jit(solution)/shard_map/ppermute | solution.py:338
  35.3 3.2 %all-to-all-done.far = bf16[64,16,128]{2,1,0:T(8,128)(2,1)S(1)} async-done(((bf16[64,16,128]{2,1,0:T(8,128)(2,1)}), bf16[64,16,128]{2,1,0:T(8,128)(2,1)S(1)}, u32[]{:S(2)}, u32[]{:S(2)}) %all-to-all-start) | async-done | bytes 262176 | tf_op jit(solution)/shard_map/all_to_all | solution.py:334
  38.5 0.6 shard_map.156
  39.1 0.1 collective-permute-start.9
  39.2 0.6 shard_map.155
  39.8 1.5 %collective-permute-start.8 = (bf16[512,128]{1,0:T(8,128)(2,1)S(1)}, bf16[512,128]{1,0:T(8,128)(2,1)S(1)}, u32[]{:S(2)}, u32[]{:S(2)}) collective-permute-start(bf16[512,128]{1,0:T(8,128)(2,1)S(1)} %shard_map.155), channel_id=1, source_target_pairs={{0,2},{1,3},{2,0},{3,1},{4,6},{5,7},{6,4},{7,5},{8,10},{9,11},{10,... | collective-permute-start | bytes 393224 | tf_op jit(solution)/shard_map/ppermute | solution.py:327
  41.3 0.6 shard_map.154
  41.9 0.0 copy-start.1
  41.9 0.0 copy-start.7
  41.9 0.0 copy-start.8
  41.9 0.0 copy-start.9
  42.0 2.1 %collective-permute-start.7 = (bf16[512,128]{1,0:T(8,128)(2,1)S(1)}, bf16[512,128]{1,0:T(8,128)(2,1)S(1)}, u32[]{:S(2)}, u32[]{:S(2)}) collective-permute-start(bf16[512,128]{1,0:T(8,128)(2,1)S(1)} %shard_map.154), channel_id=1, source_target_pairs={{0,3},{1,0},{2,1},{3,2},{4,7},{5,4},{6,5},{7,6},{8,11},{9,8},{10,9... | collective-permute-start | bytes 393224 | tf_op jit(solution)/shard_map/ppermute | solution.py:327
  44.0 1.1 %slice.3.w1 = bf16[512,512]{1,0:T(8,128)(2,1)S(1)} slice(bf16[1536,512]{1,0:T(8,128)(2,1)} %w1.2), slice={[0:512], [0:512]} | slice | bytes 1048576 | tf_op jit(solution)/shard_map/slice | solution.py:404
  45.8 0.6 shard_map.153.tile0
  46.4 1.6 %collective-permute-done.9.tile3 = bf16[512,128]{1,0:T(8,128)(2,1)S(1)} collective-permute-done((bf16[512,128]{1,0:T(8,128)(2,1)S(1)}, bf16[512,128]{1,0:T(8,128)(2,1)S(1)}, u32[]{:S(2)}, u32[]{:S(2)}) %collective-permute-start.9) | collective-permute-done | bytes 131104 | tf_op jit(solution)/shard_map/ppermute | solution.py:327
  48.0 1.0 %collective-permute-done.7.tile1 = bf16[512,128]{1,0:T(8,128)(2,1)S(1)} collective-permute-done((bf16[512,128]{1,0:T(8,128)(2,1)S(1)}, bf16[512,128]{1,0:T(8,128)(2,1)S(1)}, u32[]{:S(2)}, u32[]{:S(2)}) %collective-permute-start.7) | collective-permute-done | bytes 131104 | tf_op jit(solution)/shard_map/ppermute | solution.py:327
  49.0 1.4 %shard_map.157 = (bf16[512,128]{1,0:T(8,128)(2,1)S(1)}, bf16[512,128]{1,0:T(8,128)(2,1)S(1)}, bf16[512,128]{1,0:T(8,128)(2,1)S(1)}, bf16[512,128]{1,0:T(8,128)(2,1)S(1)}) custom-call(s32[1]{0:T(128)S(6)} %copy.20.count, bf16[512,512]{1,0:T(8,128)(2,1)S(1)} %copy-done.1, bf16[512,128]{1,0:T(8,128)(2,1)S(1)} %shard_map.153.tile0, ...), custom_call_target="tpu_custom_call" | custom-call | flops 1000000000 | bytes 1000000 | tf_op jit(solution)/shard_map/pallas_call | solution.py:394
  50.4 1.1 %collective-permute-start.10 = (bf16[512,128]{1,0:T(8,128)(2,1)S(1)}, bf16[512,128]{1,0:T(8,128)(2,1)S(1)}, u32[]{:S(2)}, u32[]{:S(2)}) collective-permute-start(bf16[512,128]{1,0:T(8,128)(2,1)S(1)} %get-tuple-element.40.tile1), channel_id=1, source_target_pairs={{0,1},{1,2},{2,3},{3,0},{4,5},{5,6},{6,7},{7,4},{8,9},{9,10},{10,1... | collective-permute-start | bytes 393224 | tf_op jit(solution)/shard_map/ppermute | solution.py:327
  51.5 2.2 %collective-permute-start.11 = (bf16[512,128]{1,0:T(8,128)(2,1)S(1)}, bf16[512,128]{1,0:T(8,128)(2,1)S(1)}, u32[]{:S(2)}, u32[]{:S(2)}) collective-permute-start(bf16[512,128]{1,0:T(8,128)(2,1)S(1)} %get-tuple-element.42.tile3), channel_id=1, source_target_pairs={{0,3},{1,0},{2,1},{3,2},{4,7},{5,4},{6,5},{7,6},{8,11},{9,8},{10,9... | collective-permute-start | bytes 393224 | tf_op jit(solution)/shard_map/ppermute | solution.py:327
  53.6 1.1 %collective-permute-start.12 = (bf16[512,128]{1,0:T(8,128)(2,1)S(1)}, bf16[512,128]{1,0:T(8,128)(2,1)S(1)}, u32[]{:S(2)}, u32[]{:S(2)}) collective-permute-start(bf16[512,128]{1,0:T(8,128)(2,1)S(1)} %get-tuple-element.41.tile2), channel_id=1, source_target_pairs={{0,2},{1,3},{2,0},{3,1},{4,6},{5,7},{6,4},{7,5},{8,10},{9,11},{10,... | collective-permute-start | bytes 393224 | tf_op jit(solution)/shard_map/ppermute | solution.py:327
  54.7 0.6 shard_map.160.acc
  55.3 1.1 %shard_map.158 = (bf16[512,512]{1,0:T(8,128)(2,1)}, f32[8,128]{1,0:T(8,128)S(1)}) custom-call(s32[1]{0:T(128)S(6)} %copy.20.count, bf16[512,512]{1,0:T(8,128)(2,1)S(1)} %copy-done.1, bf16[512,128]{1,0:T(8,128)(2,1)S(1)} %get-tuple-element.39.tile0.tile, bf16[512,128]{1,0:T(8,128)(2,1)S(1)} %get-tuple-element.40.tile1, ...), custom_call_target="tpu_custom_call" | custom-call | flops 100000000 | bytes 1000000 | tf_op jit(solution)/shard_map/pallas_call | solution.py:409
  56.5 0.7 shard_map.161.acc
  57.1 0.7 shard_map.162.acc
  57.8 2.8 %collective-permute-done.12.tile = bf16[512,128]{1,0:T(8,128)(2,1)S(1)} collective-permute-done((bf16[512,128]{1,0:T(8,128)(2,1)S(1)}, bf16[512,128]{1,0:T(8,128)(2,1)S(1)}, u32[]{:S(2)}, u32[]{:S(2)}) %collective-permute-start.12) | collective-permute-done | bytes 131104 | tf_op jit(solution)/shard_map/ppermute | solution.py:327
  60.6 1.1 %shard_map.163.far = bf16[64,16,128]{2,1,0:T(8,128)(2,1)} custom-call(f32[1664,128]{1,0:T(8,128)S(1)} %shard_map.162.acc, bf16[512,128]{1,0:T(8,128)(2,1)S(1)} %collective-permute-done.12.tile, s32[16,128]{1,0:T(8,128)S(1)} %get-tuple-element.33.rowid, f32[8,128]{1,0:T(8,128)S(1)} %get-tuple-element.44.done), custom_call_target="tpu_custom_call" | custom-call | flops 100000000 | bytes 1000000 | tf_op jit(solution)/shard_map/pallas_call | solution.py:422
  61.7 6.2 %all-to-all-start.1 = ((bf16[64,16,128]{2,1,0:T(8,128)(2,1)}), bf16[64,16,128]{2,1,0:T(8,128)(2,1)S(1)}, u32[]{:S(2)}, u32[]{:S(2)}) async-start(bf16[64,16,128]{2,1,0:T(8,128)(2,1)} %shard_map.163.far), calls=%async_computation.1 | async-start | bytes 524288 | tf_op jit(solution)/shard_map/all_to_all | solution.py:334
  67.9 0.0 copy-start
  67.9 0.0 copy-start.2
  67.9 0.0 copy-start.3
  68.0 0.0 copy-start.5
  68.0 0.0 copy-start.6
  68.0 0.3 shard_map.164
  68.3 5.1 %collective-permute-start.13 = (bf16[80,128]{1,0:T(8,128)(2,1)S(1)}, bf16[80,128]{1,0:T(8,128)(2,1)S(1)}, u32[]{:S(2)}, u32[]{:S(2)}) collective-permute-start(bf16[80,128]{1,0:T(8,128)(2,1)S(1)} %get-tuple-element.46), channel_id=1, source_target_pairs={{0,248},{4,252},{8,0},{12,4},{16,8},{20,12},{24,16},{28,20},{32,24... | collective-permute-start | bytes 61448 | tf_op jit(solution)/shard_map/ppermute | solution.py:338
  73.4 0.7 collective-permute-start.14
  74.0 1.1 %collective-permute-start.15 = (bf16[80,128]{1,0:T(8,128)(2,1)S(1)}, bf16[80,128]{1,0:T(8,128)(2,1)S(1)}, u32[]{:S(2)}, u32[]{:S(2)}) collective-permute-start(bf16[80,128]{1,0:T(8,128)(2,1)S(1)} %get-tuple-element.48), channel_id=1, source_target_pairs={{0,4},{4,8},{8,12},{12,16},{16,20},{20,24},{24,28},{28,32},{32,36}... | collective-permute-start | bytes 61448 | tf_op jit(solution)/shard_map/ppermute | solution.py:338
  75.1 0.0 collective-permute-start.16
  75.1 0.7 shard_map.159.spread
  75.9 0.0 collective-permute-done.13.near0
  75.9 1.0 %collective-permute-done.14.near1 = bf16[80,128]{1,0:T(8,128)(2,1)S(1)} collective-permute-done((bf16[80,128]{1,0:T(8,128)(2,1)S(1)}, bf16[80,128]{1,0:T(8,128)(2,1)S(1)}, u32[]{:S(2)}, u32[]{:S(2)}) %collective-permute-start.14) | collective-permute-done | bytes 20512 | tf_op jit(solution)/shard_map/ppermute | solution.py:338
  76.9 0.0 collective-permute-done.15.near2
  76.9 4.6 %collective-permute-done.16.near3 = bf16[80,128]{1,0:T(8,128)(2,1)S(1)} collective-permute-done((bf16[80,128]{1,0:T(8,128)(2,1)S(1)}, bf16[80,128]{1,0:T(8,128)(2,1)S(1)}, u32[]{:S(2)}, u32[]{:S(2)}) %collective-permute-start.16) | collective-permute-done | bytes 20512 | tf_op jit(solution)/shard_map/ppermute | solution.py:338
  81.5 0.0 all-to-all-done.1.far
  81.5 0.4 shard_map.165
  81.9 2.3 %collective-permute-start.17 = (bf16[80,128]{1,0:T(8,128)(2,1)S(1)}, bf16[80,128]{1,0:T(8,128)(2,1)S(1)}, u32[]{:S(2)}, u32[]{:S(2)}) collective-permute-start(bf16[80,128]{1,0:T(8,128)(2,1)S(1)} %get-tuple-element.51), channel_id=1, source_target_pairs={{0,3},{1,0},{2,1},{3,2},{4,7},{5,4},{6,5},{7,6},{8,11},{9,8},{10,9... | collective-permute-start | bytes 61448 | tf_op jit(solution)/shard_map/ppermute | solution.py:327
  84.2 0.0 collective-permute-start.18
  84.2 0.7 collective-permute-start.19
  84.9 0.2 collective-permute-done.17.tile1
  85.1 3.2 %collective-permute-done.18.tile2 = bf16[80,128]{1,0:T(8,128)(2,1)S(1)} collective-permute-done((bf16[80,128]{1,0:T(8,128)(2,1)S(1)}, bf16[80,128]{1,0:T(8,128)(2,1)S(1)}, u32[]{:S(2)}, u32[]{:S(2)}) %collective-permute-start.18) | collective-permute-done | bytes 20512 | tf_op jit(solution)/shard_map/ppermute | solution.py:327
  88.4 0.0 collective-permute-done.19.tile3
  88.4 1.3 %shard_map.166 = bf16[80,512]{1,0:T(8,128)(2,1)} custom-call(bf16[80,512]{1,0:T(8,128)(2,1)S(1)} %copy-done.3, bf16[80,128]{1,0:T(8,128)(2,1)S(1)} %get-tuple-element.50.tile0, bf16[80,128]{1,0:T(8,128)(2,1)S(1)} %collective-permute-done.17.tile1, bf16[80,128]{1,0:T(8,128)(2,1)S(1)} %collective-permute-done.18.tile2, ...), custom_call_target="tpu_custom_call" | custom-call | flops 100000000 | bytes 1000000 | tf_op jit(solution)/shard_map/pallas_call | solution.py:438
  (19 shorter events, 0.0 us)
Async XLA Ops:
  0.6 6.1 %copy-start.4 = (s32[1,64,96]{2,1,0:T(8,128)S(1)}, s32[1,64,96]{2,1,0:T(8,128)}, u32[]{:S(2)}) copy-start(s32[1,64,96]{2,1,0:T(8,128)} %param.18) | copy-start | bytes 73732
  2.2 5.0 %collective-permute-start = (bf16[96,256]{1,0:T(8,128)(2,1)S(1)}, bf16[96,256]{1,0:T(8,128)(2,1)S(1)}, u32[]{:S(2)}, u32[]{:S(2)}) collective-permute-start(bf16[96,256]{1,0:T(8,128)(2,1)S(1)} %get-tuple-element.29), channel_id=1, source_target_pairs={{0,3},{1,0},{2,1},{3,2},{4,7},{5,4},{6,5},{7,6},{8,11},{9,8},{10,9... | collective-permute-start | bytes 147464 | tf_op jit(solution)/shard_map/ppermute | solution.py:327
  5.6 4.5 %collective-permute-start.1 = (bf16[96,256]{1,0:T(8,128)(2,1)S(1)}, bf16[96,256]{1,0:T(8,128)(2,1)S(1)}, u32[]{:S(2)}, u32[]{:S(2)}) collective-permute-start(bf16[96,256]{1,0:T(8,128)(2,1)S(1)} %get-tuple-element.30), channel_id=1, source_target_pairs={{0,2},{1,3},{2,0},{3,1},{4,6},{5,7},{6,4},{7,5},{8,10},{9,11},{10,... | collective-permute-start | bytes 147464 | tf_op jit(solution)/shard_map/ppermute | solution.py:327
  6.1 4.5 %collective-permute-start.2 = (bf16[96,256]{1,0:T(8,128)(2,1)S(1)}, bf16[96,256]{1,0:T(8,128)(2,1)S(1)}, u32[]{:S(2)}, u32[]{:S(2)}) collective-permute-start(bf16[96,256]{1,0:T(8,128)(2,1)S(1)} %get-tuple-element.31), channel_id=1, source_target_pairs={{0,1},{1,2},{2,3},{3,0},{4,5},{5,6},{6,7},{7,4},{8,9},{9,10},{10,1... | collective-permute-start | bytes 147464 | tf_op jit(solution)/shard_map/ppermute | solution.py:327
  11.7 26.8 %all-to-all-start = ((bf16[64,16,128]{2,1,0:T(8,128)(2,1)}), bf16[64,16,128]{2,1,0:T(8,128)(2,1)S(1)}, u32[]{:S(2)}, u32[]{:S(2)}) async-start(bf16[64,16,128]{2,1,0:T(8,128)(2,1)} %get-tuple-element.34), calls=%async_computation | async-start | bytes 524288 | tf_op jit(solution)/shard_map/all_to_all | solution.py:334
  25.4 9.9 %collective-permute-start.3 = (bf16[80,128]{1,0:T(8,128)(2,1)S(1)}, bf16[80,128]{1,0:T(8,128)(2,1)S(1)}, u32[]{:S(2)}, u32[]{:S(2)}) collective-permute-start(bf16[80,128]{1,0:T(8,128)(2,1)S(1)} %get-tuple-element.35), channel_id=1, source_target_pairs={{0,8},{4,12},{8,16},{12,20},{16,24},{20,28},{24,32},{28,36},{32,40... | collective-permute-start | bytes 61448 | tf_op jit(solution)/shard_map/ppermute | solution.py:338
  26.8 8.5 %collective-permute-start.4 = (bf16[80,128]{1,0:T(8,128)(2,1)S(1)}, bf16[80,128]{1,0:T(8,128)(2,1)S(1)}, u32[]{:S(2)}, u32[]{:S(2)}) collective-permute-start(bf16[80,128]{1,0:T(8,128)(2,1)S(1)} %get-tuple-element.36), channel_id=1, source_target_pairs={{0,4},{4,8},{8,12},{12,16},{16,20},{20,24},{24,28},{28,32},{32,36}... | collective-permute-start | bytes 61448 | tf_op jit(solution)/shard_map/ppermute | solution.py:338
  28.6 6.7 %collective-permute-start.5 = (bf16[80,128]{1,0:T(8,128)(2,1)S(1)}, bf16[80,128]{1,0:T(8,128)(2,1)S(1)}, u32[]{:S(2)}, u32[]{:S(2)}) collective-permute-start(bf16[80,128]{1,0:T(8,128)(2,1)S(1)} %get-tuple-element.37), channel_id=1, source_target_pairs={{0,252},{4,0},{8,4},{12,8},{16,12},{20,16},{24,20},{28,24},{32,28}... | collective-permute-start | bytes 61448 | tf_op jit(solution)/shard_map/ppermute | solution.py:338
  28.6 6.7 %collective-permute-start.6 = (bf16[80,128]{1,0:T(8,128)(2,1)S(1)}, bf16[80,128]{1,0:T(8,128)(2,1)S(1)}, u32[]{:S(2)}, u32[]{:S(2)}) collective-permute-start(bf16[80,128]{1,0:T(8,128)(2,1)S(1)} %get-tuple-element.38), channel_id=1, source_target_pairs={{0,248},{4,252},{8,0},{12,4},{16,8},{20,12},{24,16},{28,20},{32,24... | collective-permute-start | bytes 61448 | tf_op jit(solution)/shard_map/ppermute | solution.py:338
  39.1 8.9 %collective-permute-start.9 = (bf16[512,128]{1,0:T(8,128)(2,1)S(1)}, bf16[512,128]{1,0:T(8,128)(2,1)S(1)}, u32[]{:S(2)}, u32[]{:S(2)}) collective-permute-start(bf16[512,128]{1,0:T(8,128)(2,1)S(1)} %shard_map.156), channel_id=1, source_target_pairs={{0,1},{1,2},{2,3},{3,0},{4,5},{5,6},{6,7},{7,4},{8,9},{9,10},{10,1... | collective-permute-start | bytes 393224 | tf_op jit(solution)/shard_map/ppermute | solution.py:327
  39.8 8.2 %collective-permute-start.8 = (bf16[512,128]{1,0:T(8,128)(2,1)S(1)}, bf16[512,128]{1,0:T(8,128)(2,1)S(1)}, u32[]{:S(2)}, u32[]{:S(2)}) collective-permute-start(bf16[512,128]{1,0:T(8,128)(2,1)S(1)} %shard_map.155), channel_id=1, source_target_pairs={{0,2},{1,3},{2,0},{3,1},{4,6},{5,7},{6,4},{7,5},{8,10},{9,11},{10,... | collective-permute-start | bytes 393224 | tf_op jit(solution)/shard_map/ppermute | solution.py:327
  41.9 7.0 %copy-start.1 = (bf16[512,512]{1,0:T(8,128)(2,1)S(1)}, bf16[512,512]{1,0:T(8,128)(2,1)}, u32[]{:S(2)}) copy-start(bf16[512,512]{1,0:T(8,128)(2,1)} %edges.3) | copy-start | bytes 1572868
  41.9 7.0 %copy-start.7 = (bf16[512,512]{1,0:T(8,128)(2,1)S(1)}, bf16[512,512]{1,0:T(8,128)(2,1)}, u32[]{:S(2)}) copy-start(bf16[512,512]{1,0:T(8,128)(2,1)} %w2.2) | copy-start | bytes 1572868
  41.9 7.0 %copy-start.8 = (bf16[512]{0:T(512)(128)(2,1)S(1)}, bf16[512]{0:T(512)(128)(2,1)}, u32[]{:S(2)}) copy-start(bf16[512]{0:T(512)(128)(2,1)} %param.22) | copy-start | bytes 3076
  41.9 7.0 %copy-start.9 = (bf16[512]{0:T(512)(128)(2,1)S(1)}, bf16[512]{0:T(512)(128)(2,1)}, u32[]{:S(2)}) copy-start(bf16[512]{0:T(512)(128)(2,1)} %param.23) | copy-start | bytes 3076
  42.0 7.0 %collective-permute-start.7 = (bf16[512,128]{1,0:T(8,128)(2,1)S(1)}, bf16[512,128]{1,0:T(8,128)(2,1)S(1)}, u32[]{:S(2)}, u32[]{:S(2)}) collective-permute-start(bf16[512,128]{1,0:T(8,128)(2,1)S(1)} %shard_map.154), channel_id=1, source_target_pairs={{0,3},{1,0},{2,1},{3,2},{4,7},{5,4},{6,5},{7,6},{8,11},{9,8},{10,9... | collective-permute-start | bytes 393224 | tf_op jit(solution)/shard_map/ppermute | solution.py:327
  50.4 6.0 %collective-permute-start.10 = (bf16[512,128]{1,0:T(8,128)(2,1)S(1)}, bf16[512,128]{1,0:T(8,128)(2,1)S(1)}, u32[]{:S(2)}, u32[]{:S(2)}) collective-permute-start(bf16[512,128]{1,0:T(8,128)(2,1)S(1)} %get-tuple-element.40.tile1), channel_id=1, source_target_pairs={{0,1},{1,2},{2,3},{3,0},{4,5},{5,6},{6,7},{7,4},{8,9},{9,10},{10,1... | collective-permute-start | bytes 393224 | tf_op jit(solution)/shard_map/ppermute | solution.py:327
  51.5 5.6 %collective-permute-start.11 = (bf16[512,128]{1,0:T(8,128)(2,1)S(1)}, bf16[512,128]{1,0:T(8,128)(2,1)S(1)}, u32[]{:S(2)}, u32[]{:S(2)}) collective-permute-start(bf16[512,128]{1,0:T(8,128)(2,1)S(1)} %get-tuple-element.42.tile3), channel_id=1, source_target_pairs={{0,3},{1,0},{2,1},{3,2},{4,7},{5,4},{6,5},{7,6},{8,11},{9,8},{10,9... | collective-permute-start | bytes 393224 | tf_op jit(solution)/shard_map/ppermute | solution.py:327
  53.6 6.9 %collective-permute-start.12 = (bf16[512,128]{1,0:T(8,128)(2,1)S(1)}, bf16[512,128]{1,0:T(8,128)(2,1)S(1)}, u32[]{:S(2)}, u32[]{:S(2)}) collective-permute-start(bf16[512,128]{1,0:T(8,128)(2,1)S(1)} %get-tuple-element.41.tile2), channel_id=1, source_target_pairs={{0,2},{1,3},{2,0},{3,1},{4,6},{5,7},{6,4},{7,5},{8,10},{9,11},{10,... | collective-permute-start | bytes 393224 | tf_op jit(solution)/shard_map/ppermute | solution.py:327
  61.7 19.8 %all-to-all-start.1 = ((bf16[64,16,128]{2,1,0:T(8,128)(2,1)}), bf16[64,16,128]{2,1,0:T(8,128)(2,1)S(1)}, u32[]{:S(2)}, u32[]{:S(2)}) async-start(bf16[64,16,128]{2,1,0:T(8,128)(2,1)} %shard_map.163.far), calls=%async_computation.1 | async-start | bytes 524288 | tf_op jit(solution)/shard_map/all_to_all | solution.py:334
  67.9 20.4 %copy-start = (bf16[1024,512]{1,0:T(8,128)(2,1)S(1)}, bf16[1024,512]{1,0:T(8,128)(2,1)}, u32[]{:S(2)}) copy-start(bf16[1024,512]{1,0:T(8,128)(2,1)} %w1.3) | copy-start | bytes 3145732
  67.9 20.4 %copy-start.2 = (bf16[512,512]{1,0:T(8,128)(2,1)S(1)}, bf16[512,512]{1,0:T(8,128)(2,1)}, u32[]{:S(2)}) copy-start(bf16[512,512]{1,0:T(8,128)(2,1)} %w2.3) | copy-start | bytes 1572868
  67.9 20.4 %copy-start.3 = (bf16[80,512]{1,0:T(8,128)(2,1)S(1)}, bf16[80,512]{1,0:T(8,128)(2,1)}, u32[]{:S(2)}) copy-start(bf16[80,512]{1,0:T(8,128)(2,1)} %nodes.1) | copy-start | bytes 245764
  68.0 20.4 %copy-start.5 = (bf16[512]{0:T(512)(128)(2,1)S(1)}, bf16[512]{0:T(512)(128)(2,1)}, u32[]{:S(2)}) copy-start(bf16[512]{0:T(512)(128)(2,1)} %param.26) | copy-start | bytes 3076
  68.0 20.4 %copy-start.6 = (bf16[512]{0:T(512)(128)(2,1)S(1)}, bf16[512]{0:T(512)(128)(2,1)}, u32[]{:S(2)}) copy-start(bf16[512]{0:T(512)(128)(2,1)} %param.27) | copy-start | bytes 3076
  68.3 7.6 %collective-permute-start.13 = (bf16[80,128]{1,0:T(8,128)(2,1)S(1)}, bf16[80,128]{1,0:T(8,128)(2,1)S(1)}, u32[]{:S(2)}, u32[]{:S(2)}) collective-permute-start(bf16[80,128]{1,0:T(8,128)(2,1)S(1)} %get-tuple-element.46), channel_id=1, source_target_pairs={{0,248},{4,252},{8,0},{12,4},{16,8},{20,12},{24,16},{28,20},{32,24... | collective-permute-start | bytes 61448 | tf_op jit(solution)/shard_map/ppermute | solution.py:338
  73.4 3.5 %collective-permute-start.14 = (bf16[80,128]{1,0:T(8,128)(2,1)S(1)}, bf16[80,128]{1,0:T(8,128)(2,1)S(1)}, u32[]{:S(2)}, u32[]{:S(2)}) collective-permute-start(bf16[80,128]{1,0:T(8,128)(2,1)S(1)} %get-tuple-element.47), channel_id=1, source_target_pairs={{0,252},{4,0},{8,4},{12,8},{16,12},{20,16},{24,20},{28,24},{32,28}... | collective-permute-start | bytes 61448 | tf_op jit(solution)/shard_map/ppermute | solution.py:338
  74.0 2.8 %collective-permute-start.15 = (bf16[80,128]{1,0:T(8,128)(2,1)S(1)}, bf16[80,128]{1,0:T(8,128)(2,1)S(1)}, u32[]{:S(2)}, u32[]{:S(2)}) collective-permute-start(bf16[80,128]{1,0:T(8,128)(2,1)S(1)} %get-tuple-element.48), channel_id=1, source_target_pairs={{0,4},{4,8},{8,12},{12,16},{16,20},{20,24},{24,28},{28,32},{32,36}... | collective-permute-start | bytes 61448 | tf_op jit(solution)/shard_map/ppermute | solution.py:338
  75.1 6.4 %collective-permute-start.16 = (bf16[80,128]{1,0:T(8,128)(2,1)S(1)}, bf16[80,128]{1,0:T(8,128)(2,1)S(1)}, u32[]{:S(2)}, u32[]{:S(2)}) collective-permute-start(bf16[80,128]{1,0:T(8,128)(2,1)S(1)} %get-tuple-element.49), channel_id=1, source_target_pairs={{0,8},{4,12},{8,16},{12,20},{16,24},{20,28},{24,32},{28,36},{32,40... | collective-permute-start | bytes 61448 | tf_op jit(solution)/shard_map/ppermute | solution.py:338
  81.9 3.2 %collective-permute-start.17 = (bf16[80,128]{1,0:T(8,128)(2,1)S(1)}, bf16[80,128]{1,0:T(8,128)(2,1)S(1)}, u32[]{:S(2)}, u32[]{:S(2)}) collective-permute-start(bf16[80,128]{1,0:T(8,128)(2,1)S(1)} %get-tuple-element.51), channel_id=1, source_target_pairs={{0,3},{1,0},{2,1},{3,2},{4,7},{5,4},{6,5},{7,6},{8,11},{9,8},{10,9... | collective-permute-start | bytes 61448 | tf_op jit(solution)/shard_map/ppermute | solution.py:327
  84.2 4.1 %collective-permute-start.18 = (bf16[80,128]{1,0:T(8,128)(2,1)S(1)}, bf16[80,128]{1,0:T(8,128)(2,1)S(1)}, u32[]{:S(2)}, u32[]{:S(2)}) collective-permute-start(bf16[80,128]{1,0:T(8,128)(2,1)S(1)} %get-tuple-element.52), channel_id=1, source_target_pairs={{0,2},{1,3},{2,0},{3,1},{4,6},{5,7},{6,4},{7,5},{8,10},{9,11},{10,... | collective-permute-start | bytes 61448 | tf_op jit(solution)/shard_map/ppermute | solution.py:327
  84.2 4.1 %collective-permute-start.19 = (bf16[80,128]{1,0:T(8,128)(2,1)S(1)}, bf16[80,128]{1,0:T(8,128)(2,1)S(1)}, u32[]{:S(2)}, u32[]{:S(2)}) collective-permute-start(bf16[80,128]{1,0:T(8,128)(2,1)S(1)} %get-tuple-element.53), channel_id=1, source_target_pairs={{0,1},{1,2},{2,3},{3,0},{4,5},{5,6},{6,7},{7,4},{8,9},{9,10},{10,1... | collective-permute-start | bytes 61448 | tf_op jit(solution)/shard_map/ppermute | solution.py:327

commit v4 on v3

--- a/solution.py
+++ b/solution.py
@@ -6,6 +6,7 @@
 from jax.experimental import pallas as pl
 from jax.experimental.pallas import tpu as pltpu
 from jax.sharding import PartitionSpec as P
+
 
 D = 512
 Q = 128
@@ -19,6 +20,7 @@
 EDGES = 512
 REGION_EDGES = FEAT * EDGES
 OFFSETS = (-2, -1, 1, 2)
+SEND_ORDER = (2, 1, 3)
 FAR_ROWS = GROUPS * FAR
 NEAR_ROWS = len(OFFSETS) * NEAR
 LIST_ROWS = FAR_ROWS + NEAR_ROWS
@@ -71,12 +73,12 @@
 
 
 def peer(p):
-    return (lax.axis_index("feat") + p) & (FEAT - 1)
+    return lax.axis_index("feat") ^ p
 
 
 def relative(node):
     owner = lax.shift_right_logical(node * 205, 14)
-    return ((owner - lax.axis_index("feat")) & (FEAT - 1)) * OWN + node - owner * OWN
+    return (owner ^ lax.axis_index("feat")) * OWN + node - owner * OWN
 
 
 def project_body(nodes_hbm, w1, senders, refs, *rest):
@@ -272,15 +274,15 @@
 
 def far_sums_body(acc, tile, rowid, done, far):
     for base, size in BLOCKS[1:5]:
-        total = acc[base : base + size, :] + block_sum(base, size, rowid, tile, 2)
+        total = acc[base : base + size, :] + block_sum(base, size, rowid, tile, SEND_ORDER[2])
         at = (base - NODES) // FAR
         far[at : at + 16] = total.astype(BF16).reshape(16, FAR, Q)
 
 
 def rest_sums_body(acc, tile, rowid, far, own, near0, near1, near2, near3):
-    own[...] = acc[0:NODES, :] + block_sum(0, NODES, rowid, tile, 2)
+    own[...] = acc[0:NODES, :] + block_sum(0, NODES, rowid, tile, SEND_ORDER[2])
     base = NODES + FAR_ROWS
-    total = acc[base:TABLE_ROWS, :] + block_sum(base, NEAR_ROWS, rowid, tile, 2)
+    total = acc[base:TABLE_ROWS, :] + block_sum(base, NEAR_ROWS, rowid, tile, SEND_ORDER[2])
     for j, out in enumerate((near0, near1, near2, near3)):
         out[...] = total[j * NEAR : (j + 1) * NEAR].astype(BF16)
 
@@ -323,11 +325,10 @@
 
 
 def exchanged(tiles):
-    arrived = [
-        lax.ppermute(tiles[j], "feat", [(i, (i + j) % FEAT) for i in range(FEAT)])
-        for j in (2, 1, 3)
-    ]
-    return tiles[0], arrived[2], arrived[0], arrived[1]
+    arrived = list(tiles)
+    for p in SEND_ORDER:
+        arrived[p] = lax.ppermute(tiles[p], "feat", [(i, i ^ p) for i in range(FEAT)])
+    return arrived
 
 
 def swapped(value):
@@ -415,15 +416,15 @@
     arrived = exchanged(messages)
     acc_shape = shape((TABLE_ROWS, Q), F32)
     acc = call(first_sums_body, acc_shape, [VMEM] * 2)(messages[0], rowid)
-    for p in (3, 1):
+    for p in SEND_ORDER[:2]:
         acc = call(functools.partial(more_sums_body, p), acc_shape, [VMEM] * 3, alias={0: 0})(
             acc, arrived[p], rowid
         )
-    sent = call(far_sums_body, far_shape, [VMEM] * 4)(acc, arrived[2], rowid, done)
+    sent = call(far_sums_body, far_shape, [VMEM] * 4)(acc, arrived[SEND_ORDER[2]], rowid, done)
     far = swapped(sent)
     own, *near = call(
         rest_sums_body, (shape((NODES, Q), F32), *near_shape), [VMEM] * 3 + [HBM]
-    )(acc, arrived[2], rowid, sent)
+    )(acc, arrived[SEND_ORDER[2]], rowid, sent)
     near = [moved(value, d) for value, d in zip(near, OFFSETS)]
     spread = call(
         flip_body,

time: 90 us -> 89.6 us (level)
  transfers between devices with their start and end apart: 22 -> 22, of which waited for: 11 -> 12; matrix products, arithmetic and copies ran while one was open for 1% -> 1% of each run, Pallas kernels for 9% -> 9%
where the time goes in v4:
time: 89.6 us; the launch traced here: 89.3 us
  starting transfers between devices  49.4 us (55%)
  waiting for transfers between devices  21.8 us (24%)
  Pallas kernels  15.3 us (17%)
  between operations  1.56 us (2%)
  local copies, waits for them, and re-layouts  1.14 us (1%)
    all_to_all x2, starting transfers between devices, swapped(): lax.all_to_all(value, 'graph', split_axis=0, concat_axis=0, tiled=True)  20.3 us
    ppermute x12, starting transfers between devices, exchanged(): lax.ppermute(tiles[p], 'feat', [(i, i ^ p) for i in range(FEAT)])  15.6 us
    ppermute x8, starting transfers between devices, moved(): lax.ppermute(value, 'graph', [(i, (i + by) % GROUPS) for i in range(GROUP...  13.6 us
    ppermute x12, waiting for transfers between devices, exchanged(): lax.ppermute(tiles[p], 'feat', [(i, i ^ p) for i in range(FEAT)])  11.4 us
    ppermute x8, waiting for transfers between devices, moved(): lax.ppermute(value, 'graph', [(i, (i + by) % GROUPS) for i in range(GROUP...  7.21 us
    all_to_all x2, waiting for transfers between devices, swapped(): lax.all_to_all(value, 'graph', split_axis=0, concat_axis=0, tiled=True)  3.18 us
    pallas_call x4, Pallas kernels, per_device(): call(functools.partial(gather_body, p), quarter[0], [VMEM] * 7)  2.35 us
  transfers between devices with their start and end apart: 22, of which 12 were waited for; matrix products, arithmetic and copies ran while one was open for 1% of the time, Pallas kernels for 9%

profile of v4, /device:TPU:1, one launch (start us, length us, event | category | flops | bytes accessed | tf_op | source)
XLA Modules:
  0.0 89.3 jit_solution(17467307595372081164)
XLA Ops:
  0.6 1.6 %shard_map.149 = (bf16[96,256]{1,0:T(8,128)(2,1)S(1)}, bf16[96,256]{1,0:T(8,128)(2,1)S(1)}, bf16[96,256]{1,0:T(8,128)(2,1)S(1)}, bf16[96,256]{1,0:T(8,128)(2,1)S(1)}) custom-call(bf16[80,512]{1,0:T(8,128)(2,1)} %nodes.1, bf16[1536,512]{1,0:T(8,128)(2,1)} %w1.2, s32[4,128]{1,0:T(4,128)} %bitcast.13, s32[4,128]{1,0:T(4,128)} %bitcast.14), custom_call_target="tpu_custom_call" | custom-call | flops 100000000 | bytes 1000000 | tf_op jit(solution)/shard_map/pallas_call | solution.py:358
  2.2 2.1 %collective-permute-start = (bf16[96,256]{1,0:T(8,128)(2,1)S(1)}, bf16[96,256]{1,0:T(8,128)(2,1)S(1)}, u32[]{:S(2)}, u32[]{:S(2)}) collective-permute-start(bf16[96,256]{1,0:T(8,128)(2,1)S(1)} %get-tuple-element.29), channel_id=1, source_target_pairs={{0,1},{1,0},{2,3},{3,2},{4,5},{5,4},{6,7},{7,6},{8,9},{9,8},{10,11... | collective-permute-start | bytes 147464 | tf_op jit(solution)/shard_map/ppermute | solution.py:330
  4.4 2.5 %collective-permute-start.1 = (bf16[96,256]{1,0:T(8,128)(2,1)S(1)}, bf16[96,256]{1,0:T(8,128)(2,1)S(1)}, u32[]{:S(2)}, u32[]{:S(2)}) collective-permute-start(bf16[96,256]{1,0:T(8,128)(2,1)S(1)} %get-tuple-element.30), channel_id=1, source_target_pairs={{0,2},{1,3},{2,0},{3,1},{4,6},{5,7},{6,4},{7,5},{8,10},{9,11},{10,... | collective-permute-start | bytes 147464 | tf_op jit(solution)/shard_map/ppermute | solution.py:330
  6.8 0.0 collective-permute-start.2
  6.9 0.5 shard_map.151.select
  7.3 1.5 %collective-permute-done.1.tile2 = bf16[96,256]{1,0:T(8,128)(2,1)S(1)} collective-permute-done((bf16[96,256]{1,0:T(8,128)(2,1)S(1)}, bf16[96,256]{1,0:T(8,128)(2,1)S(1)}, u32[]{:S(2)}, u32[]{:S(2)}) %collective-permute-start.1) | collective-permute-done | bytes 49184 | tf_op jit(solution)/shard_map/ppermute | solution.py:330
  8.8 2.2 %collective-permute-done.2.tile3 = bf16[96,256]{1,0:T(8,128)(2,1)S(1)} collective-permute-done((bf16[96,256]{1,0:T(8,128)(2,1)S(1)}, bf16[96,256]{1,0:T(8,128)(2,1)S(1)}, u32[]{:S(2)}, u32[]{:S(2)}) %collective-permute-start.2) | collective-permute-done | bytes 49184 | tf_op jit(solution)/shard_map/ppermute | solution.py:330
  11.1 1.1 %shard_map.152 = (bf16[64,16,128]{2,1,0:T(8,128)(2,1)}, bf16[80,128]{1,0:T(8,128)(2,1)S(1)}, bf16[80,128]{1,0:T(8,128)(2,1)S(1)}, bf16[80,128]{1,0:T(8,128)(2,1)S(1)}, bf16[80,128]{1,0:T(8,128)(2,1)S(1)}) custom-call(bf16[96,256]{1,0:T(8,128)(2,1)S(1)} %get-tuple-element.28.tile0, bf16[96,256]{1,0:T(8,128)(2,1)S(1)} %collective-permute-done.tile1, ...), custom_call_target="tpu_custom_call" | custom-call | flops 100000000 | bytes 1000000 | tf_op jit(solution)/shard_map/pallas_call | solution.py:375
  12.1 13.9 %all-to-all-start = ((bf16[64,16,128]{2,1,0:T(8,128)(2,1)}), bf16[64,16,128]{2,1,0:T(8,128)(2,1)S(1)}, u32[]{:S(2)}, u32[]{:S(2)}) async-start(bf16[64,16,128]{2,1,0:T(8,128)(2,1)} %get-tuple-element.34), calls=%async_computation | async-start | bytes 524288 | tf_op jit(solution)/shard_map/all_to_all | solution.py:335
  26.1 1.4 %collective-permute-start.3 = (bf16[80,128]{1,0:T(8,128)(2,1)S(1)}, bf16[80,128]{1,0:T(8,128)(2,1)S(1)}, u32[]{:S(2)}, u32[]{:S(2)}) collective-permute-start(bf16[80,128]{1,0:T(8,128)(2,1)S(1)} %get-tuple-element.35), channel_id=1, source_target_pairs={{0,8},{4,12},{8,16},{12,20},{16,24},{20,28},{24,32},{28,36},{32,40... | collective-permute-start | bytes 61448 | tf_op jit(solution)/shard_map/ppermute | solution.py:339
  27.5 1.7 %collective-permute-start.4 = (bf16[80,128]{1,0:T(8,128)(2,1)S(1)}, bf16[80,128]{1,0:T(8,128)(2,1)S(1)}, u32[]{:S(2)}, u32[]{:S(2)}) collective-permute-start(bf16[80,128]{1,0:T(8,128)(2,1)S(1)} %get-tuple-element.36), channel_id=1, source_target_pairs={{0,4},{4,8},{8,12},{12,16},{16,20},{20,24},{24,28},{28,32},{32,36}... | collective-permute-start | bytes 61448 | tf_op jit(solution)/shard_map/ppermute | solution.py:339
  29.2 3.6 %collective-permute-start.6 = (bf16[80,128]{1,0:T(8,128)(2,1)S(1)}, bf16[80,128]{1,0:T(8,128)(2,1)S(1)}, u32[]{:S(2)}, u32[]{:S(2)}) collective-permute-start(bf16[80,128]{1,0:T(8,128)(2,1)S(1)} %get-tuple-element.38), channel_id=1, source_target_pairs={{0,248},{4,252},{8,0},{12,4},{16,8},{20,12},{24,16},{28,20},{32,24... | collective-permute-start | bytes 61448 | tf_op jit(solution)/shard_map/ppermute | solution.py:339
  32.8 1.5 %shard_map.150 = (s32[16,128]{1,0:T(8,128)S(1)}, f32[2048,128]{1,0:T(8,128)S(1)}) custom-call(bf16[96,256]{1,0:T(8,128)(2,1)S(1)} %get-tuple-element.28.tile0, bf16[96,256]{1,0:T(8,128)(2,1)S(1)} %collective-permute-done.tile1, bf16[96,256]{1,0:T(8,128)(2,1)S(1)} %collective-permute-done.1.tile2, bf16[96,256]{1,0:T(8,128)(2,1)S(1)} %collective-permute-done.2.tile3), custom_call_target="tpu_custom_call" | custom-call | flops 1000000000 | bytes 1000000 | tf_op jit(solution)/shard_map/pallas_call | solution.py:379
  34.3 1.6 %collective-permute-done.3.near0 = bf16[80,128]{1,0:T(8,128)(2,1)S(1)} collective-permute-done((bf16[80,128]{1,0:T(8,128)(2,1)S(1)}, bf16[80,128]{1,0:T(8,128)(2,1)S(1)}, u32[]{:S(2)}, u32[]{:S(2)}) %collective-permute-start.3) | collective-permute-done | bytes 20512 | tf_op jit(solution)/shard_map/ppermute | solution.py:339
  35.9 0.0 collective-permute-done.4.near1
  36.0 3.2 %all-to-all-done.far = bf16[64,16,128]{2,1,0:T(8,128)(2,1)S(1)} async-done(((bf16[64,16,128]{2,1,0:T(8,128)(2,1)}), bf16[64,16,128]{2,1,0:T(8,128)(2,1)S(1)}, u32[]{:S(2)}, u32[]{:S(2)}) %all-to-all-start) | async-done | bytes 262176 | tf_op jit(solution)/shard_map/all_to_all | solution.py:335
  39.1 0.6 shard_map.156
  39.7 0.3 collective-permute-start.9
  40.0 0.6 shard_map.155
  40.6 0.4 collective-permute-start.8
  41.0 0.6 shard_map.154
  41.6 0.0 copy-start.1
  41.6 0.0 copy-start.7
  41.6 0.0 copy-start.8
  41.7 0.0 copy-start.9
  41.7 3.0 %collective-permute-start.7 = (bf16[512,128]{1,0:T(8,128)(2,1)S(1)}, bf16[512,128]{1,0:T(8,128)(2,1)S(1)}, u32[]{:S(2)}, u32[]{:S(2)}) collective-permute-start(bf16[512,128]{1,0:T(8,128)(2,1)S(1)} %shard_map.154), channel_id=1, source_target_pairs={{0,1},{1,0},{2,3},{3,2},{4,5},{5,4},{6,7},{7,6},{8,9},{9,8},{10,11... | collective-permute-start | bytes 393224 | tf_op jit(solution)/shard_map/ppermute | solution.py:330
  44.7 1.1 %slice.3.w1 = bf16[512,512]{1,0:T(8,128)(2,1)S(1)} slice(bf16[1536,512]{1,0:T(8,128)(2,1)} %w1.2), slice={[0:512], [0:512]} | slice | bytes 1048576 | tf_op jit(solution)/shard_map/slice | solution.py:405
  46.4 0.6 shard_map.153.tile0
  47.0 1.5 %collective-permute-done.9.tile3 = bf16[512,128]{1,0:T(8,128)(2,1)S(1)} collective-permute-done((bf16[512,128]{1,0:T(8,128)(2,1)S(1)}, bf16[512,128]{1,0:T(8,128)(2,1)S(1)}, u32[]{:S(2)}, u32[]{:S(2)}) %collective-permute-start.9) | collective-permute-done | bytes 131104 | tf_op jit(solution)/shard_map/ppermute | solution.py:330
  48.5 0.0 collective-permute-done.8.tile2
  48.5 1.1 %collective-permute-done.7.tile1 = bf16[512,128]{1,0:T(8,128)(2,1)S(1)} collective-permute-done((bf16[512,128]{1,0:T(8,128)(2,1)S(1)}, bf16[512,128]{1,0:T(8,128)(2,1)S(1)}, u32[]{:S(2)}, u32[]{:S(2)}) %collective-permute-start.7) | collective-permute-done | bytes 131104 | tf_op jit(solution)/shard_map/ppermute | solution.py:330
  49.6 1.4 %shard_map.157 = (bf16[512,128]{1,0:T(8,128)(2,1)S(1)}, bf16[512,128]{1,0:T(8,128)(2,1)S(1)}, bf16[512,128]{1,0:T(8,128)(2,1)S(1)}, bf16[512,128]{1,0:T(8,128)(2,1)S(1)}) custom-call(s32[1]{0:T(128)S(6)} %copy.20.count, bf16[512,512]{1,0:T(8,128)(2,1)S(1)} %copy-done.1, bf16[512,128]{1,0:T(8,128)(2,1)S(1)} %shard_map.153.tile0, ...), custom_call_target="tpu_custom_call" | custom-call | flops 1000000000 | bytes 1000000 | tf_op jit(solution)/shard_map/pallas_call | solution.py:395
  51.0 1.0 %collective-permute-start.10 = (bf16[512,128]{1,0:T(8,128)(2,1)S(1)}, bf16[512,128]{1,0:T(8,128)(2,1)S(1)}, u32[]{:S(2)}, u32[]{:S(2)}) collective-permute-start(bf16[512,128]{1,0:T(8,128)(2,1)S(1)} %get-tuple-element.41.tile2), channel_id=1, source_target_pairs={{0,2},{1,3},{2,0},{3,1},{4,6},{5,7},{6,4},{7,5},{8,10},{9,11},{10,... | collective-permute-start | bytes 393224 | tf_op jit(solution)/shard_map/ppermute | solution.py:330
  52.1 2.3 %collective-permute-start.12 = (bf16[512,128]{1,0:T(8,128)(2,1)S(1)}, bf16[512,128]{1,0:T(8,128)(2,1)S(1)}, u32[]{:S(2)}, u32[]{:S(2)}) collective-permute-start(bf16[512,128]{1,0:T(8,128)(2,1)S(1)} %get-tuple-element.42.tile3), channel_id=1, source_target_pairs={{0,3},{1,2},{2,1},{3,0},{4,7},{5,6},{6,5},{7,4},{8,11},{9,10},{10,... | collective-permute-start | bytes 393224 | tf_op jit(solution)/shard_map/ppermute | solution.py:330
  54.4 0.6 shard_map.160.acc
  55.0 1.1 %shard_map.158 = (bf16[512,512]{1,0:T(8,128)(2,1)}, f32[8,128]{1,0:T(8,128)S(1)}) custom-call(s32[1]{0:T(128)S(6)} %copy.20.count, bf16[512,512]{1,0:T(8,128)(2,1)S(1)} %copy-done.1, bf16[512,128]{1,0:T(8,128)(2,1)S(1)} %get-tuple-element.39.tile0.tile, bf16[512,128]{1,0:T(8,128)(2,1)S(1)} %get-tuple-element.40.tile1, ...), custom_call_target="tpu_custom_call" | custom-call | flops 100000000 | bytes 1000000 | tf_op jit(solution)/shard_map/pallas_call | solution.py:410
  56.1 0.4 collective-permute-done.10.tile
  56.5 0.7 shard_map.161.acc
  57.2 0.7 shard_map.162.acc
  57.9 1.9 %collective-permute-done.12.tile = bf16[512,128]{1,0:T(8,128)(2,1)S(1)} collective-permute-done((bf16[512,128]{1,0:T(8,128)(2,1)S(1)}, bf16[512,128]{1,0:T(8,128)(2,1)S(1)}, u32[]{:S(2)}, u32[]{:S(2)}) %collective-permute-start.12) | collective-permute-done | bytes 131104 | tf_op jit(solution)/shard_map/ppermute | solution.py:330
  59.8 1.1 %shard_map.163.far = bf16[64,16,128]{2,1,0:T(8,128)(2,1)} custom-call(f32[1664,128]{1,0:T(8,128)S(1)} %shard_map.162.acc, bf16[512,128]{1,0:T(8,128)(2,1)S(1)} %collective-permute-done.12.tile, s32[16,128]{1,0:T(8,128)S(1)} %get-tuple-element.33.rowid, f32[8,128]{1,0:T(8,128)S(1)} %get-tuple-element.44.done), custom_call_target="tpu_custom_call" | custom-call | flops 100000000 | bytes 1000000 | tf_op jit(solution)/shard_map/pallas_call | solution.py:423
  60.9 6.3 %all-to-all-start.1 = ((bf16[64,16,128]{2,1,0:T(8,128)(2,1)}), bf16[64,16,128]{2,1,0:T(8,128)(2,1)S(1)}, u32[]{:S(2)}, u32[]{:S(2)}) async-start(bf16[64,16,128]{2,1,0:T(8,128)(2,1)} %shard_map.163.far), calls=%async_computation.1 | async-start | bytes 524288 | tf_op jit(solution)/shard_map/all_to_all | solution.py:335
  67.2 0.0 copy-start
  67.2 0.0 copy-start.2
  67.2 0.0 copy-start.3
  67.3 0.0 copy-start.5
  67.3 0.0 copy-start.6
  67.3 0.3 shard_map.164
  67.6 5.1 %collective-permute-start.13 = (bf16[80,128]{1,0:T(8,128)(2,1)S(1)}, bf16[80,128]{1,0:T(8,128)(2,1)S(1)}, u32[]{:S(2)}, u32[]{:S(2)}) collective-permute-start(bf16[80,128]{1,0:T(8,128)(2,1)S(1)} %get-tuple-element.46), channel_id=1, source_target_pairs={{0,248},{4,252},{8,0},{12,4},{16,8},{20,12},{24,16},{28,20},{32,24... | collective-permute-start | bytes 61448 | tf_op jit(solution)/shard_map/ppermute | solution.py:339
  72.7 0.7 collective-permute-start.14
  73.3 1.1 %collective-permute-start.15 = (bf16[80,128]{1,0:T(8,128)(2,1)S(1)}, bf16[80,128]{1,0:T(8,128)(2,1)S(1)}, u32[]{:S(2)}, u32[]{:S(2)}) collective-permute-start(bf16[80,128]{1,0:T(8,128)(2,1)S(1)} %get-tuple-element.48), channel_id=1, source_target_pairs={{0,4},{4,8},{8,12},{12,16},{16,20},{20,24},{24,28},{28,32},{32,36}... | collective-permute-start | bytes 61448 | tf_op jit(solution)/shard_map/ppermute | solution.py:339
  74.4 0.0 collective-permute-start.16
  74.4 0.7 shard_map.159.spread
  75.2 1.0 %collective-permute-done.14.near1 = bf16[80,128]{1,0:T(8,128)(2,1)S(1)} collective-permute-done((bf16[80,128]{1,0:T(8,128)(2,1)S(1)}, bf16[80,128]{1,0:T(8,128)(2,1)S(1)}, u32[]{:S(2)}, u32[]{:S(2)}) %collective-permute-start.14) | collective-permute-done | bytes 20512 | tf_op jit(solution)/shard_map/ppermute | solution.py:339
  76.2 0.0 collective-permute-done.15.near2
  76.2 4.6 %collective-permute-done.16.near3 = bf16[80,128]{1,0:T(8,128)(2,1)S(1)} collective-permute-done((bf16[80,128]{1,0:T(8,128)(2,1)S(1)}, bf16[80,128]{1,0:T(8,128)(2,1)S(1)}, u32[]{:S(2)}, u32[]{:S(2)}) %collective-permute-start.16) | collective-permute-done | bytes 20512 | tf_op jit(solution)/shard_map/ppermute | solution.py:339
  80.8 0.0 all-to-all-done.1.far
  80.8 0.4 shard_map.165
  81.2 0.1 collective-permute-start.17
  81.3 2.8 %collective-permute-start.18 = (bf16[80,128]{1,0:T(8,128)(2,1)S(1)}, bf16[80,128]{1,0:T(8,128)(2,1)S(1)}, u32[]{:S(2)}, u32[]{:S(2)}) collective-permute-start(bf16[80,128]{1,0:T(8,128)(2,1)S(1)} %get-tuple-element.52), channel_id=1, source_target_pairs={{0,2},{1,3},{2,0},{3,1},{4,6},{5,7},{6,4},{7,5},{8,10},{9,11},{10,... | collective-permute-start | bytes 61448 | tf_op jit(solution)/shard_map/ppermute | solution.py:330
  84.1 1.1 %collective-permute-start.19 = (bf16[80,128]{1,0:T(8,128)(2,1)S(1)}, bf16[80,128]{1,0:T(8,128)(2,1)S(1)}, u32[]{:S(2)}, u32[]{:S(2)}) collective-permute-start(bf16[80,128]{1,0:T(8,128)(2,1)S(1)} %get-tuple-element.53), channel_id=1, source_target_pairs={{0,3},{1,2},{2,1},{3,0},{4,7},{5,6},{6,5},{7,4},{8,11},{9,10},{10,... | collective-permute-start | bytes 61448 | tf_op jit(solution)/shard_map/ppermute | solution.py:330
  85.2 0.4 collective-permute-done.18.tile2
  85.5 2.4 %collective-permute-done.19.tile3 = bf16[80,128]{1,0:T(8,128)(2,1)S(1)} collective-permute-done((bf16[80,128]{1,0:T(8,128)(2,1)S(1)}, bf16[80,128]{1,0:T(8,128)(2,1)S(1)}, u32[]{:S(2)}, u32[]{:S(2)}) %collective-permute-start.19) | collective-permute-done | bytes 20512 | tf_op jit(solution)/shard_map/ppermute | solution.py:330
  88.0 1.3 %shard_map.166 = bf16[80,512]{1,0:T(8,128)(2,1)} custom-call(bf16[80,512]{1,0:T(8,128)(2,1)S(1)} %copy-done.3, bf16[80,128]{1,0:T(8,128)(2,1)S(1)} %get-tuple-element.50.tile0, bf16[80,128]{1,0:T(8,128)(2,1)S(1)} %collective-permute-done.17.tile1, bf16[80,128]{1,0:T(8,128)(2,1)S(1)} %collective-permute-done.18.tile2, ...), custom_call_target="tpu_custom_call" | custom-call | flops 100000000 | bytes 1000000 | tf_op jit(solution)/shard_map/pallas_call | solution.py:439
  (19 shorter events, 0.0 us)
Async XLA Ops:
  0.6 6.2 %copy-start.4 = (s32[1,64,96]{2,1,0:T(8,128)S(1)}, s32[1,64,96]{2,1,0:T(8,128)}, u32[]{:S(2)}) copy-start(s32[1,64,96]{2,1,0:T(8,128)} %param.18) | copy-start | bytes 73732
  2.2 5.1 %collective-permute-start = (bf16[96,256]{1,0:T(8,128)(2,1)S(1)}, bf16[96,256]{1,0:T(8,128)(2,1)S(1)}, u32[]{:S(2)}, u32[]{:S(2)}) collective-permute-start(bf16[96,256]{1,0:T(8,128)(2,1)S(1)} %get-tuple-element.29), channel_id=1, source_target_pairs={{0,1},{1,0},{2,3},{3,2},{4,5},{5,4},{6,7},{7,6},{8,9},{9,8},{10,11... | collective-permute-start | bytes 147464 | tf_op jit(solution)/shard_map/ppermute | solution.py:330
  4.4 4.5 %collective-permute-start.1 = (bf16[96,256]{1,0:T(8,128)(2,1)S(1)}, bf16[96,256]{1,0:T(8,128)(2,1)S(1)}, u32[]{:S(2)}, u32[]{:S(2)}) collective-permute-start(bf16[96,256]{1,0:T(8,128)(2,1)S(1)} %get-tuple-element.30), channel_id=1, source_target_pairs={{0,2},{1,3},{2,0},{3,1},{4,6},{5,7},{6,4},{7,5},{8,10},{9,11},{10,... | collective-permute-start | bytes 147464 | tf_op jit(solution)/shard_map/ppermute | solution.py:330
  6.8 4.2 %collective-permute-start.2 = (bf16[96,256]{1,0:T(8,128)(2,1)S(1)}, bf16[96,256]{1,0:T(8,128)(2,1)S(1)}, u32[]{:S(2)}, u32[]{:S(2)}) collective-permute-start(bf16[96,256]{1,0:T(8,128)(2,1)S(1)} %get-tuple-element.31), channel_id=1, source_target_pairs={{0,3},{1,2},{2,1},{3,0},{4,7},{5,6},{6,5},{7,4},{8,11},{9,10},{10,... | collective-permute-start | bytes 147464 | tf_op jit(solution)/shard_map/ppermute | solution.py:330
  12.1 27.0 %all-to-all-start = ((bf16[64,16,128]{2,1,0:T(8,128)(2,1)}), bf16[64,16,128]{2,1,0:T(8,128)(2,1)S(1)}, u32[]{:S(2)}, u32[]{:S(2)}) async-start(bf16[64,16,128]{2,1,0:T(8,128)(2,1)} %get-tuple-element.34), calls=%async_computation | async-start | bytes 524288 | tf_op jit(solution)/shard_map/all_to_all | solution.py:335
  26.1 9.9 %collective-permute-start.3 = (bf16[80,128]{1,0:T(8,128)(2,1)S(1)}, bf16[80,128]{1,0:T(8,128)(2,1)S(1)}, u32[]{:S(2)}, u32[]{:S(2)}) collective-permute-start(bf16[80,128]{1,0:T(8,128)(2,1)S(1)} %get-tuple-element.35), channel_id=1, source_target_pairs={{0,8},{4,12},{8,16},{12,20},{16,24},{20,28},{24,32},{28,36},{32,40... | collective-permute-start | bytes 61448 | tf_op jit(solution)/shard_map/ppermute | solution.py:339
  27.5 8.5 %collective-permute-start.4 = (bf16[80,128]{1,0:T(8,128)(2,1)S(1)}, bf16[80,128]{1,0:T(8,128)(2,1)S(1)}, u32[]{:S(2)}, u32[]{:S(2)}) collective-permute-start(bf16[80,128]{1,0:T(8,128)(2,1)S(1)} %get-tuple-element.36), channel_id=1, source_target_pairs={{0,4},{4,8},{8,12},{12,16},{16,20},{20,24},{24,28},{28,32},{32,36}... | collective-permute-start | bytes 61448 | tf_op jit(solution)/shard_map/ppermute | solution.py:339
  29.2 6.7 %collective-permute-start.5 = (bf16[80,128]{1,0:T(8,128)(2,1)S(1)}, bf16[80,128]{1,0:T(8,128)(2,1)S(1)}, u32[]{:S(2)}, u32[]{:S(2)}) collective-permute-start(bf16[80,128]{1,0:T(8,128)(2,1)S(1)} %get-tuple-element.37), channel_id=1, source_target_pairs={{0,252},{4,0},{8,4},{12,8},{16,12},{20,16},{24,20},{28,24},{32,28}... | collective-permute-start | bytes 61448 | tf_op jit(solution)/shard_map/ppermute | solution.py:339
  29.2 6.7 %collective-permute-start.6 = (bf16[80,128]{1,0:T(8,128)(2,1)S(1)}, bf16[80,128]{1,0:T(8,128)(2,1)S(1)}, u32[]{:S(2)}, u32[]{:S(2)}) collective-permute-start(bf16[80,128]{1,0:T(8,128)(2,1)S(1)} %get-tuple-element.38), channel_id=1, source_target_pairs={{0,248},{4,252},{8,0},{12,4},{16,8},{20,12},{24,16},{28,20},{32,24... | collective-permute-start | bytes 61448 | tf_op jit(solution)/shard_map/ppermute | solution.py:339
  39.7 8.8 %collective-permute-start.9 = (bf16[512,128]{1,0:T(8,128)(2,1)S(1)}, bf16[512,128]{1,0:T(8,128)(2,1)S(1)}, u32[]{:S(2)}, u32[]{:S(2)}) collective-permute-start(bf16[512,128]{1,0:T(8,128)(2,1)S(1)} %shard_map.156), channel_id=1, source_target_pairs={{0,3},{1,2},{2,1},{3,0},{4,7},{5,6},{6,5},{7,4},{8,11},{9,10},{10,... | collective-permute-start | bytes 393224 | tf_op jit(solution)/shard_map/ppermute | solution.py:330
  40.6 7.9 %collective-permute-start.8 = (bf16[512,128]{1,0:T(8,128)(2,1)S(1)}, bf16[512,128]{1,0:T(8,128)(2,1)S(1)}, u32[]{:S(2)}, u32[]{:S(2)}) collective-permute-start(bf16[512,128]{1,0:T(8,128)(2,1)S(1)} %shard_map.155), channel_id=1, source_target_pairs={{0,2},{1,3},{2,0},{3,1},{4,6},{5,7},{6,4},{7,5},{8,10},{9,11},{10,... | collective-permute-start | bytes 393224 | tf_op jit(solution)/shard_map/ppermute | solution.py:330
  41.6 8.0 %copy-start.1 = (bf16[512,512]{1,0:T(8,128)(2,1)S(1)}, bf16[512,512]{1,0:T(8,128)(2,1)}, u32[]{:S(2)}) copy-start(bf16[512,512]{1,0:T(8,128)(2,1)} %edges.3) | copy-start | bytes 1572868
  41.6 8.0 %copy-start.7 = (bf16[512,512]{1,0:T(8,128)(2,1)S(1)}, bf16[512,512]{1,0:T(8,128)(2,1)}, u32[]{:S(2)}) copy-start(bf16[512,512]{1,0:T(8,128)(2,1)} %w2.2) | copy-start | bytes 1572868
  41.6 8.0 %copy-start.8 = (bf16[512]{0:T(512)(128)(2,1)S(1)}, bf16[512]{0:T(512)(128)(2,1)}, u32[]{:S(2)}) copy-start(bf16[512]{0:T(512)(128)(2,1)} %param.22) | copy-start | bytes 3076
  41.7 8.0 %copy-start.9 = (bf16[512]{0:T(512)(128)(2,1)S(1)}, bf16[512]{0:T(512)(128)(2,1)}, u32[]{:S(2)}) copy-start(bf16[512]{0:T(512)(128)(2,1)} %param.23) | copy-start | bytes 3076
  41.7 7.9 %collective-permute-start.7 = (bf16[512,128]{1,0:T(8,128)(2,1)S(1)}, bf16[512,128]{1,0:T(8,128)(2,1)S(1)}, u32[]{:S(2)}, u32[]{:S(2)}) collective-permute-start(bf16[512,128]{1,0:T(8,128)(2,1)S(1)} %shard_map.154), channel_id=1, source_target_pairs={{0,1},{1,0},{2,3},{3,2},{4,5},{5,4},{6,7},{7,6},{8,9},{9,8},{10,11... | collective-permute-start | bytes 393224 | tf_op jit(solution)/shard_map/ppermute | solution.py:330
  51.0 5.5 %collective-permute-start.10 = (bf16[512,128]{1,0:T(8,128)(2,1)S(1)}, bf16[512,128]{1,0:T(8,128)(2,1)S(1)}, u32[]{:S(2)}, u32[]{:S(2)}) collective-permute-start(bf16[512,128]{1,0:T(8,128)(2,1)S(1)} %get-tuple-element.41.tile2), channel_id=1, source_target_pairs={{0,2},{1,3},{2,0},{3,1},{4,6},{5,7},{6,4},{7,5},{8,10},{9,11},{10,... | collective-permute-start | bytes 393224 | tf_op jit(solution)/shard_map/ppermute | solution.py:330
  52.1 5.2 %collective-permute-start.11 = (bf16[512,128]{1,0:T(8,128)(2,1)S(1)}, bf16[512,128]{1,0:T(8,128)(2,1)S(1)}, u32[]{:S(2)}, u32[]{:S(2)}) collective-permute-start(bf16[512,128]{1,0:T(8,128)(2,1)S(1)} %get-tuple-element.40.tile1), channel_id=1, source_target_pairs={{0,1},{1,0},{2,3},{3,2},{4,5},{5,4},{6,7},{7,6},{8,9},{9,8},{10,11... | collective-permute-start | bytes 393224 | tf_op jit(solution)/shard_map/ppermute | solution.py:330
  52.1 7.7 %collective-permute-start.12 = (bf16[512,128]{1,0:T(8,128)(2,1)S(1)}, bf16[512,128]{1,0:T(8,128)(2,1)S(1)}, u32[]{:S(2)}, u32[]{:S(2)}) collective-permute-start(bf16[512,128]{1,0:T(8,128)(2,1)S(1)} %get-tuple-element.42.tile3), channel_id=1, source_target_pairs={{0,3},{1,2},{2,1},{3,0},{4,7},{5,6},{6,5},{7,4},{8,11},{9,10},{10,... | collective-permute-start | bytes 393224 | tf_op jit(solution)/shard_map/ppermute | solution.py:330
  60.9 19.9 %all-to-all-start.1 = ((bf16[64,16,128]{2,1,0:T(8,128)(2,1)}), bf16[64,16,128]{2,1,0:T(8,128)(2,1)S(1)}, u32[]{:S(2)}, u32[]{:S(2)}) async-start(bf16[64,16,128]{2,1,0:T(8,128)(2,1)} %shard_map.163.far), calls=%async_computation.1 | async-start | bytes 524288 | tf_op jit(solution)/shard_map/all_to_all | solution.py:335
  67.2 20.7 %copy-start = (bf16[1024,512]{1,0:T(8,128)(2,1)S(1)}, bf16[1024,512]{1,0:T(8,128)(2,1)}, u32[]{:S(2)}) copy-start(bf16[1024,512]{1,0:T(8,128)(2,1)} %w1.3) | copy-start | bytes 3145732
  67.2 20.7 %copy-start.2 = (bf16[512,512]{1,0:T(8,128)(2,1)S(1)}, bf16[512,512]{1,0:T(8,128)(2,1)}, u32[]{:S(2)}) copy-start(bf16[512,512]{1,0:T(8,128)(2,1)} %w2.3) | copy-start | bytes 1572868
  67.2 20.7 %copy-start.3 = (bf16[80,512]{1,0:T(8,128)(2,1)S(1)}, bf16[80,512]{1,0:T(8,128)(2,1)}, u32[]{:S(2)}) copy-start(bf16[80,512]{1,0:T(8,128)(2,1)} %nodes.1) | copy-start | bytes 245764
  67.3 20.7 %copy-start.5 = (bf16[512]{0:T(512)(128)(2,1)S(1)}, bf16[512]{0:T(512)(128)(2,1)}, u32[]{:S(2)}) copy-start(bf16[512]{0:T(512)(128)(2,1)} %param.26) | copy-start | bytes 3076
  67.3 20.7 %copy-start.6 = (bf16[512]{0:T(512)(128)(2,1)S(1)}, bf16[512]{0:T(512)(128)(2,1)}, u32[]{:S(2)}) copy-start(bf16[512]{0:T(512)(128)(2,1)} %param.27) | copy-start | bytes 3076
  67.6 7.6 %collective-permute-start.13 = (bf16[80,128]{1,0:T(8,128)(2,1)S(1)}, bf16[80,128]{1,0:T(8,128)(2,1)S(1)}, u32[]{:S(2)}, u32[]{:S(2)}) collective-permute-start(bf16[80,128]{1,0:T(8,128)(2,1)S(1)} %get-tuple-element.46), channel_id=1, source_target_pairs={{0,248},{4,252},{8,0},{12,4},{16,8},{20,12},{24,16},{28,20},{32,24... | collective-permute-start | bytes 61448 | tf_op jit(solution)/shard_map/ppermute | solution.py:339
  72.7 3.5 %collective-permute-start.14 = (bf16[80,128]{1,0:T(8,128)(2,1)S(1)}, bf16[80,128]{1,0:T(8,128)(2,1)S(1)}, u32[]{:S(2)}, u32[]{:S(2)}) collective-permute-start(bf16[80,128]{1,0:T(8,128)(2,1)S(1)} %get-tuple-element.47), channel_id=1, source_target_pairs={{0,252},{4,0},{8,4},{12,8},{16,12},{20,16},{24,20},{28,24},{32,28}... | collective-permute-start | bytes 61448 | tf_op jit(solution)/shard_map/ppermute | solution.py:339
  73.3 2.8 %collective-permute-start.15 = (bf16[80,128]{1,0:T(8,128)(2,1)S(1)}, bf16[80,128]{1,0:T(8,128)(2,1)S(1)}, u32[]{:S(2)}, u32[]{:S(2)}) collective-permute-start(bf16[80,128]{1,0:T(8,128)(2,1)S(1)} %get-tuple-element.48), channel_id=1, source_target_pairs={{0,4},{4,8},{8,12},{12,16},{16,20},{20,24},{24,28},{28,32},{32,36}... | collective-permute-start | bytes 61448 | tf_op jit(solution)/shard_map/ppermute | solution.py:339
  74.4 6.4 %collective-permute-start.16 = (bf16[80,128]{1,0:T(8,128)(2,1)S(1)}, bf16[80,128]{1,0:T(8,128)(2,1)S(1)}, u32[]{:S(2)}, u32[]{:S(2)}) collective-permute-start(bf16[80,128]{1,0:T(8,128)(2,1)S(1)} %get-tuple-element.49), channel_id=1, source_target_pairs={{0,8},{4,12},{8,16},{12,20},{16,24},{20,28},{24,32},{28,36},{32,40... | collective-permute-start | bytes 61448 | tf_op jit(solution)/shard_map/ppermute | solution.py:339
  81.2 3.9 %collective-permute-start.17 = (bf16[80,128]{1,0:T(8,128)(2,1)S(1)}, bf16[80,128]{1,0:T(8,128)(2,1)S(1)}, u32[]{:S(2)}, u32[]{:S(2)}) collective-permute-start(bf16[80,128]{1,0:T(8,128)(2,1)S(1)} %get-tuple-element.51), channel_id=1, source_target_pairs={{0,1},{1,0},{2,3},{3,2},{4,5},{5,4},{6,7},{7,6},{8,9},{9,8},{10,11... | collective-permute-start | bytes 61448 | tf_op jit(solution)/shard_map/ppermute | solution.py:330
  81.3 4.2 %collective-permute-start.18 = (bf16[80,128]{1,0:T(8,128)(2,1)S(1)}, bf16[80,128]{1,0:T(8,128)(2,1)S(1)}, u32[]{:S(2)}, u32[]{:S(2)}) collective-permute-start(bf16[80,128]{1,0:T(8,128)(2,1)S(1)} %get-tuple-element.52), channel_id=1, source_target_pairs={{0,2},{1,3},{2,0},{3,1},{4,6},{5,7},{6,4},{7,5},{8,10},{9,11},{10,... | collective-permute-start | bytes 61448 | tf_op jit(solution)/shard_map/ppermute | solution.py:330
  84.1 3.8 %collective-permute-start.19 = (bf16[80,128]{1,0:T(8,128)(2,1)S(1)}, bf16[80,128]{1,0:T(8,128)(2,1)S(1)}, u32[]{:S(2)}, u32[]{:S(2)}) collective-permute-start(bf16[80,128]{1,0:T(8,128)(2,1)S(1)} %get-tuple-element.53), channel_id=1, source_target_pairs={{0,3},{1,2},{2,1},{3,0},{4,7},{5,6},{6,5},{7,4},{8,11},{9,10},{10,... | collective-permute-start | bytes 61448 | tf_op jit(solution)/shard_map/ppermute | solution.py:330
